TPU v7x, 64 devices: a 2x2x8 block of a 4x4x8 slice. The times are simulated.
64 devices in a mesh: req: 4 (over x, y), dap: 16 (over z, core).
Axes of the slice: x: 2, y: 2, z: 8, core: 2. Of those that a mesh axis runs over, the one named last changes fastest.
The devices are a block of a 4x4x8 slice.
Arguments:
- msa_act: bfloat16 [2048, 128, 256], P(('req', 'dap')), parts along dimension 0
- pair_act: bfloat16 [512, 128, 128], P(('req', 'dap')), parts along dimension 0
- msa_mask: int32 [2048, 128], P(('req', 'dap')), parts along dimension 0
- pair_mask: int32 [512, 128], P(('req', 'dap')), parts along dimension 0
- row_qkvg: bfloat16 [2, 256, 1024], replicated
- row_bias: bfloat16 [2, 128, 8], replicated
- row_out: bfloat16 [2, 256, 256], replicated
- col_qkvg: bfloat16 [2, 256, 1024], replicated
- col_out: bfloat16 [2, 256, 256], replicated
- mtr_in: bfloat16 [2, 256, 1024], replicated
- mtr_out: bfloat16 [2, 1024, 256], replicated
- opm_proj: bfloat16 [2, 256, 64], replicated
- opm_out: bfloat16 [2, 1024, 128], replicated
- tmo_proj: bfloat16 [2, 128, 640], replicated
- tmo_out: bfloat16 [2, 128, 128], replicated
- tmi_proj: bfloat16 [2, 128, 640], replicated
- tmi_out: bfloat16 [2, 128, 128], replicated
- tas_qkvg: bfloat16 [2, 128, 512], replicated
- tas_bias: bfloat16 [2, 128, 4], replicated
- tas_out: bfloat16 [2, 128, 128], replicated
- tae_qkvg: bfloat16 [2, 128, 512], replicated
- tae_bias: bfloat16 [2, 128, 4], replicated
- tae_out: bfloat16 [2, 128, 128], replicated
- ptr_in: bfloat16 [2, 128, 512], replicated
- ptr_out: bfloat16 [2, 512, 128], replicated
Outputs:
- output 1: bfloat16 [2048, 128, 256], P(('req', 'dap')), parts along dimension 0
- output 2: bfloat16 [512, 128, 128], P(('req', 'dap')), parts along dimension 0
There are 4 independent parts. A program takes and returns all parts, laid end to end along the dimension named above; an argument that names none is the same for every part.
All inputs are finite; a program needn't handle non-finite values.
Results may differ from a plain program's by a relative error of at most 0.02.
Values are sent between devices in bfloat16 or wider.
A program may use at most 768 MiB of HBM per device.

v0:
```python
import jax
import jax.numpy as jnp
from jax import lax
from jax.sharding import PartitionSpec as P

GROUP_AXIS = 'dap'
PARTS_AXIS = 'req'
MASKED_LOGIT = -1e9


def layer_norm(x):
    values = x.astype(jnp.float32)
    centered = values - jnp.mean(values, axis=-1, keepdims=True)
    variance = jnp.mean(centered * centered, axis=-1, keepdims=True)
    return (centered * lax.rsqrt(variance + 1e-5)).astype(jnp.bfloat16)


def residual(x, update):
    return (x.astype(jnp.float32) + update).astype(jnp.bfloat16)


def dense(x, weight):
    return jnp.einsum('...c,cf->...f', x, weight, preferred_element_type=jnp.float32)


def attend(queries, gate_raw, keyvals, num_heads, pair_bias, key_mask, w_out):
    n_batch, q_len, head_width = queries.shape
    k_len = keyvals.shape[1]
    head_dim = head_width // num_heads
    q_heads = queries.reshape(n_batch, q_len, num_heads, head_dim)
    k_heads = keyvals[..., :head_width].reshape(n_batch, k_len, num_heads, head_dim)
    v_heads = keyvals[..., head_width:].reshape(n_batch, k_len, num_heads, head_dim)
    logits = jnp.einsum('bqhd,bkhd->bhqk', q_heads, k_heads, preferred_element_type=jnp.float32) * head_dim ** -0.5
    if pair_bias is not None:
        logits = logits + pair_bias.astype(jnp.float32)
    logits = jnp.where(key_mask[:, None, None, :] > 0, logits, MASKED_LOGIT)
    attn_prob = jax.nn.softmax(logits, axis=-1).astype(jnp.bfloat16)
    attended = jnp.einsum('bhqk,bkhd->bqhd', attn_prob, v_heads, preferred_element_type=jnp.float32)
    gated = (attended.reshape(n_batch, q_len, head_width) * jax.nn.sigmoid(gate_raw.astype(jnp.float32))).astype(jnp.bfloat16)
    return dense(gated, w_out)


def self_attention(x_norm, w_qkvg, num_heads, pair_bias, key_mask, w_out):
    head_width = w_out.shape[0]
    projected = dense(x_norm, w_qkvg).astype(jnp.bfloat16)
    return attend(projected[..., :head_width], projected[..., 3 * head_width:], projected[..., head_width:3 * head_width], num_heads, pair_bias, key_mask, w_out)


def head_bias(pair_norm, w_bias):
    return jnp.einsum('ijc,ch->hij', pair_norm, w_bias, preferred_element_type=jnp.float32).astype(jnp.bfloat16)


def transition(x, w_in, w_out):
    hidden = jnp.maximum(dense(layer_norm(x), w_in), 0.0).astype(jnp.bfloat16)
    return dense(hidden, w_out)


def outer_update(array_b7, res_mask, full_mask, w_proj, w_out):
    opm_dim = w_proj.shape[1] // 2
    projected = dense(layer_norm(array_b7), w_proj).astype(jnp.bfloat16)
    mask_bf = res_mask.astype(jnp.bfloat16)[:, :, None]
    left_act = projected[..., :opm_dim] * mask_bf
    right_act = projected[..., opm_dim:] * mask_bf
    right_full = lax.all_gather(right_act, GROUP_AXIS, axis=1, tiled=True)
    outer_prod = jnp.einsum('sic,sje->ijce', left_act, right_full, preferred_element_type=jnp.float32).astype(jnp.bfloat16)
    n_rows, n_cols = outer_prod.shape[:2]
    update = dense(outer_prod.reshape(n_rows, n_cols, opm_dim * opm_dim), w_out)
    overlap = jnp.einsum('si,sj->ij', res_mask.astype(jnp.float32), full_mask.astype(jnp.float32))
    return update / (1e-3 + overlap)[:, :, None]


def tri_gates(pair_rows, mask_rows, w_proj):
    tri_dim = (w_proj.shape[1] - pair_rows.shape[-1]) // 4
    projected = dense(layer_norm(pair_rows), w_proj)
    mask_f = mask_rows.astype(jnp.float32)[:, :, None]
    left_act = (mask_f * jax.nn.sigmoid(projected[..., 2 * tri_dim:3 * tri_dim]) * projected[..., :tri_dim]).astype(jnp.bfloat16)
    right_act = (mask_f * jax.nn.sigmoid(projected[..., 3 * tri_dim:4 * tri_dim]) * projected[..., tri_dim:2 * tri_dim]).astype(jnp.bfloat16)
    gate_act = jax.nn.sigmoid(projected[..., 4 * tri_dim:])
    return left_act, right_act, gate_act


def tri_finish(product, gate_act, w_out):
    return gate_act * dense(layer_norm(product), w_out)


def tri_attention(pair_rows, mask_rows, w_qkvg, w_bias, w_out):
    pair_norm = layer_norm(pair_rows)
    bias_full = lax.all_gather(head_bias(pair_norm, w_bias), GROUP_AXIS, axis=1, tiled=True)
    return self_attention(pair_norm, w_qkvg, w_bias.shape[1], bias_full, mask_rows, w_out)


def pair_stack(pair_loc, pair_mask, pair_mask_t, pair_w):
    (tmo_proj, tmo_out, tmi_proj, tmi_out, tas_qkvg, tas_bias, tas_out,
     tae_qkvg, tae_bias, tae_out, ptr_in, ptr_out) = pair_w
    left_act, right_act, gate_act = tri_gates(pair_loc, pair_mask, tmo_proj)
    right_full = lax.all_gather(right_act, GROUP_AXIS, axis=0, tiled=True)
    product = jnp.einsum('ikc,jkc->ijc', left_act, right_full, preferred_element_type=jnp.float32)
    pair_loc = residual(pair_loc, tri_finish(product, gate_act, tmo_out))
    left_act, right_act, gate_act = tri_gates(pair_loc, pair_mask, tmi_proj)
    left_cols = lax.all_to_all(left_act, GROUP_AXIS, 1, 0, tiled=True)
    right_full = lax.all_gather(right_act, GROUP_AXIS, axis=0, tiled=True)
    product = jnp.einsum('kic,kjc->ijc', left_cols, right_full, preferred_element_type=jnp.float32)
    pair_loc = residual(pair_loc, tri_finish(product, gate_act, tmi_out))
    pair_loc = residual(pair_loc, tri_attention(pair_loc, pair_mask, tas_qkvg, tas_bias, tas_out))
    pair_cols = lax.all_to_all(pair_loc, GROUP_AXIS, 1, 0, tiled=True)
    pair_t = jnp.swapaxes(pair_cols, 0, 1)
    pair_t = residual(pair_t, tri_attention(pair_t, pair_mask_t, tae_qkvg, tae_bias, tae_out))
    pair_loc = lax.all_to_all(jnp.swapaxes(pair_t, 0, 1), GROUP_AXIS, 0, 1, tiled=True)
    return residual(pair_loc, transition(pair_loc, ptr_in, ptr_out))


def evoformer_block(value_a7, pair_loc, full_mask, full_pair_mask, layer_w):
    (row_qkvg, row_bias, row_out, col_qkvg, col_out, mtr_in, mtr_out, opm_proj, opm_out) = layer_w[:9]
    shard_idx = lax.axis_index(GROUP_AXIS)
    seq_loc = value_a7.shape[0]
    res_loc = pair_loc.shape[0]
    seq_mask = lax.dynamic_slice_in_dim(full_mask, shard_idx * seq_loc, seq_loc, 0)
    res_mask = lax.dynamic_slice_in_dim(full_mask, shard_idx * res_loc, res_loc, 1)
    pair_mask = lax.dynamic_slice_in_dim(full_pair_mask, shard_idx * res_loc, res_loc, 0)
    pair_mask_t = lax.dynamic_slice_in_dim(full_pair_mask, shard_idx * res_loc, res_loc, 1).T
    value_a9 = row_bias.shape[1]
    row_bias_full = lax.all_gather(head_bias(layer_norm(pair_loc), row_bias), GROUP_AXIS, axis=1, tiled=True)
    value_a7 = residual(value_a7, self_attention(layer_norm(value_a7), row_qkvg, value_a9, row_bias_full, seq_mask, row_out))
    array_b7 = lax.all_to_all(value_a7, GROUP_AXIS, 1, 0, tiled=True)
    col_norm = jnp.swapaxes(layer_norm(array_b7), 0, 1)
    col_update = self_attention(col_norm, col_qkvg, value_a9, None, res_mask.T, col_out)
    array_b7 = residual(array_b7, jnp.swapaxes(col_update, 0, 1))
    array_b7 = residual(array_b7, transition(array_b7, mtr_in, mtr_out))
    pair_loc = residual(pair_loc, outer_update(array_b7, res_mask, full_mask, opm_proj, opm_out))
    pair_loc = pair_stack(pair_loc, pair_mask, pair_mask_t, layer_w[9:])
    value_a7 = lax.all_to_all(array_b7, GROUP_AXIS, 0, 1, tiled=True)
    return value_a7, pair_loc


def solution(mesh):
    row_spec = P((PARTS_AXIS, GROUP_AXIS))

    def local_body(value_a7, pair_loc, value_a12, pair_mask_loc, *weights):
        full_mask = lax.all_gather(value_a12, GROUP_AXIS, axis=0, tiled=True)
        full_pair_mask = lax.all_gather(pair_mask_loc, GROUP_AXIS, axis=0, tiled=True)
        for layer_idx in range(weights[0].shape[0]):
            layer_w = tuple(weight[layer_idx] for weight in weights)
            value_a7, pair_loc = evoformer_block(value_a7, pair_loc, full_mask, full_pair_mask, layer_w)
        return value_a7, pair_loc

    def run_blocks(*arrays):
        n_weights = len(arrays) - 4
        return jax.shard_map(local_body, mesh=mesh, in_specs=(row_spec,) * 4 + (P(),) * n_weights, out_specs=(row_spec, row_spec), check_vma=False)(*arrays)

    return run_blocks
```

profile of v0, /device:TPU:21, one launch (start us, length us, event | category | flops | bytes accessed | tf_op | source)
XLA Modules:
  0.0 1098.2 jit_solution(17007212930109638832)
XLA Ops:
  13.0 23.4 %all_gather.43 = bf16[8,128,128]{2,0,1:T(8,128)(2,1)S(1)} all-gather(bf16[8,8,128]{2,0,1:T(8,128)(2,1)S(1)} %fusion.154), channel_id=1, replica_groups=mesh['req'=4,'dap'=16] {'dap'}, dimensions={1}, use_global_device_ids=true | all-gather | bytes 278528 | tf_op jit(solution)/shard_map/all_gather | solution.py:122
  36.4 15.2 %all_gather.42 = s32[512,128]{1,0:T(8,128)S(1)} all-gather(s32[32,128]{1,0:T(8,128)S(1)} %copy-done.43), channel_id=1, replica_groups=mesh['req'=4,'dap'=16] {'dap'}, dimensions={0}, use_global_device_ids=true | all-gather | bytes 278528 | tf_op jit(solution)/shard_map/all_gather | solution.py:139
  73.2 12.0 %fusion.416 = (f32[32,8,128]{2,1,0:T(8,128)S(1)}, f32[32,8,128,128]{2,3,1,0:T(8,128)}) fusion(f32[8,128,128]{1,2,0:T(8,128)S(1)} %copy.1153, pred[32,128]{1,0:T(8,128)(4,1)S(1)} %dynamic-slice_compare_fusion.1, bf16[32,128,8,32]{1,3,2,0:T(8,128)(2,1)} %bitcast.548, bf16[32,128,8,32]{1,3,2,0:T(8,128)(2,1)} %bitcast.547), kind=kOutput, calls=%fused_computation.586 | convolution fusion | flops 289407104 | bytes 21630976 | tf_op jit(solution)/shard_map/sub | solution.py:37
  85.2 10.7 fusion.26
  96.0 5.6 copy.1155
  112.8 48.5 %all-to-all-done = bf16[32,128,256]{2,0,1:T(8,128)(2,1)S(1)} async-done(((bf16[32,128,256]{2,0,1:T(8,128)(2,1)}), bf16[32,128,256]{2,0,1:T(8,128)(2,1)S(1)}, u32[]{:S(2)}, u32[]{:S(2)}) %all-to-all-start) | async-done | bytes 2097184 | tf_op jit(solution)/shard_map/all_to_all | solution.py:124
  171.5 5.3 copy.1174
  196.9 34.8 %fusion.417 = (f32[8,8,512]{2,1,0:T(8,128)S(1)}, f32[8,8,512,512]{2,3,1,0:T(8,128)}) fusion(pred[8,512]{1,0:T(8,128)(4,1)S(1)} %compare_bitcast_fusion, bf16[8,512,8,32]{1,3,2,0:T(8,128)(2,1)} %bitcast.554, bf16[8,512,8,32]{1,3,2,0:T(8,128)(2,1)} %bitcast.551), kind=kOutput, calls=%fused_computation.587 | convolution fusion | flops 1140851200 | bytes 71438336 | tf_op jit(solution)/shard_map/sub | solution.py:37
  231.7 23.7 %fusion.16 = f32[8,8,32,512]{3,2,1,0:T(8,128)} fusion(bf16[8,512,8,32]{1,3,2,0:T(8,128)(2,1)S(1)} %bitcast.555, f32[8,8,512,512]{2,3,1,0:T(8,128)} %get-tuple-element.37, f32[8,8,512]{2,1,0:T(8,128)S(1)} %get-tuple-element.36), kind=kOutput, calls=%fused_computation.22 | convolution fusion | flops 1107296256 | bytes 73531392 | tf_op jit(solution)/shard_map/bhqk,bkhd->bqhd/dot_general | solution.py:38
  255.4 5.5 copy.1172
  260.9 5.6 convert_reduce_fusion.1
  267.9 7.3 convert_reduce_fusion.4
  277.4 16.3 %all_gather.45 = s32[128,128]{1,0:T(8,128)S(1)} all-gather(s32[8,128]{1,0:T(8,128)S(1)} %copy-done.46), channel_id=1, replica_groups=mesh['req'=4,'dap'=16] {'dap'}, dimensions={0}, use_global_device_ids=true | all-gather | bytes 69632 | tf_op jit(solution)/shard_map/all_gather | solution.py:140
  293.8 22.1 %all-gather.7.cloned.1.call-done = bf16[512,128,32]{0,2,1:T(8,128)(2,1)} async-done(((bf16[512,8,32]{0,2,1:T(8,128)(2,1)}), bf16[512,128,32]{0,2,1:T(8,128)(2,1)}) %all-gather.7.cloned.1.call-update) | async-done | bytes 4194320 | tf_op jit(solution)/shard_map/all_gather | solution.py:64
  315.9 7.4 convert_bitcast_fusion.4
  327.9 36.7 %all-gather.9.cloned.1.call-done = bf16[128,128,128]{2,1,0:T(8,128)(2,1)} async-done(((bf16[8,128,128]{2,1,0:T(8,128)(2,1)}), bf16[128,128,128]{2,1,0:T(8,128)(2,1)}) %all-gather.9.cloned.1.call-update) | async-done | bytes 4194320 | tf_op jit(solution)/shard_map/all_gather | solution.py:96
  364.6 6.7 copy.1195
  388.3 65.6 %all-to-all-done.1 = bf16[512,8,256]{2,1,0:T(8,128)(2,1)S(1)} async-done(((bf16[512,8,256]{2,1,0:T(8,128)(2,1)}), bf16[512,8,256]{2,1,0:T(8,128)(2,1)S(1)}, u32[]{:S(2)}, u32[]{:S(2)}) %all-to-all-start.1) | async-done | bytes 2097184 | tf_op jit(solution)/shard_map/all_to_all | solution.py:131
  453.9 5.5 all-to-all-start.2
  460.1 10.6 all-to-all-done.2
  472.6 6.7 copy.1209
  484.7 14.9 %all_gather.48 = bf16[4,128,128]{2,0,1:T(4,128)(2,1)S(1)} all-gather(bf16[4,8,128]{2,0,1:T(4,128)(2,1)S(1)} %fusion.156), channel_id=1, replica_groups=mesh['req'=4,'dap'=16] {'dap'}, dimensions={1}, use_global_device_ids=true | all-gather | bytes 139264 | tf_op jit(solution)/shard_map/all_gather | solution.py:88
  510.6 5.0 all-to-all-start.3
  517.7 9.2 all-to-all-done.3
  528.3 15.0 %all_gather.49 = bf16[4,128,128]{2,0,1:T(4,128)(2,1)S(1)} all-gather(bf16[4,8,128]{2,0,1:T(4,128)(2,1)S(1)} %fusion.157), channel_id=1, replica_groups=mesh['req'=4,'dap'=16] {'dap'}, dimensions={1}, use_global_device_ids=true | all-gather | bytes 139264 | tf_op jit(solution)/shard_map/all_gather | solution.py:88
  584.0 18.1 %all_gather.50 = bf16[8,128,128]{2,0,1:T(8,128)(2,1)S(1)} all-gather(bf16[8,8,128]{2,0,1:T(8,128)(2,1)S(1)} %fusion.155), channel_id=1, replica_groups=mesh['req'=4,'dap'=16] {'dap'}, dimensions={1}, use_global_device_ids=true | all-gather | bytes 278528 | tf_op jit(solution)/shard_map/all_gather | solution.py:122
  602.4 12.0 %fusion.434 = (f32[32,8,128]{2,1,0:T(8,128)S(1)}, f32[32,8,128,128]{2,3,1,0:T(8,128)}) fusion(f32[8,128,128]{1,2,0:T(8,128)S(1)} %copy.1236, pred[32,128]{1,0:T(8,128)(4,1)S(1)} %copy-done.50, bf16[32,128,8,32]{1,3,2,0:T(8,128)(2,1)} %bitcast.545, bf16[32,128,8,32]{1,3,2,0:T(8,128)(2,1)} %bitcast.543), kind=kOutput, calls=%fused_computation.596 | convolution fusion | flops 289407104 | bytes 21630976 | tf_op jit(solution)/shard_map/sub | solution.py:37
  614.4 10.7 fusion.27
  625.1 5.6 copy.1238
  636.1 55.6 %all_to_all.117 = bf16[32,128,256]{2,0,1:T(8,128)(2,1)S(1)} all-to-all(bf16[32,128,256]{2,0,1:T(8,128)(2,1)S(1)} %copy.1239), channel_id=1, replica_groups=mesh['req'=4,'dap'=16] {'dap'}, dimensions={1} | all-to-all | bytes 4194304 | tf_op jit(solution)/shard_map/all_to_all | solution.py:124
  701.9 5.3 copy.1256
  727.3 34.5 %fusion.435 = (f32[8,8,512]{2,1,0:T(8,128)S(1)}, f32[8,8,512,512]{2,3,1,0:T(8,128)}) fusion(pred[8,512]{1,0:T(8,128)(4,1)S(1)} %copy-done.48, bf16[8,512,8,32]{1,3,2,0:T(8,128)(2,1)} %bitcast.552, bf16[8,512,8,32]{1,3,2,0:T(8,128)(2,1)} %bitcast.550), kind=kOutput, calls=%fused_computation.597 | convolution fusion | flops 1140851200 | bytes 71438336 | tf_op jit(solution)/shard_map/sub | solution.py:37
  761.8 23.8 %fusion.17 = f32[8,8,32,512]{3,2,1,0:T(8,128)} fusion(bf16[8,512,8,32]{1,3,2,0:T(8,128)(2,1)S(1)} %bitcast.553, f32[8,8,512,512]{2,3,1,0:T(8,128)} %get-tuple-element.61, f32[8,8,512]{2,1,0:T(8,128)S(1)} %get-tuple-element.60), kind=kOutput, calls=%fused_computation.23 | convolution fusion | flops 1107296256 | bytes 73531392 | tf_op jit(solution)/shard_map/bhqk,bkhd->bqhd/dot_general | solution.py:38
  785.5 5.6 copy.1254
  791.2 5.7 convert_reduce_fusion
  798.2 7.1 convert_reduce_fusion.3
  808.0 35.2 %all-gather.13.cloned.1.call-done = bf16[512,128,32]{0,2,1:T(8,128)(2,1)} async-done(((bf16[512,8,32]{0,2,1:T(8,128)(2,1)}), bf16[512,128,32]{0,2,1:T(8,128)(2,1)}) %all-gather.13.cloned.1.call-update) | async-done | bytes 4194320 | tf_op jit(solution)/shard_map/all_gather | solution.py:64
  843.2 7.4 convert_bitcast_fusion.3
  856.0 36.9 %all-gather.15.cloned.1.call-done = bf16[128,128,128]{2,1,0:T(8,128)(2,1)} async-done(((bf16[8,128,128]{2,1,0:T(8,128)(2,1)}), bf16[128,128,128]{2,1,0:T(8,128)(2,1)}) %all-gather.15.cloned.1.call-update) | async-done | bytes 4194320 | tf_op jit(solution)/shard_map/all_gather | solution.py:96
  893.0 6.7 copy.1273
  907.6 17.8 %all_to_all.118 = bf16[8,128,128]{2,0,1:T(8,128)(2,1)S(1)} all-to-all(bf16[8,128,128]{2,0,1:T(8,128)(2,1)S(1)} %copy.1284), channel_id=1, replica_groups=mesh['req'=4,'dap'=16] {'dap'}, dimensions={1} | all-to-all | bytes 524288 | tf_op jit(solution)/shard_map/all_to_all | solution.py:100
  925.7 22.2 %all-gather.17.cloned.1.call-done = bf16[128,128,128]{2,1,0:T(8,128)(2,1)} async-done(((bf16[8,128,128]{2,1,0:T(8,128)(2,1)}), bf16[128,128,128]{2,1,0:T(8,128)(2,1)}) %all-gather.17.cloned.1.call-update) | async-done | bytes 4194320 | tf_op jit(solution)/shard_map/all_gather | solution.py:101
  947.9 6.7 copy.1287
  959.4 16.9 %all_gather.54 = bf16[4,128,128]{2,0,1:T(4,128)(2,1)S(1)} all-gather(bf16[4,8,128]{2,0,1:T(4,128)(2,1)S(1)} %fusion.158), channel_id=1, replica_groups=mesh['req'=4,'dap'=16] {'dap'}, dimensions={1}, use_global_device_ids=true | all-gather | bytes 139264 | tf_op jit(solution)/shard_map/all_gather | solution.py:88
  990.4 8.2 all-to-all-done.8
  1004.0 57.9 %all_gather.55 = bf16[4,128,128]{2,0,1:T(4,128)(2,1)S(1)} all-gather(bf16[4,8,128]{2,0,1:T(4,128)(2,1)S(1)} %fusion.159), channel_id=1, replica_groups=mesh['req'=4,'dap'=16] {'dap'}, dimensions={1}, use_global_device_ids=true | all-gather | bytes 139264 | tf_op jit(solution)/shard_map/all_gather | solution.py:88
  1072.3 5.4 all-to-all-start.9
  1079.3 9.7 all-to-all-done.9
  (395 shorter events, 247.6 us)
Async XLA Ops:
  7.2 44.7 %copy-start.3 = (bf16[32,128,256]{2,1,0:T(8,128)(2,1)S(1)}, bf16[32,128,256]{2,1,0:T(8,128)(2,1)}, u32[]{:S(2)}) copy-start(bf16[32,128,256]{2,1,0:T(8,128)(2,1)} %param.25) | copy-start | bytes 6291460
  7.2 29.2 %copy-start.43 = (s32[32,128]{1,0:T(8,128)S(1)}, s32[32,128]{1,0:T(8,128)}, u32[]{:S(2)}) copy-start(s32[32,128]{1,0:T(8,128)} %param.27) | copy-start | bytes 49156
  73.2 12.0 %copy-start.49 = (pred[32,128]{1,0:T(8,128)(4,1)}, pred[32,128]{1,0:T(8,128)(4,1)S(1)}, u32[]{:S(2)}) copy-start(pred[32,128]{1,0:T(8,128)(4,1)S(1)} %dynamic-slice_compare_fusion.1) | copy-start | bytes 12292
  95.9 5.6 copy-start.64
  108.3 53.0 %all-to-all-start = ((bf16[32,128,256]{2,0,1:T(8,128)(2,1)}), bf16[32,128,256]{2,0,1:T(8,128)(2,1)S(1)}, u32[]{:S(2)}, u32[]{:S(2)}) async-start(bf16[32,128,256]{2,0,1:T(8,128)(2,1)} %copy.1156), calls=%async_computation | async-start | bytes 4194304 | tf_op jit(solution)/shard_map/all_to_all | solution.py:124
  112.4 203.5 %all-gather.7.cloned.1.call-start = ((), (), s32[]{:S(2)}) async-start(), calls=%async_computation.10 | async-start | bytes 4456448 | tf_op jit(solution)/shard_map/all_gather | solution.py:64
  112.7 203.2 %copy-start.37 = (bf16[512,8]{0,1:T(8,128)(2,1)}, bf16[512,8]{0,1:T(8,128)(2,1)S(1)}, u32[]{:S(2)}) copy-start(bf16[512,8]{0,1:T(8,128)(2,1)S(1)} %convert_element_type.589) | copy-start | bytes 24580
  112.8 84.1 %copy-start.47 = (pred[8,512]{1,0:T(8,128)(4,1)}, pred[8,512]{1,0:T(8,128)(4,1)S(1)}, u32[]{:S(2)}) copy-start(pred[8,512]{1,0:T(8,128)(4,1)S(1)} %compare_bitcast_fusion) | copy-start | bytes 12292
  196.9 34.8 %copy-start.23 = (bf16[8,512,256]{1,2,0:T(8,128)(2,1)S(1)}, bf16[8,512,256]{1,2,0:T(8,128)(2,1)}, u32[]{:S(2)}) copy-start(bf16[8,512,256]{1,2,0:T(8,128)(2,1)} %copy.1167) | copy-start | bytes 6291460
  255.4 5.6 copy-start.66
  267.9 7.9 copy-start.70
  275.2 48.1 %copy-start.7 = (bf16[512,8,256]{0,2,1:T(8,128)(2,1)}, bf16[512,8,256]{0,2,1:T(8,128)(2,1)S(1)}, u32[]{:S(2)}) copy-start(bf16[512,8,256]{0,2,1:T(8,128)(2,1)S(1)} %get-tuple-element.41) | copy-start | bytes 6291460
  277.3 87.3 %all-gather.9.cloned.1.call-start = ((), (), s32[]{:S(2)}) async-start(), calls=%async_computation.11 | async-start | bytes 4456448 | tf_op jit(solution)/shard_map/all_gather | solution.py:96
  293.7 83.4 %copy-start.35 = (f32[8,128]{1,0:T(8,128)}, f32[8,128]{1,0:T(8,128)S(1)}, u32[]{:S(2)}) copy-start(f32[8,128]{1,0:T(8,128)S(1)} %dynamic-slice_convert_fusion) | copy-start | bytes 12292
  293.8 30.9 %copy-start.44 = (f32[8,128]{1,0:T(8,128)}, f32[8,128]{1,0:T(8,128)S(1)}, u32[]{:S(2)}) copy-start(f32[8,128]{1,0:T(8,128)S(1)} %convolution_add_fusion.2) | copy-start | bytes 12292
  327.8 144.8 %all-gather.11.cloned.1.call-start = ((), (), s32[]{:S(2)}) async-start(), calls=%async_computation.12 | async-start | bytes 4456448 | tf_op jit(solution)/shard_map/all_gather | solution.py:101
  382.9 70.9 %all-to-all-start.1 = ((bf16[512,8,256]{2,1,0:T(8,128)(2,1)}), bf16[512,8,256]{2,1,0:T(8,128)(2,1)S(1)}, u32[]{:S(2)}, u32[]{:S(2)}) async-start(bf16[512,8,256]{2,1,0:T(8,128)(2,1)} %copy.1177), calls=%async_computation.1 | async-start | bytes 4194304 | tf_op jit(solution)/shard_map/all_to_all | solution.py:131
  453.9 16.8 %all-to-all-start.2 = ((bf16[8,128,128]{2,0,1:T(8,128)(2,1)}), bf16[8,128,128]{2,0,1:T(8,128)(2,1)S(1)}, u32[]{:S(2)}, u32[]{:S(2)}) async-start(bf16[8,128,128]{2,0,1:T(8,128)(2,1)} %copy.1206), calls=%async_computation.2 | async-start | bytes 524288 | tf_op jit(solution)/shard_map/all_to_all | solution.py:100
  459.3 43.6 %copy-start.59 = (pred[8,128]{1,0:T(8,128)(4,1)}, pred[8,128]{1,0:T(8,128)(4,1)S(1)}, u32[]{:S(2)}) copy-start(pred[8,128]{1,0:T(8,128)(4,1)S(1)} %dynamic-slice_compare_fusion.2) | copy-start | bytes 3076
  459.4 87.6 %copy-start.57 = (pred[8,128]{1,0:T(8,128)(4,1)}, pred[8,128]{1,0:T(8,128)(4,1)S(1)}, u32[]{:S(2)}) copy-start(pred[8,128]{1,0:T(8,128)(4,1)S(1)} %copy.1225) | copy-start | bytes 3076
  508.3 19.5 %copy-start.53 = (bf16[2,128,4]{1,2,0:T(4,128)(2,1)S(1)}, bf16[2,128,4]{1,2,0:T(4,128)(2,1)}, u32[]{:S(2)}) copy-start(bf16[2,128,4]{1,2,0:T(4,128)(2,1)} %param.46) | copy-start | bytes 6148
  510.6 16.3 %all-to-all-start.3 = ((bf16[8,128,128]{2,0,1:T(8,128)(2,1)}), bf16[8,128,128]{2,0,1:T(8,128)(2,1)S(1)}, u32[]{:S(2)}, u32[]{:S(2)}) async-start(bf16[8,128,128]{2,0,1:T(8,128)(2,1)} %copy.1221), calls=%async_computation.3 | async-start | bytes 524288 | tf_op jit(solution)/shard_map/all_to_all | solution.py:105
  554.8 26.2 %all-to-all-start.4 = ((bf16[128,8,128]{2,1,0:T(8,128)(2,1)}), bf16[128,8,128]{2,1,0:T(8,128)(2,1)S(1)}, u32[]{:S(2)}, u32[]{:S(2)}) async-start(bf16[128,8,128]{2,1,0:T(8,128)(2,1)} %copy.1230), calls=%async_computation.4 | async-start | bytes 524288 | tf_op jit(solution)/shard_map/all_to_all | solution.py:108
  559.8 283.4 %all-gather.13.cloned.1.call-start = ((), (), s32[]{:S(2)}) async-start(), calls=%async_computation.13 | async-start | bytes 4456448 | tf_op jit(solution)/shard_map/all_gather | solution.py:64
  577.0 6.9 copy-start.56
  581.1 21.3 %copy-start.50 = (pred[32,128]{1,0:T(8,128)(4,1)S(1)}, pred[32,128]{1,0:T(8,128)(4,1)}, u32[]{:S(2)}) copy-start(pred[32,128]{1,0:T(8,128)(4,1)} %copy-done.49) | copy-start | bytes 12292
  583.7 30.7 %copy-start.24 = (f32[8,128,128]{1,2,0:T(8,128)}, f32[8,128,128]{1,2,0:T(8,128)S(1)}, u32[]{:S(2)}) copy-start(f32[8,128,128]{1,2,0:T(8,128)S(1)} %get-tuple-element.57) | copy-start | bytes 1572868
  625.1 5.6 copy-start.65
  721.0 6.3 copy-start.48
  727.3 34.5 %copy-start.22 = (bf16[8,512,256]{1,2,0:T(8,128)(2,1)S(1)}, bf16[8,512,256]{1,2,0:T(8,128)(2,1)}, u32[]{:S(2)}) copy-start(bf16[8,512,256]{1,2,0:T(8,128)(2,1)} %copy.1250) | copy-start | bytes 6291460
  785.5 5.6 copy-start.67
  791.1 7.1 copy-start.61
  798.2 7.8 copy-start.71
  805.3 45.2 %copy-start.5 = (bf16[512,8,256]{0,2,1:T(8,128)(2,1)}, bf16[512,8,256]{0,2,1:T(8,128)(2,1)S(1)}, u32[]{:S(2)}) copy-start(bf16[512,8,256]{0,2,1:T(8,128)(2,1)S(1)} %get-tuple-element.65) | copy-start | bytes 6291460
  807.5 85.5 %all-gather.15.cloned.1.call-start = ((), (), s32[]{:S(2)}) async-start(), calls=%async_computation.14 | async-start | bytes 4456448 | tf_op jit(solution)/shard_map/all_gather | solution.py:96
  856.0 91.9 %all-gather.17.cloned.1.call-start = ((), (), s32[]{:S(2)}) async-start(), calls=%async_computation.15 | async-start | bytes 4456448 | tf_op jit(solution)/shard_map/all_gather | solution.py:101
  899.7 5.9 copy-start.31
  958.3 18.3 %copy-start.60 = (pred[8,128]{1,0:T(8,128)(4,1)S(1)}, pred[8,128]{1,0:T(8,128)(4,1)}, u32[]{:S(2)}) copy-start(pred[8,128]{1,0:T(8,128)(4,1)} %copy-done.59) | copy-start | bytes 3076
  959.4 19.6 %copy-start.10 = (bf16[8,128,512]{1,2,0:T(8,128)(2,1)}, bf16[8,128,512]{1,2,0:T(8,128)(2,1)S(1)}, u32[]{:S(2)}) copy-start(bf16[8,128,512]{1,2,0:T(8,128)(2,1)S(1)} %convolution_convert_fusion.5) | copy-start | bytes 3145732
  979.0 8.4 copy-start.6
  983.4 15.2 %all-to-all-start.8 = ((bf16[8,128,128]{2,0,1:T(8,128)(2,1)}), bf16[8,128,128]{2,0,1:T(8,128)(2,1)S(1)}, u32[]{:S(2)}, u32[]{:S(2)}) async-start(bf16[8,128,128]{2,0,1:T(8,128)(2,1)} %copy.1299), calls=%async_computation.8 | async-start | bytes 524288 | tf_op jit(solution)/shard_map/all_to_all | solution.py:105
  987.3 16.1 %copy-start.54 = (bf16[2,128,4]{1,2,0:T(4,128)(2,1)S(1)}, bf16[2,128,4]{1,2,0:T(4,128)(2,1)}, u32[]{:S(2)}) copy-start(bf16[2,128,4]{1,2,0:T(4,128)(2,1)} %param.46) | copy-start | bytes 6148
  990.4 71.6 %copy-start.34 = (bf16[2,128,512]{2,1,0:T(8,128)(2,1)S(1)}, bf16[2,128,512]{2,1,0:T(8,128)(2,1)}, u32[]{:S(2)}) copy-start(bf16[2,128,512]{2,1,0:T(8,128)(2,1)} %param.45) | copy-start | bytes 786436
  998.6 73.7 %all-to-all-start.6 = ((bf16[512,8,256]{2,1,0:T(8,128)(2,1)}), bf16[512,8,256]{2,1,0:T(8,128)(2,1)S(1)}, u32[]{:S(2)}, u32[]{:S(2)}) async-start(bf16[512,8,256]{2,1,0:T(8,128)(2,1)} %copy.1259), calls=%async_computation.6 | async-start | bytes 4194304 | tf_op jit(solution)/shard_map/all_to_all | solution.py:131
  1002.5 61.9 %copy-start.58 = (pred[8,128]{1,0:T(8,128)(4,1)S(1)}, pred[8,128]{1,0:T(8,128)(4,1)}, u32[]{:S(2)}) copy-start(pred[8,128]{1,0:T(8,128)(4,1)} %copy-done.57) | copy-start | bytes 3076
  1069.8 19.9 %copy-start.68 = (bf16[2,512,128]{2,1,0:T(8,128)(2,1)S(1)}, bf16[2,512,128]{2,1,0:T(8,128)(2,1)}, u32[]{:S(2)}) copy-start(bf16[2,512,128]{2,1,0:T(8,128)(2,1)} %param.49) | copy-start | bytes 786436
  1069.8 19.9 %copy-start.69 = (bf16[2,128,512]{2,1,0:T(8,128)(2,1)S(1)}, bf16[2,128,512]{2,1,0:T(8,128)(2,1)}, u32[]{:S(2)}) copy-start(bf16[2,128,512]{2,1,0:T(8,128)(2,1)} %param.48) | copy-start | bytes 786436
  1072.3 16.7 %all-to-all-start.9 = ((bf16[128,8,128]{2,1,0:T(8,128)(2,1)}), bf16[128,8,128]{2,1,0:T(8,128)(2,1)S(1)}, u32[]{:S(2)}, u32[]{:S(2)}) async-start(bf16[128,8,128]{2,1,0:T(8,128)(2,1)} %copy.1307), calls=%async_computation.9 | async-start | bytes 524288 | tf_op jit(solution)/shard_map/all_to_all | solution.py:108
  (42 other events, 122.2 us)
Sparse Core Ops, SparseCore 0:
  277.4 38.4 all-gather.6
  328.0 36.5 all-gather.8
  380.0 75.7 all-gather.10
  807.6 35.5 all-gather.12
  856.1 36.8 all-gather.14
  907.5 40.3 all-gather.16
where the time goes:
time: 1100 us
  waiting for transfers between devices  305 us (28%)
  matrix products  277 us (25%)
  blocking collectives  251 us (23%)
  local copies, waits for them, and re-layouts  168 us (15%)
  other arithmetic  42.7 us (4%)
  starting transfers between devices  37.9 us (3%)
  between operations  16.1 us (1%)
    sub x8, matrix products, attend(): attn_prob = jax.nn.softmax(logits, axis=-1).astype(jnp.bfloat16)  106 us
    all_gather x4, blocking collectives, tri_attention(): lax.all_gather(head_bias(pair_norm, w_bias), GROUP_AXIS, axis=1, tiled=True)  105 us
    all_gather x4, waiting for transfers between devices, pair_stack(): right_full = lax.all_gather(right_act, GROUP_AXIS, axis=0, tiled=True)  95.8 us
    dot_general x8, matrix products, attend(): jnp.einsum('bhqk,bkhd->bqhd', attn_prob, v_heads, preferred_element_type=...  77 us
    all_to_all x2, waiting for transfers between devices, evoformer_block(): value_a7 = lax.all_to_all(array_b7, GROUP_AXIS, 0, 1, tiled=True)  65.6 us
    dot_general x32, matrix products, dense(): jnp.einsum('...c,cf->...f', x, weight, preferred_element_type=jnp.float32)  62.1 us
    all_gather x2, waiting for transfers between devices, outer_update(): right_full = lax.all_gather(right_act, GROUP_AXIS, axis=1, tiled=True)  57.3 us
    all_to_all x1, blocking collectives, evoformer_block(): array_b7 = lax.all_to_all(value_a7, GROUP_AXIS, 1, 0, tiled=True)  55.6 us
  transfers between devices with their start and end apart: 14, of which 11 were waited for; matrix products, arithmetic and copies ran while one was open for 4% of the time, Pallas kernels for 0%

commit v1 on v0

v1 whole, which is shorter than its diff:
```python
import functools
import math

import jax
import jax.numpy as jnp
from jax import lax
from jax.experimental import pallas as pl
from jax.experimental.pallas import tpu as pltpu
from jax.sharding import PartitionSpec as P

GROUP_AXIS = 'dap'
PARTS_AXIS = 'req'
LOG2E = math.log2(math.e)
MASKED = -1e9 * LOG2E
LANES = 128
F32 = jnp.float32
BF16 = jnp.bfloat16
NT = (((1,), (1,)), ((), ()))
TN = (((0,), (0,)), ((), ()))


def layer_norm_f32(values):
    centered = values - jnp.mean(values, axis=-1, keepdims=True)
    variance = jnp.mean(centered * centered, axis=-1, keepdims=True)
    return (centered * lax.rsqrt(variance + 1e-5)).astype(BF16)


def layer_norm(x):
    return layer_norm_f32(x.astype(F32))


def residual(x, update):
    return (x.astype(F32) + update).astype(BF16)


def dense(x, weight):
    return jnp.einsum('...c,cf->...f', x, weight, preferred_element_type=F32)


def softmax_keys_first(logits):
    top = jnp.max(logits, axis=0, keepdims=True)
    raised = jnp.exp2(logits - top)
    total = jnp.sum(raised, axis=0, keepdims=True)
    return (raised * (1.0 / total)).astype(BF16)


def row_attention_kernel(heads, x_ref, mask_ref, bias_ref, w_ref, wo_ref, o_ref, proj, gated, *stage, swap_in, swap_out):
    width = wo_ref.shape[0]
    head_dim = width // heads
    scale = head_dim ** -0.5 * LOG2E
    n_seq = mask_ref.shape[0]
    length = mask_ref.shape[1]
    stage = list(stage)
    if swap_in:
        stage_in = stage.pop(0)
        for part in range(stage_in.shape[0]):
            stage_in[part] = x_ref[:, :, part * LANES:(part + 1) * LANES].astype(F32).reshape(stage_in.shape[1:])
    if swap_out:
        stage_out = stage.pop(0)

    def one_row(s, carry):
        if swap_in:
            x = jnp.concatenate([stage_in[part, pl.ds(s, length, stride=n_seq), :] for part in range(stage_in.shape[0])], -1)
        else:
            x = x_ref[s].astype(F32)
        x_norm = layer_norm_f32(x)
        proj[...] = lax.dot_general(w_ref[...], x_norm, NT, preferred_element_type=F32).astype(BF16)
        kept = mask_ref[s] > 0.0
        for h in range(heads):
            lo = h * head_dim
            q_t = proj[lo:lo + head_dim, :]
            k_t = proj[width + lo:width + lo + head_dim, :]
            v_t = proj[2 * width + lo:2 * width + lo + head_dim, :]
            g_t = proj[3 * width + lo:3 * width + lo + head_dim, :].astype(F32)
            logits = lax.dot_general(k_t, q_t, TN, preferred_element_type=F32) * scale + bias_ref[h]
            prob = softmax_keys_first(jnp.where(kept, logits, MASKED))
            out_t = jnp.dot(v_t, prob, preferred_element_type=F32)
            gated[lo:lo + head_dim, :] = (out_t * jax.nn.sigmoid(g_t)).astype(BF16)
        update = lax.dot_general(gated[...], wo_ref[...], TN, preferred_element_type=F32)
        result = x + update
        if swap_out:
            for part in range(stage_out.shape[0]):
                stage_out[part, pl.ds(s, length, stride=n_seq), :] = result[:, part * LANES:(part + 1) * LANES]
        else:
            o_ref[s] = result.astype(BF16)
        return carry

    lax.fori_loop(0, n_seq, one_row, 0)
    if swap_out:
        for part in range(stage_out.shape[0]):
            o_ref[:, :, part * LANES:(part + 1) * LANES] = stage_out[part].reshape(length, n_seq, LANES).astype(BF16)


def row_attention(x, mask_lanes, bias_t, w_qkvg_t, w_out, heads, block, swap_in=False, swap_out=False):
    n_rows, length = mask_lanes.shape[:2]
    dim = x.shape[-1]
    width = w_out.shape[0]
    natural = pl.BlockSpec((block, length, dim), lambda i: (i, 0, 0))
    swapped = pl.BlockSpec((length, block, dim), lambda i: (0, i, 0))
    whole2 = lambda shape: pl.BlockSpec(shape, lambda i: (0,) * len(shape))
    scratch = [pltpu.VMEM((4 * width, length), BF16), pltpu.VMEM((width, length), BF16)]
    scratch += [pltpu.VMEM((dim // LANES, length * block, LANES), F32)] * (int(swap_in) + int(swap_out))
    out_shape = (length, n_rows, dim) if swap_out else (n_rows, length, dim)
    return pl.pallas_call(
        functools.partial(row_attention_kernel, heads, swap_in=swap_in, swap_out=swap_out),
        grid=(n_rows // block,),
        in_specs=[
            swapped if swap_in else natural,
            pl.BlockSpec((block, length, length), lambda i: (i, 0, 0)),
            whole2(bias_t.shape), whole2(w_qkvg_t.shape), whole2(w_out.shape),
        ],
        out_specs=swapped if swap_out else natural,
        out_shape=jax.ShapeDtypeStruct(out_shape, BF16),
        scratch_shapes=scratch,
        cost_estimate=pl.CostEstimate(flops=n_rows * length * (dim * width * 10 + 4 * length * width), bytes_accessed=4 * x.size, transcendentals=n_rows * heads * length * length),
        name='row_attention',
    )(x, mask_lanes, bias_t, w_qkvg_t, w_out)


def column_kernel(heads, x_ref, mask_ref, mrow_ref, w_ref, wo_ref, win_ref, wtr_ref, wopm_ref, o_ref, ab_ref, proj, gated):
    width = wo_ref.shape[0]
    head_dim = width // heads
    scale = head_dim ** -0.5 * LOG2E
    length = mask_ref.shape[1]
    lanes = mask_ref.shape[2]
    x = x_ref[...].reshape(length, x_ref.shape[-1]).astype(F32)
    proj[...] = lax.dot_general(w_ref[...], layer_norm_f32(x), NT, preferred_element_type=F32).astype(BF16)

    def one_head(h, carry):
        lo = pl.multiple_of(h * head_dim, head_dim)
        keys = proj[pl.ds(width + lo, head_dim), :].T
        v_t = proj[pl.ds(2 * width + lo, head_dim), :]
        for c in range(length // lanes):
            cols = slice(c * lanes, (c + 1) * lanes)
            q_t = proj[pl.ds(lo, head_dim), cols]
            g_t = proj[pl.ds(3 * width + lo, head_dim), cols].astype(F32)
            logits = jnp.dot(keys, q_t, preferred_element_type=F32) * scale
            prob = softmax_keys_first(jnp.where(mask_ref[0] > 0.0, logits, MASKED))
            out_t = jnp.dot(v_t, prob, preferred_element_type=F32)
            gated[pl.ds(lo, head_dim), cols] = (out_t * jax.nn.sigmoid(g_t)).astype(BF16)
        return carry

    lax.fori_loop(0, heads, one_head, 0)
    update = lax.dot_general(gated[...], wo_ref[...], TN, preferred_element_type=F32)
    x = (x + update).astype(BF16).astype(F32)
    hidden = jnp.maximum(jnp.dot(layer_norm_f32(x), win_ref[...], preferred_element_type=F32), 0.0).astype(BF16)
    x = (x + jnp.dot(hidden, wtr_ref[...], preferred_element_type=F32)).astype(BF16)
    o_ref[...] = x.reshape(o_ref.shape)
    ab_t = lax.dot_general(wopm_ref[...], layer_norm_f32(x.astype(F32)), NT, preferred_element_type=F32).astype(BF16)
    ab_ref[0] = (ab_t.astype(F32) * mrow_ref[0]).astype(BF16)


def column_stack(x, mask_lanes, mask_row, w_qkvg_t, w_out, w_in, w_tr, w_opm_t, heads):
    n_dev, n_res, n_seq, dim = x.shape
    length = n_dev * n_seq
    width = w_out.shape[0]
    block = pl.BlockSpec((n_dev, 1, n_seq, dim), lambda r: (0, r, 0, 0))
    whole2 = lambda shape: pl.BlockSpec(shape, lambda i: (0,) * len(shape))
    n_opm = w_opm_t.shape[0]
    return pl.pallas_call(
        functools.partial(column_kernel, heads),
        grid=(n_res,),
        in_specs=[
            block,
            pl.BlockSpec((1, length, mask_lanes.shape[2]), lambda r: (r, 0, 0)),
            pl.BlockSpec((1, 1, length), lambda r: (r, 0, 0)),
            whole2(w_qkvg_t.shape), whole2(w_out.shape), whole2(w_in.shape), whole2(w_tr.shape), whole2(w_opm_t.shape),
        ],
        out_specs=[block, pl.BlockSpec((1, n_opm, length), lambda r: (r, 0, 0))],
        out_shape=[jax.ShapeDtypeStruct(x.shape, BF16), jax.ShapeDtypeStruct((n_res, n_opm, length), BF16)],
        scratch_shapes=[pltpu.VMEM((4 * width, length), BF16), pltpu.VMEM((width, length), BF16)],
        cost_estimate=pl.CostEstimate(flops=n_res * length * (dim * width * 26 + 4 * length * width), bytes_accessed=4 * x.size, transcendentals=n_res * heads * length * length),
        name='column_stack',
    )(x, mask_lanes, mask_row, w_qkvg_t, w_out, w_in, w_tr, w_opm_t)


def head_bias(pair_norm, w_bias):
    return jnp.einsum('ijc,ch->hij', pair_norm, w_bias, preferred_element_type=F32).astype(BF16)


def gather_bias(pair_rows, w_bias):
    full = lax.all_gather(head_bias(layer_norm(pair_rows), w_bias), GROUP_AXIS, axis=1, tiled=True)
    return jnp.swapaxes(full, 1, 2).astype(F32) * LOG2E


def transition(x, w_in, w_out):
    hidden = jnp.maximum(dense(layer_norm(x), w_in), 0.0).astype(BF16)
    return dense(hidden, w_out)


def outer_update(ab, overlap, w_out):
    opm_dim = ab.shape[1] // 2
    left_act = ab[:, :opm_dim]
    right_full = lax.all_gather(ab[:, opm_dim:], GROUP_AXIS, axis=0, tiled=True)
    outer_prod = jnp.einsum('ics,jes->ijce', left_act, right_full, preferred_element_type=F32).astype(BF16)
    n_rows, n_cols = outer_prod.shape[:2]
    update = dense(outer_prod.reshape(n_rows, n_cols, opm_dim * opm_dim), w_out)
    return update / (1e-3 + overlap)[:, :, None]


def tri_gates(pair_rows, mask_rows, w_proj):
    tri_dim = (w_proj.shape[1] - pair_rows.shape[-1]) // 4
    projected = dense(layer_norm(pair_rows), w_proj)
    mask_f = mask_rows[:, :, None]
    left_act = (mask_f * jax.nn.sigmoid(projected[..., 2 * tri_dim:3 * tri_dim]) * projected[..., :tri_dim]).astype(BF16)
    right_act = (mask_f * jax.nn.sigmoid(projected[..., 3 * tri_dim:4 * tri_dim]) * projected[..., tri_dim:2 * tri_dim]).astype(BF16)
    gate_act = jax.nn.sigmoid(projected[..., 4 * tri_dim:])
    return left_act, right_act, gate_act


def tri_finish(product, gate_act, w_out):
    return gate_act * dense(layer_norm(product), w_out)


def tri_attention(pair_rows, mask_lanes, w_qkvg, w_bias, w_out):
    bias_t = gather_bias(pair_rows, w_bias)
    return row_attention(pair_rows, mask_lanes, bias_t, w_qkvg.T, w_out, w_bias.shape[1], pair_rows.shape[0])


def pair_stack(pair_loc, masks, pair_w):
    (tmo_proj, tmo_out, tmi_proj, tmi_out, tas_qkvg, tas_bias, tas_out,
     tae_qkvg, tae_bias, tae_out, ptr_in, ptr_out) = pair_w
    pair_mask = masks['pair_rows']
    left_act, right_act, gate_act = tri_gates(pair_loc, pair_mask, tmo_proj)
    right_full = lax.all_gather(right_act, GROUP_AXIS, axis=0, tiled=True)
    product = jnp.einsum('ikc,jkc->ijc', left_act, right_full, preferred_element_type=F32)
    pair_loc = residual(pair_loc, tri_finish(product, gate_act, tmo_out))
    left_act, right_act, gate_act = tri_gates(pair_loc, pair_mask, tmi_proj)
    left_cols = lax.all_to_all(left_act, GROUP_AXIS, 1, 0, tiled=True)
    right_full = lax.all_gather(right_act, GROUP_AXIS, axis=0, tiled=True)
    product = jnp.einsum('kic,kjc->ijc', left_cols, right_full, preferred_element_type=F32)
    pair_loc = residual(pair_loc, tri_finish(product, gate_act, tmi_out))
    pair_loc = tri_attention(pair_loc, masks['start'], tas_qkvg, tas_bias, tas_out)
    pair_cols = lax.all_to_all(pair_loc, GROUP_AXIS, 1, 0, tiled=True)
    pair_t = jnp.swapaxes(pair_cols, 0, 1)
    pair_t = tri_attention(pair_t, masks['end'], tae_qkvg, tae_bias, tae_out)
    pair_loc = lax.all_to_all(jnp.swapaxes(pair_t, 0, 1), GROUP_AXIS, 0, 1, tiled=True)
    return residual(pair_loc, transition(pair_loc, ptr_in, ptr_out))


def evoformer_block(value_a7, pair_loc, masks, layer_w, first):
    (row_qkvg, row_bias, row_out, col_qkvg, col_out, mtr_in, mtr_out, opm_proj, opm_out) = layer_w[:9]
    heads = row_bias.shape[1]
    n_dev = masks['n_dev']
    bias_t = gather_bias(pair_loc, row_bias)
    value_a7 = row_attention(value_a7, masks['seq'], bias_t, row_qkvg.T, row_out, heads, 16, swap_in=not first, swap_out=True)
    length, n_seq, dim = value_a7.shape
    by_dev = value_a7.reshape(n_dev, length // n_dev, n_seq, dim)
    by_res = lax.all_to_all(by_dev, GROUP_AXIS, 0, 0, tiled=True)
    by_res, ab = column_stack(by_res, masks['res'], masks['res_row'], col_qkvg.T, col_out, mtr_in, mtr_out, opm_proj.T, heads)
    pair_loc = residual(pair_loc, outer_update(ab, masks['overlap'], opm_out))
    pair_loc = pair_stack(pair_loc, masks, layer_w[9:])
    value_a7 = lax.all_to_all(by_res, GROUP_AXIS, 0, 0, tiled=True).reshape(length, n_seq, dim)
    return value_a7, pair_loc


def make_masks(msa_mask, pair_mask, n_dev):
    shard_idx = lax.axis_index(GROUP_AXIS)
    n_seq, length = msa_mask.shape
    n_res = pair_mask.shape[0]
    packed = jnp.concatenate([msa_mask, pair_mask], 0).astype(BF16)
    full = lax.all_gather(packed, GROUP_AXIS, axis=0, tiled=True).reshape(n_dev, n_seq + n_res, length).astype(F32)
    full_msa = full[:, :n_seq].reshape(n_dev * n_seq, length)
    full_pair = full[:, n_seq:].reshape(n_dev * n_res, length)
    res_mask = lax.dynamic_slice_in_dim(full_msa, shard_idx * n_res, n_res, 1).T
    end_mask = lax.dynamic_slice_in_dim(full_pair, shard_idx * n_res, n_res, 1).T
    lanes = lambda mask: jnp.broadcast_to(mask.astype(F32)[:, :, None], mask.shape + (length,))
    return {
        'n_dev': n_dev,
        'seq': lanes(msa_mask),
        'res': lanes(res_mask),
        'res_row': res_mask[:, None, :],
        'pair_rows': pair_mask.astype(F32),
        'start': lanes(pair_mask),
        'end': lanes(end_mask),
        'overlap': jnp.dot(res_mask, full_msa, precision=lax.Precision.DEFAULT, preferred_element_type=F32),
    }


def solution(mesh):
    row_spec = P((PARTS_AXIS, GROUP_AXIS))
    n_dev = mesh.shape[GROUP_AXIS]

    def local_body(value_a7, pair_loc, msa_mask, pair_mask, *weights):
        masks = make_masks(msa_mask, pair_mask, n_dev)
        for layer_idx in range(weights[0].shape[0]):
            layer_w = tuple(weight[layer_idx] for weight in weights)
            value_a7, pair_loc = evoformer_block(value_a7, pair_loc, masks, layer_w, layer_idx == 0)
        return jnp.swapaxes(value_a7, 0, 1), pair_loc

    def run_blocks(*arrays):
        n_weights = len(arrays) - 4
        return jax.shard_map(local_body, mesh=mesh, in_specs=(row_spec,) * 4 + (P(),) * n_weights, out_specs=(row_spec, row_spec), check_vma=False)(*arrays)

    return run_blocks
```

time: 1100 us -> 1200 us (1.091)
  Pallas kernels: 0 us -> 445 us
  matrix products: 277 us -> 43.9 us
  local copies, waits for them, and re-layouts: 168 us -> 84.2 us
  waiting for transfers between devices: 305 us -> 274 us
  other arithmetic: 42.7 us -> 18.7 us
  blocking collectives: 251 us -> 275 us
    pallas_call x0 -> x8, Pallas kernels: none -> 445 us  [the longest x2 229 us: column_stack(): pl.pallas_call(functools.partial(column_kernel, heads), grid=(n_res,), in...]
    dot_general x51 -> x23, matrix products: 165 us -> 37.1 us  [the longest x2 14.8 us: outer_update(): jnp.einsum('ics,jes->ijce', left_act, right_full, preferred_element_type=...]
    sub x8 -> x0, matrix products: 106 us -> none  [attend(): attn_prob = jax.nn.softmax(logits, axis=-1).astype(jnp.bfloat16)]
    all_to_all x3 -> x4, waiting for transfers between devices: 114 us -> 47.7 us  [the longest x2 47.7 us: evoformer_block(): by_res = lax.all_to_all(by_dev, GROUP_AXIS, 0, 0, tiled=True)]
    all_gather x8 -> x7, blocking collectives: 178 us -> 244 us  [the longest x6 184 us: gather_bias(): lax.all_gather(head_bias(layer_norm(pair_rows), w_bias), GROUP_AXIS, axis...]
    slice x20 -> x8, local copies, waits for them, and re-layouts: 60.2 us -> 8.64 us  [the longest x4 5.27 us: local_body(): layer_w = tuple((weight[layer_idx] for weight in weights))]
    all_to_all x2, blocking collectives: 73.5 us -> 31.6 us  [the longest x1 16.3 us: pair_stack(): lax.all_to_all(jnp.swapaxes(pair_t, 0, 1), GROUP_AXIS, 0, 1, tiled=True)]
    convert_element_type x25 -> x2, local copies, waits for them, and re-layouts: 36.8 us -> 2.71 us  [outer_update(): jnp.einsum('ics,jes->ijce', left_act, right_full, preferred_element_type=...]
  transfers between devices with their start and end apart: 14 -> 14, of which waited for: 11 -> 11; matrix products, arithmetic and copies ran while one was open for 4% -> 3% of each run, Pallas kernels for 0% -> 1%
where the time goes in v1:
time: 1200 us
  Pallas kernels  445 us (37%)
  blocking collectives  275 us (23%)
  waiting for transfers between devices  274 us (23%)
  local copies, waits for them, and re-layouts  84.2 us (7%)
  matrix products  43.9 us (4%)
  starting transfers between devices  38 us (3%)
  other arithmetic  18.7 us (2%)
  between operations  15.5 us (1%)
    pallas_call x2, Pallas kernels, column_stack(): pl.pallas_call(functools.partial(column_kernel, heads), grid=(n_res,), in...  229 us
    pallas_call x6, Pallas kernels, row_attention(): pl.pallas_call(functools.partial(row_attention_kernel, heads, swap_in=swa...  217 us
    all_gather x6, blocking collectives, gather_bias(): lax.all_gather(head_bias(layer_norm(pair_rows), w_bias), GROUP_AXIS, axis...  184 us
    all_gather x4, waiting for transfers between devices, pair_stack(): right_full = lax.all_gather(right_act, GROUP_AXIS, axis=0, tiled=True)  111 us
    all_gather x2, waiting for transfers between devices, outer_update(): right_full = lax.all_gather(ab[:, opm_dim:], GROUP_AXIS, axis=0, tiled=True)  75.9 us
    all_gather x1, blocking collectives, make_masks(): lax.all_gather(packed, GROUP_AXIS, axis=0, tiled=True)  59.8 us
    all_to_all x2, waiting for transfers between devices, evoformer_block(): by_res = lax.all_to_all(by_dev, GROUP_AXIS, 0, 0, tiled=True)  47.7 us
    all_gather x4, local copies, waits for them, and re-layouts, pair_stack(): right_full = lax.all_gather(right_act, GROUP_AXIS, axis=0, tiled=True)  26.8 us
  transfers between devices with their start and end apart: 14, of which 11 were waited for; matrix products, arithmetic and copies ran while one was open for 3% of the time, Pallas kernels for 1%

profile of v1, /device:TPU:21, one launch (start us, length us, event | category | flops | bytes accessed | tf_op | source)
XLA Modules:
  0.0 1195.1 jit_solution(9542100575080090091)
XLA Ops:
  11.9 23.4 %all_gather.39 = bf16[8,128,128]{2,0,1:T(8,128)(2,1)S(1)} all-gather(bf16[8,8,128]{2,0,1:T(8,128)(2,1)S(1)} %fusion.31), channel_id=1, replica_groups=mesh['req'=4,'dap'=16] {'dap'}, dimensions={1}, use_global_device_ids=true | all-gather | bytes 278528 | tf_op jit(solution)/shard_map/all_gather | solution.py:182
  40.9 80.1 %row_attention.6 = bf16[128,32,256]{2,1,0:T(8,128)(2,1)} custom-call(bf16[32,128,256]{2,1,0:T(8,128)(2,1)} %x_ref.1, f32[32,128,128]{2,1,0:T(8,128)} %broadcast_in_dim.8.mask_ref, f32[8,128,128]{2,1,0:T(8,128)} %multiply_bitcast_fusion.1.bias_ref, bf16[1024,256]{1,0:T(8,128)(2,1)} %bitcast.360, bf16[256,256]{1,0:T(8,128)(2,1)} %get-tuple-element.33.wo_ref), custom_call_target="tpu_custom_call" | custom-call | flops 3221225472 | bytes 4194304 | tf_op jit(solution)/shard_map/row_attention/pallas_call | solution.py:104
  121.0 4.0 all-to-all-start
  125.2 59.8 %all_gather.40 = bf16[640,128]{1,0:T(8,128)(2,1)S(1)} all-gather(bf16[40,128]{1,0:T(8,128)(2,1)S(1)} %pad_maximum_fusion), channel_id=1, replica_groups=mesh['req'=4,'dap'=16] {'dap'}, dimensions={0}, use_global_device_ids=true | all-gather | bytes 174080 | tf_op jit(solution)/shard_map/all_gather | solution.py:262
  190.4 2.3 slice_bitcast_fusion.1
  195.8 114.4 %column_stack.2 = (bf16[16,8,32,256]{3,2,1,0:T(8,128)(2,1)}, bf16[8,64,512]{2,1,0:T(8,128)(2,1)}) custom-call(bf16[16,8,32,256]{3,2,1,0:T(8,128)(2,1)} %copy-done.4, f32[8,512,128]{2,1,0:T(8,128)} %broadcast_in_dim.9.mask_ref, f32[8,1,512]{2,1,0:T(1,128)} %broadcast_in_dim.10.mrow_ref, bf16[1024,256]{1,0:T(8,128)(2,1)} %bitcast.358, ...), custom_call_target="tpu_custom_call" | custom-call | flops 9126805504 | bytes 4194304 | tf_op jit(solution)/shard_map/column_stack/pallas_call | solution.py:160
  312.5 38.1 %all-gather.7.cloned.1.call-done = bf16[128,32,512]{2,1,0:T(8,128)(2,1)} async-done(((bf16[8,32,512]{2,1,0:T(8,128)(2,1)}), bf16[128,32,512]{2,1,0:T(8,128)(2,1)}) %all-gather.7.cloned.1.call-update) | async-done | bytes 4194320 | tf_op jit(solution)/shard_map/all_gather | solution.py:194
  350.5 7.4 convert_bitcast_fusion.1
  363.1 36.3 %all-gather.9.cloned.1.call-done = bf16[128,128,128]{2,1,0:T(8,128)(2,1)} async-done(((bf16[8,128,128]{2,1,0:T(8,128)(2,1)}), bf16[128,128,128]{2,1,0:T(8,128)(2,1)}) %all-gather.9.cloned.1.call-update) | async-done | bytes 4194320 | tf_op jit(solution)/shard_map/all_gather | solution.py:225
  399.4 6.8 copy.399
  406.2 4.5 fusion.215
  415.4 4.4 all-to-all-start.2
  425.3 8.6 all-to-all-done.2
  437.5 18.2 %all-gather.11.cloned.1.call-done = bf16[128,128,128]{2,1,0:T(8,128)(2,1)} async-done(((bf16[8,128,128]{2,1,0:T(8,128)(2,1)}), bf16[128,128,128]{2,1,0:T(8,128)(2,1)}) %all-gather.11.cloned.1.call-update) | async-done | bytes 4194320 | tf_op jit(solution)/shard_map/all_gather | solution.py:230
  455.8 6.7 copy.407
  462.5 3.4 fusion.217
  467.8 16.4 %all_gather.44 = bf16[4,128,128]{2,0,1:T(4,128)(2,1)S(1)} all-gather(bf16[4,8,128]{2,0,1:T(4,128)(2,1)S(1)} %fusion.33), channel_id=1, replica_groups=mesh['req'=4,'dap'=16] {'dap'}, dimensions={1}, use_global_device_ids=true | all-gather | bytes 139264 | tf_op jit(solution)/shard_map/all_gather | solution.py:182
  486.1 13.8 %row_attention.7 = bf16[8,128,128]{2,1,0:T(8,128)(2,1)} custom-call(bf16[8,128,128]{2,1,0:T(8,128)(2,1)} %copy-done.13, f32[8,128,128]{2,1,0:T(8,128)} %mul.309.mask_ref, f32[4,128,128]{2,1,0:T(8,128)} %multiply_bitcast_fusion.5.bias_ref, bf16[512,128]{1,0:T(8,128)(2,1)} %bitcast.353, bf16[128,128]{1,0:T(8,128)(2,1)} %get-tuple-element.37.wo_ref), custom_call_target="tpu_custom_call" | custom-call | flops 234881024 | bytes 524288 | tf_op jit(solution)/shard_map/row_attention/pallas_call | solution.py:104
  501.7 4.1 all-to-all-start.3
  508.1 9.1 all-to-all-done.3
  518.1 14.9 %all_gather.45 = bf16[4,128,128]{2,0,1:T(4,128)(2,1)S(1)} all-gather(bf16[4,8,128]{2,0,1:T(4,128)(2,1)S(1)} %fusion.34), channel_id=1, replica_groups=mesh['req'=4,'dap'=16] {'dap'}, dimensions={1}, use_global_device_ids=true | all-gather | bytes 139264 | tf_op jit(solution)/shard_map/all_gather | solution.py:182
  535.6 13.8 %row_attention.8 = bf16[8,128,128]{2,1,0:T(8,128)(2,1)} custom-call(bf16[8,128,128]{2,1,0:T(8,128)(2,1)} %copy_bitcast_fusion.2.x_ref, f32[8,128,128]{2,1,0:T(8,128)} %broadcast_in_dim.11.mask_ref, f32[4,128,128]{2,1,0:T(8,128)} %multiply_bitcast_fusion.4.bias_ref, bf16[512,128]{1,0:T(8,128)(2,1)} %bitcast.355, bf16[128,128]{1,0:T(8,128)(2,1)} %get-tuple-element.35.wo_ref), custom_call_target="tpu_custom_call" | custom-call | flops 234881024 | bytes 524288 | tf_op jit(solution)/shard_map/row_attention/pallas_call | solution.py:104
  550.6 16.3 %all_to_all.110 = bf16[128,8,128]{2,1,0:T(8,128)(2,1)S(1)} all-to-all(bf16[128,8,128]{2,1,0:T(8,128)(2,1)S(1)} %copy.419), channel_id=1, replica_groups=mesh['req'=4,'dap'=16] {'dap'}, dimensions={0} | all-to-all | bytes 524288 | tf_op jit(solution)/shard_map/all_to_all | solution.py:237
  566.9 4.1 all-to-all-start.1
  575.9 54.9 %all_gather.46 = bf16[8,128,128]{2,0,1:T(8,128)(2,1)S(1)} all-gather(bf16[8,8,128]{2,0,1:T(8,128)(2,1)S(1)} %fusion.32), channel_id=1, replica_groups=mesh['req'=4,'dap'=16] {'dap'}, dimensions={1}, use_global_device_ids=true | all-gather | bytes 278528 | tf_op jit(solution)/shard_map/all_gather | solution.py:182
  633.2 81.4 %row_attention.9 = bf16[128,32,256]{2,1,0:T(8,128)(2,1)} custom-call(bf16[128,32,256]{2,1,0:T(8,128)(2,1)} %bitcast.342, f32[32,128,128]{2,1,0:T(8,128)} %broadcast_in_dim.8.mask_ref, f32[8,128,128]{2,1,0:T(8,128)} %multiply_bitcast_fusion.bias_ref, bf16[1024,256]{1,0:T(8,128)(2,1)} %bitcast.357, bf16[256,256]{1,0:T(8,128)(2,1)} %get-tuple-element.32.wo_ref), custom_call_target="tpu_custom_call" | custom-call | flops 3221225472 | bytes 4194304 | tf_op jit(solution)/shard_map/row_attention/pallas_call | solution.py:104
  714.6 5.5 all-to-all-start.5
  721.2 47.7 %all-to-all-done.5.x_ref = bf16[16,8,32,256]{3,2,1,0:T(8,128)(2,1)S(1)} async-done(((bf16[16,8,32,256]{3,2,1,0:T(8,128)(2,1)}), bf16[16,8,32,256]{3,2,1,0:T(8,128)(2,1)S(1)}, u32[]{:S(2)}, u32[]{:S(2)}) %all-to-all-start.5) | async-done | bytes 2097184 | tf_op jit(solution)/shard_map/all_to_all | solution.py:249
  770.2 114.4 %column_stack.3 = (bf16[16,8,32,256]{3,2,1,0:T(8,128)(2,1)}, bf16[8,64,512]{2,1,0:T(8,128)(2,1)}) custom-call(bf16[16,8,32,256]{3,2,1,0:T(8,128)(2,1)} %copy-done.6, f32[8,512,128]{2,1,0:T(8,128)} %broadcast_in_dim.9.mask_ref, f32[8,1,512]{2,1,0:T(1,128)} %broadcast_in_dim.10.mrow_ref, bf16[1024,256]{1,0:T(8,128)(2,1)} %bitcast.359, ...), custom_call_target="tpu_custom_call" | custom-call | flops 9126805504 | bytes 4194304 | tf_op jit(solution)/shard_map/column_stack/pallas_call | solution.py:160
  886.6 37.8 %all-gather.13.cloned.1.call-done = bf16[128,32,512]{2,1,0:T(8,128)(2,1)} async-done(((bf16[8,32,512]{2,1,0:T(8,128)(2,1)}), bf16[128,32,512]{2,1,0:T(8,128)(2,1)}) %all-gather.13.cloned.1.call-update) | async-done | bytes 4194320 | tf_op jit(solution)/shard_map/all_gather | solution.py:194
  924.4 7.4 convert_bitcast_fusion
  936.8 36.5 %all-gather.15.cloned.1.call-done = bf16[128,128,128]{2,1,0:T(8,128)(2,1)} async-done(((bf16[8,128,128]{2,1,0:T(8,128)(2,1)}), bf16[128,128,128]{2,1,0:T(8,128)(2,1)}) %all-gather.15.cloned.1.call-update) | async-done | bytes 4194320 | tf_op jit(solution)/shard_map/all_gather | solution.py:225
  973.3 6.7 copy.436
  980.0 4.5 fusion.224
  988.1 4.4 all-to-all-start.7
  993.3 12.8 %all-to-all-done.7 = bf16[8,128,128]{2,0,1:T(8,128)(2,1)S(1)} async-done(((bf16[8,128,128]{2,0,1:T(8,128)(2,1)}), bf16[8,128,128]{2,0,1:T(8,128)(2,1)S(1)}, u32[]{:S(2)}, u32[]{:S(2)}) %all-to-all-start.7) | async-done | bytes 262176 | tf_op jit(solution)/shard_map/all_to_all | solution.py:229
  1008.0 20.3 %all-gather.17.cloned.1.call-done = bf16[128,128,128]{2,1,0:T(8,128)(2,1)} async-done(((bf16[8,128,128]{2,1,0:T(8,128)(2,1)}), bf16[128,128,128]{2,1,0:T(8,128)(2,1)}) %all-gather.17.cloned.1.call-update) | async-done | bytes 4194320 | tf_op jit(solution)/shard_map/all_gather | solution.py:230
  1028.3 6.7 copy.444
  1035.0 3.4 fusion.226
  1039.9 16.6 %all_gather.50 = bf16[4,128,128]{2,0,1:T(4,128)(2,1)S(1)} all-gather(bf16[4,8,128]{2,0,1:T(4,128)(2,1)S(1)} %fusion.35), channel_id=1, replica_groups=mesh['req'=4,'dap'=16] {'dap'}, dimensions={1}, use_global_device_ids=true | all-gather | bytes 139264 | tf_op jit(solution)/shard_map/all_gather | solution.py:182
  1057.4 13.8 %row_attention.10 = bf16[8,128,128]{2,1,0:T(8,128)(2,1)} custom-call(bf16[8,128,128]{2,1,0:T(8,128)(2,1)} %copy-done.12, f32[8,128,128]{2,1,0:T(8,128)} %mul.309.mask_ref, f32[4,128,128]{2,1,0:T(8,128)} %multiply_bitcast_fusion.3.bias_ref, bf16[512,128]{1,0:T(8,128)(2,1)} %bitcast.354, bf16[128,128]{1,0:T(8,128)(2,1)} %get-tuple-element.36.wo_ref), custom_call_target="tpu_custom_call" | custom-call | flops 234881024 | bytes 524288 | tf_op jit(solution)/shard_map/row_attention/pallas_call | solution.py:104
  1072.3 15.3 %all_to_all.111 = bf16[8,128,128]{2,0,1:T(8,128)(2,1)S(1)} all-to-all(bf16[8,128,128]{2,0,1:T(8,128)(2,1)S(1)} %copy.451), channel_id=1, replica_groups=mesh['req'=4,'dap'=16] {'dap'}, dimensions={1} | all-to-all | bytes 524288 | tf_op jit(solution)/shard_map/all_to_all | solution.py:234
  1087.7 4.0 all-to-all-start.6
  1093.4 57.5 %all_gather.51 = bf16[4,128,128]{2,0,1:T(4,128)(2,1)S(1)} all-gather(bf16[4,8,128]{2,0,1:T(4,128)(2,1)S(1)} %fusion.36), channel_id=1, replica_groups=mesh['req'=4,'dap'=16] {'dap'}, dimensions={1}, use_global_device_ids=true | all-gather | bytes 139264 | tf_op jit(solution)/shard_map/all_gather | solution.py:182
  1152.6 13.8 %row_attention.11 = bf16[8,128,128]{2,1,0:T(8,128)(2,1)} custom-call(bf16[8,128,128]{2,1,0:T(8,128)(2,1)} %copy_bitcast_fusion.1.x_ref, f32[8,128,128]{2,1,0:T(8,128)} %broadcast_in_dim.11.mask_ref, f32[4,128,128]{2,1,0:T(8,128)} %multiply_bitcast_fusion.2.bias_ref, bf16[512,128]{1,0:T(8,128)(2,1)} %bitcast.356, bf16[128,128]{1,0:T(8,128)(2,1)} %get-tuple-element.34.wo_ref), custom_call_target="tpu_custom_call" | custom-call | flops 234881024 | bytes 524288 | tf_op jit(solution)/shard_map/row_attention/pallas_call | solution.py:104
  1168.2 6.0 all-to-all-start.9
  1174.3 2.5 copy.552
  1176.8 8.4 all-to-all-done.9
  (246 shorter events, 86.4 us)
Async XLA Ops:
  7.2 29.2 %copy-start.9 = (bf16[2,256,1024]{2,1,0:T(8,128)(2,1)S(1)}, bf16[2,256,1024]{2,1,0:T(8,128)(2,1)}, u32[]{:S(2)}) copy-start(bf16[2,256,1024]{2,1,0:T(8,128)(2,1)} %param.29) | copy-start | bytes 3145732
  10.4 27.8 %copy-start.20 = (bf16[2,256,256]{2,1,0:T(8,128)(2,1)S(1)}, bf16[2,256,256]{2,1,0:T(8,128)(2,1)}, u32[]{:S(2)}) copy-start(bf16[2,256,256]{2,1,0:T(8,128)(2,1)} %param.31) | copy-start | bytes 786436
  121.0 4.1 copy-start.26
  121.0 72.7 %all-to-all-start = ((bf16[16,8,32,256]{3,2,1,0:T(8,128)(2,1)}), bf16[16,8,32,256]{3,2,1,0:T(8,128)(2,1)S(1)}, u32[]{:S(2)}, u32[]{:S(2)}) async-start(bf16[16,8,32,256]{3,2,1,0:T(8,128)(2,1)} %bitcast.341), calls=%async_computation | async-start | bytes 4194304 | tf_op jit(solution)/shard_map/all_to_all | solution.py:249
  125.0 64.0 %copy-start.23 = (bf16[2,256,64]{1,2,0:T(8,128)(2,1)S(1)}, bf16[2,256,64]{1,2,0:T(8,128)(2,1)}, u32[]{:S(2)}) copy-start(bf16[2,256,64]{1,2,0:T(8,128)(2,1)} %param.36) | copy-start | bytes 196612
  125.1 64.6 %copy-start.21 = (bf16[2,256,256]{2,1,0:T(8,128)(2,1)S(1)}, bf16[2,256,256]{2,1,0:T(8,128)(2,1)}, u32[]{:S(2)}) copy-start(bf16[2,256,256]{2,1,0:T(8,128)(2,1)} %param.33) | copy-start | bytes 786436
  125.1 225.5 %all-gather.7.cloned.1.call-start = ((), (), s32[]{:S(2)}) async-start(), calls=%async_computation.10 | async-start | bytes 4456448 | tf_op jit(solution)/shard_map/all_gather | solution.py:194
  189.0 3.6 copy-start.10
  193.7 2.1 copy-start.4
  311.9 87.5 %all-gather.9.cloned.1.call-start = ((), (), s32[]{:S(2)}) async-start(), calls=%async_computation.11 | async-start | bytes 4456448 | tf_op jit(solution)/shard_map/all_gather | solution.py:225
  358.0 1.4 copy-start.11
  358.0 1.4 copy-start.28
  359.4 1.3 copy-start.15
  360.3 2.1 copy-start.2
  362.4 93.3 %all-gather.11.cloned.1.call-start = ((), (), s32[]{:S(2)}) async-start(), calls=%async_computation.12 | async-start | bytes 4456448 | tf_op jit(solution)/shard_map/all_gather | solution.py:230
  406.2 4.8 copy-start.3
  406.2 4.8 copy-start.32
  412.4 11.4 copy-start.24
  415.4 18.5 %all-to-all-start.2 = ((bf16[8,128,128]{2,0,1:T(8,128)(2,1)}), bf16[8,128,128]{2,0,1:T(8,128)(2,1)}, u32[]{:S(2)}, u32[]{:S(2)}) async-start(bf16[8,128,128]{2,0,1:T(8,128)(2,1)} %copy.404), calls=%async_computation.2 | async-start | bytes 524288 | tf_op jit(solution)/shard_map/all_to_all | solution.py:229
  462.5 3.7 copy-start.34
  465.9 1.4 copy-start.36
  466.6 39.3 %copy-start.22 = (bf16[2,128,512]{2,1,0:T(8,128)(2,1)S(1)}, bf16[2,128,512]{2,1,0:T(8,128)(2,1)}, u32[]{:S(2)}) copy-start(bf16[2,128,512]{2,1,0:T(8,128)(2,1)} %param.45) | copy-start | bytes 786436
  467.3 40.1 %copy-start.25 = (bf16[2,128,128]{2,1,0:T(8,128)(2,1)S(1)}, bf16[2,128,128]{2,1,0:T(8,128)(2,1)}, u32[]{:S(2)}) copy-start(bf16[2,128,128]{2,1,0:T(8,128)(2,1)} %param.47) | copy-start | bytes 196612
  484.3 33.3 %copy-start.37 = (bf16[2,128,4]{1,2,0:T(4,128)(2,1)S(1)}, bf16[2,128,4]{1,2,0:T(4,128)(2,1)}, u32[]{:S(2)}) copy-start(bf16[2,128,4]{1,2,0:T(4,128)(2,1)} %param.46) | copy-start | bytes 6148
  501.7 15.4 %all-to-all-start.3 = ((bf16[8,128,128]{2,0,1:T(8,128)(2,1)}), bf16[8,128,128]{2,0,1:T(8,128)(2,1)S(1)}, u32[]{:S(2)}, u32[]{:S(2)}) async-start(bf16[8,128,128]{2,0,1:T(8,128)(2,1)} %copy.414), calls=%async_computation.3 | async-start | bytes 524288 | tf_op jit(solution)/shard_map/all_to_all | solution.py:234
  549.4 21.5 %copy-start.8 = (bf16[1,256,1024]{2,1,0:T(8,128)(2,1)S(1)}, bf16[1,256,1024]{2,1,0:T(8,128)(2,1)}, u32[]{:S(2)}) copy-start(bf16[1,256,1024]{2,1,0:T(8,128)(2,1)} %get-tuple-element.24) | copy-start | bytes 1572868
  566.9 64.9 %all-to-all-start.1 = ((bf16[16,8,32,256]{3,2,1,0:T(8,128)(2,1)}), bf16[16,8,32,256]{3,2,1,0:T(8,128)(2,1)S(1)}, u32[]{:S(2)}, u32[]{:S(2)}) async-start(bf16[16,8,32,256]{3,2,1,0:T(8,128)(2,1)} %get-tuple-element.6), calls=%async_computation.1 | async-start | bytes 4194304 | tf_op jit(solution)/shard_map/all_to_all | solution.py:253
  572.1 3.4 copy-start.27
  631.8 1.4 copy-start.5
  714.6 5.6 copy-start.7
  714.6 54.3 %all-to-all-start.5 = ((bf16[16,8,32,256]{3,2,1,0:T(8,128)(2,1)}), bf16[16,8,32,256]{3,2,1,0:T(8,128)(2,1)S(1)}, u32[]{:S(2)}, u32[]{:S(2)}) async-start(bf16[16,8,32,256]{3,2,1,0:T(8,128)(2,1)} %bitcast.344), calls=%async_computation.5 | async-start | bytes 4194304 | tf_op jit(solution)/shard_map/all_to_all | solution.py:249
  720.1 204.3 %all-gather.13.cloned.1.call-start = ((), (), s32[]{:S(2)}) async-start(), calls=%async_computation.13 | async-start | bytes 4456448 | tf_op jit(solution)/shard_map/all_gather | solution.py:194
  886.3 87.0 %all-gather.15.cloned.1.call-start = ((), (), s32[]{:S(2)}) async-start(), calls=%async_computation.14 | async-start | bytes 4456448 | tf_op jit(solution)/shard_map/all_gather | solution.py:225
  931.8 1.4 copy-start.29
  933.2 1.4 copy-start.16
  934.2 2.0 copy-start
  936.3 92.0 %all-gather.17.cloned.1.call-start = ((), (), s32[]{:S(2)}) async-start(), calls=%async_computation.15 | async-start | bytes 4456448 | tf_op jit(solution)/shard_map/all_gather | solution.py:230
  980.0 4.8 copy-start.1
  980.0 4.8 copy-start.33
  988.1 17.9 %all-to-all-start.7 = ((bf16[8,128,128]{2,0,1:T(8,128)(2,1)}), bf16[8,128,128]{2,0,1:T(8,128)(2,1)S(1)}, u32[]{:S(2)}, u32[]{:S(2)}) async-start(bf16[8,128,128]{2,0,1:T(8,128)(2,1)} %copy.441), calls=%async_computation.7 | async-start | bytes 524288 | tf_op jit(solution)/shard_map/all_to_all | solution.py:229
  1035.0 3.7 copy-start.35
  1039.0 18.3 %copy-start.12 = (bf16[8,128,128]{2,1,0:T(8,128)(2,1)}, bf16[8,128,128]{2,1,0:T(8,128)(2,1)S(1)}, u32[]{:S(2)}) copy-start(bf16[8,128,128]{2,1,0:T(8,128)(2,1)S(1)} %get-tuple-element.65.x_ref) | copy-start | bytes 786436
  1071.2 20.5 %copy-start.14 = (bf16[1,128,512]{2,1,0:T(8,128)(2,1)S(1)}, bf16[1,128,512]{2,1,0:T(8,128)(2,1)}, u32[]{:S(2)}) copy-start(bf16[1,128,512]{2,1,0:T(8,128)(2,1)} %get-tuple-element.26) | copy-start | bytes 393220
  1087.7 5.3 copy-start.38
  1087.7 80.6 %all-to-all-start.6 = ((bf16[16,8,32,256]{3,2,1,0:T(8,128)(2,1)}), bf16[16,8,32,256]{3,2,1,0:T(8,128)(2,1)S(1)}, u32[]{:S(2)}, u32[]{:S(2)}) async-start(bf16[16,8,32,256]{3,2,1,0:T(8,128)(2,1)} %get-tuple-element.8), calls=%async_computation.6 | async-start | bytes 4194304 | tf_op jit(solution)/shard_map/all_to_all | solution.py:253
  1168.2 17.0 %all-to-all-start.9 = ((bf16[128,8,128]{2,1,0:T(8,128)(2,1)}), bf16[128,8,128]{2,1,0:T(8,128)(2,1)S(1)}, u32[]{:S(2)}, u32[]{:S(2)}) async-start(bf16[128,8,128]{2,1,0:T(8,128)(2,1)} %copy.455), calls=%async_computation.9 | async-start | bytes 524288 | tf_op jit(solution)/shard_map/all_to_all | solution.py:237
  1174.3 12.0 %copy-start.30 = (bf16[2,512,128]{2,1,0:T(8,128)(2,1)S(1)}, bf16[2,512,128]{2,1,0:T(8,128)(2,1)}, u32[]{:S(2)}) copy-start(bf16[2,512,128]{2,1,0:T(8,128)(2,1)} %param.49) | copy-start | bytes 786436
  1174.3 12.0 %copy-start.31 = (bf16[2,128,512]{2,1,0:T(8,128)(2,1)S(1)}, bf16[2,128,512]{2,1,0:T(8,128)(2,1)}, u32[]{:S(2)}) copy-start(bf16[2,128,512]{2,1,0:T(8,128)(2,1)} %param.48) | copy-start | bytes 786436
  (5 other events, 4.9 us)
Sparse Core Ops, SparseCore 0:
  312.0 38.4 all-gather.6
  362.5 36.8 all-gather.8
  413.7 41.9 all-gather.10
  886.5 37.9 all-gather.12
  936.4 36.8 all-gather.14
  987.4 40.8 all-gather.16

commit v2 on v1

v2 whole, which is shorter than its diff:
```python
import functools
import math

import jax
import jax.numpy as jnp
from jax import lax
from jax.experimental import pallas as pl
from jax.experimental.pallas import tpu as pltpu
from jax.sharding import PartitionSpec as P

GROUP_AXIS = 'dap'
PARTS_AXIS = 'req'
LOG2E = math.log2(math.e)
MASKED = -1e9 * LOG2E
LANES = 128
AHEAD = 4
F32 = jnp.float32
BF16 = jnp.bfloat16
NT = (((1,), (1,)), ((), ()))
TN = (((0,), (0,)), ((), ()))


def layer_norm_f32(values):
    centered = values - jnp.mean(values, axis=-1, keepdims=True)
    variance = jnp.mean(centered * centered, axis=-1, keepdims=True)
    return (centered * lax.rsqrt(variance + 1e-5)).astype(BF16)


def layer_norm(x):
    return layer_norm_f32(x.astype(F32))


def residual(x, update):
    return (x.astype(F32) + update).astype(BF16)


def dense(x, weight):
    return jnp.einsum('...c,cf->...f', x, weight, preferred_element_type=F32)


def softmax_keys_first(logits):
    top = jnp.max(logits, axis=0, keepdims=True)
    raised = jnp.exp2(logits - top)
    total = jnp.sum(raised, axis=0, keepdims=True)
    return (raised * (1.0 / total)).astype(BF16)


def pipelined_units(units, ahead, first_stage, second_stage):
    ready = {}
    for idx in range(min(ahead, len(units))):
        ready[idx] = first_stage(*units[idx])
    for idx in range(len(units)):
        if idx + ahead < len(units):
            ready[idx + ahead] = first_stage(*units[idx + ahead])
        second_stage(ready.pop(idx), *units[idx])


def row_attention_kernel(heads, group, x_ref, mask_ref, bias_ref, w_ref, wo_ref, o_ref, proj, gated, *stage, swap_in, swap_out):
    width = wo_ref.shape[0]
    head_dim = width // heads
    scale = head_dim ** -0.5 * LOG2E
    n_seq = mask_ref.shape[0]
    length = mask_ref.shape[1]
    stage = list(stage)
    if swap_in:
        stage_in = stage.pop(0)
        for part in range(stage_in.shape[0]):
            stage_in[part] = x_ref[:, :, part * LANES:(part + 1) * LANES].astype(F32).reshape(stage_in.shape[1:])
    if swap_out:
        stage_out = stage.pop(0)

    def load_row(s):
        if swap_in:
            return jnp.concatenate([stage_in[part, pl.ds(s, length, stride=n_seq), :] for part in range(stage_in.shape[0])], -1)
        return x_ref[s].astype(F32)

    def head_rows(j, part, h):
        lo = part * width + h * head_dim
        return proj[j, lo:lo + head_dim, :]

    def some_rows(t, carry):
        base = t * group
        normed = [layer_norm_f32(load_row(base + j)) for j in range(group)]
        for j in range(group):
            proj[j] = lax.dot_general(w_ref[...], normed[j], NT, preferred_element_type=F32).astype(BF16)

        def logits_of(j, h):
            return lax.dot_general(head_rows(j, 1, h), head_rows(j, 0, h), TN, preferred_element_type=F32)

        def finish(raw, j, h):
            logits = jnp.where(mask_ref[base + j] > 0.0, raw * scale + bias_ref[h], MASKED)
            out_t = jnp.dot(head_rows(j, 2, h), softmax_keys_first(logits), preferred_element_type=F32)
            gate = jax.nn.sigmoid(head_rows(j, 3, h).astype(F32))
            gated[j, h * head_dim:(h + 1) * head_dim, :] = (out_t * gate).astype(BF16)

        pipelined_units([(j, h) for j in range(group) for h in range(heads)], AHEAD, logits_of, finish)
        for j in range(group):
            s = base + j
            result = load_row(s) + lax.dot_general(gated[j], wo_ref[...], TN, preferred_element_type=F32)
            if swap_out:
                for part in range(stage_out.shape[0]):
                    stage_out[part, pl.ds(s, length, stride=n_seq), :] = result[:, part * LANES:(part + 1) * LANES]
            else:
                o_ref[s] = result.astype(BF16)
        return carry

    lax.fori_loop(0, n_seq // group, some_rows, 0)
    if swap_out:
        for part in range(stage_out.shape[0]):
            o_ref[:, :, part * LANES:(part + 1) * LANES] = stage_out[part].reshape(length, n_seq, LANES).astype(BF16)


def row_attention(x, mask_lanes, bias_t, w_qkvg_t, w_out, heads, block, group, swap_in=False, swap_out=False):
    n_rows, length = mask_lanes.shape[:2]
    dim = x.shape[-1]
    width = w_out.shape[0]
    natural = pl.BlockSpec((block, length, dim), lambda i: (i, 0, 0))
    swapped = pl.BlockSpec((length, block, dim), lambda i: (0, i, 0))
    whole2 = lambda shape: pl.BlockSpec(shape, lambda i: (0,) * len(shape))
    scratch = [pltpu.VMEM((group, 4 * width, length), BF16), pltpu.VMEM((group, width, length), BF16)]
    scratch += [pltpu.VMEM((dim // LANES, length * block, LANES), F32)] * (int(swap_in) + int(swap_out))
    out_shape = (length, n_rows, dim) if swap_out else (n_rows, length, dim)
    return pl.pallas_call(
        functools.partial(row_attention_kernel, heads, group, swap_in=swap_in, swap_out=swap_out),
        grid=(n_rows // block,),
        in_specs=[
            swapped if swap_in else natural,
            pl.BlockSpec((block, length, length), lambda i: (i, 0, 0)),
            whole2(bias_t.shape), whole2(w_qkvg_t.shape), whole2(w_out.shape),
        ],
        out_specs=swapped if swap_out else natural,
        out_shape=jax.ShapeDtypeStruct(out_shape, BF16),
        scratch_shapes=scratch,
        cost_estimate=pl.CostEstimate(flops=n_rows * length * (dim * width * 10 + 4 * length * width), bytes_accessed=4 * x.size, transcendentals=n_rows * heads * length * length),
        name='row_attention',
    )(x, mask_lanes, bias_t, w_qkvg_t, w_out)


def column_kernel(heads, x_ref, mask_ref, mrow_ref, w_ref, wo_ref, win_ref, wtr_ref, wopm_ref, o_ref, ab_ref, proj, gated):
    width = wo_ref.shape[0]
    head_dim = width // heads
    scale = head_dim ** -0.5 * LOG2E
    length = mask_ref.shape[1]
    lanes = mask_ref.shape[2]
    x = x_ref[...].reshape(length, x_ref.shape[-1]).astype(F32)
    proj[...] = lax.dot_general(w_ref[...], layer_norm_f32(x), NT, preferred_element_type=F32).astype(BF16)

    def head_rows(part, h, cols=slice(None)):
        lo = part * width + h * head_dim
        return proj[lo:lo + head_dim, cols]

    def columns(c):
        return slice(c * lanes, (c + 1) * lanes)

    def logits_of(h, c):
        return lax.dot_general(head_rows(1, h), head_rows(0, h, columns(c)), TN, preferred_element_type=F32)

    def finish(raw, h, c):
        logits = jnp.where(mask_ref[0] > 0.0, raw * scale, MASKED)
        out_t = jnp.dot(head_rows(2, h), softmax_keys_first(logits), preferred_element_type=F32)
        gate = jax.nn.sigmoid(head_rows(3, h, columns(c)).astype(F32))
        gated[h * head_dim:(h + 1) * head_dim, columns(c)] = (out_t * gate).astype(BF16)

    pipelined_units([(h, c) for h in range(heads) for c in range(length // lanes)], AHEAD, logits_of, finish)
    update = lax.dot_general(gated[...], wo_ref[...], TN, preferred_element_type=F32)
    x = (x + update).astype(BF16).astype(F32)
    hidden = jnp.maximum(jnp.dot(layer_norm_f32(x), win_ref[...], preferred_element_type=F32), 0.0).astype(BF16)
    x = (x + jnp.dot(hidden, wtr_ref[...], preferred_element_type=F32)).astype(BF16)
    o_ref[...] = x.reshape(o_ref.shape)
    ab_t = lax.dot_general(wopm_ref[...], layer_norm_f32(x.astype(F32)), NT, preferred_element_type=F32).astype(BF16)
    ab_ref[0] = (ab_t.astype(F32) * mrow_ref[0]).astype(BF16)


def column_stack(x, mask_lanes, mask_row, w_qkvg_t, w_out, w_in, w_tr, w_opm_t, heads):
    n_dev, n_res, n_seq, dim = x.shape
    length = n_dev * n_seq
    width = w_out.shape[0]
    block = pl.BlockSpec((n_dev, 1, n_seq, dim), lambda r: (0, r, 0, 0))
    whole2 = lambda shape: pl.BlockSpec(shape, lambda i: (0,) * len(shape))
    n_opm = w_opm_t.shape[0]
    return pl.pallas_call(
        functools.partial(column_kernel, heads),
        grid=(n_res,),
        in_specs=[
            block,
            pl.BlockSpec((1, length, mask_lanes.shape[2]), lambda r: (r, 0, 0)),
            pl.BlockSpec((1, 1, length), lambda r: (r, 0, 0)),
            whole2(w_qkvg_t.shape), whole2(w_out.shape), whole2(w_in.shape), whole2(w_tr.shape), whole2(w_opm_t.shape),
        ],
        out_specs=[block, pl.BlockSpec((1, n_opm, length), lambda r: (r, 0, 0))],
        out_shape=[jax.ShapeDtypeStruct(x.shape, BF16), jax.ShapeDtypeStruct((n_res, n_opm, length), BF16)],
        scratch_shapes=[pltpu.VMEM((4 * width, length), BF16), pltpu.VMEM((width, length), BF16)],
        cost_estimate=pl.CostEstimate(flops=n_res * length * (dim * width * 26 + 4 * length * width), bytes_accessed=4 * x.size, transcendentals=n_res * heads * length * length),
        name='column_stack',
    )(x, mask_lanes, mask_row, w_qkvg_t, w_out, w_in, w_tr, w_opm_t)


class Exchange:
    def __init__(self, n_dev, me, sends, recvs):
        self.n_dev, self.me, self.sends, self.recvs, self.used = n_dev, me, sends, recvs, 0

    def start(self, source, target, broadcast=False):
        phase = self.used
        self.used += 1
        pick = (lambda d: source) if broadcast else (lambda d: source.at[d])

        def copy(dst_dev, slot):
            return pltpu.make_async_remote_copy(
                src_ref=pick(dst_dev), dst_ref=target.at[slot], send_sem=self.sends.at[phase, dst_dev], recv_sem=self.recvs.at[phase, slot],
                device_id={GROUP_AXIS: dst_dev}, device_id_type=pl.DeviceIdType.MESH)

        def send(step, carry):
            copy(lax.rem(self.me + step, self.n_dev), self.me).start()
            return carry

        lax.fori_loop(1, self.n_dev, send, 0)
        target[self.me] = source[...] if broadcast else source[self.me]

        def finish():
            def wait(step, carry):
                other = lax.rem(self.me + step, self.n_dev)
                copy(other, other).wait_recv()
                copy(other, self.me).wait_send()
                return carry

            lax.fori_loop(1, self.n_dev, wait, 0)

        return finish


def entry_barrier(n_dev, me):
    barrier = pltpu.get_barrier_semaphore()

    def signal(step, carry):
        pl.semaphore_signal(barrier, inc=1, device_id={GROUP_AXIS: lax.rem(me + step, n_dev)}, device_id_type=pl.DeviceIdType.MESH)
        return carry

    lax.fori_loop(1, n_dev, signal, 0)
    pl.semaphore_wait(barrier, n_dev - 1)


def pair_kernel(n_dev, with_bias, *refs):
    (z_ref, mrow_ref, start_ref, end_ref, m_ref,
     tmo_w, tmo_g, tmo_out, tmi_w, tmi_g, tmi_out, tas_w, tas_b, tas_out, tae_w, tae_b, tae_out, ptr_in, ptr_out, next_b,
     o_ref, mback_ref, bias_ref,
     zbuf, tbuf, stage, ab_send, ab_recv, x_send, x_recv, ln_stage, gate, proj, gated, bias_t, bias_send, bias_recv, z_send, z_recv, zb_recv, nb_send, nb_recv,
     sends, recvs, m_sends, m_recvs, m_own) = refs
    n_res, length, dim = z_ref.shape
    tri = tmo_out.shape[0]
    n_chan = tri // n_dev
    tokens = n_res * length
    me = lax.axis_index(GROUP_AXIS)
    entry_barrier(n_dev, me)
    exchange = Exchange(n_dev, me, sends, recvs)

    def m_copy(dst_dev, slot):
        return pltpu.make_async_remote_copy(
            src_ref=m_ref.at[dst_dev], dst_ref=mback_ref.at[slot], send_sem=m_sends.at[dst_dev], recv_sem=m_recvs.at[slot],
            device_id={GROUP_AXIS: dst_dev}, device_id_type=pl.DeviceIdType.MESH)

    own = pltpu.make_async_copy(m_ref.at[me], mback_ref.at[me], m_own)
    own.start()

    def m_steps(lo, hi):
        def send(step, carry):
            m_copy(lax.rem(me + step, n_dev), me).start()
            return carry
        lax.fori_loop(lo, hi, send, 0)

    def normed_tokens():
        return layer_norm_f32(zbuf[...].astype(F32).reshape(tokens, dim))

    def tri_mul(turn, w_ref, g_ref, out_ref, contract):
        x_norm = normed_tokens()
        for part in range(2):
            value = lax.dot_general(w_ref[part * tri:(part + 1) * tri, :], x_norm, NT, preferred_element_type=F32)
            opened = lax.dot_general(w_ref[(2 + part) * tri:(3 + part) * tri, :], x_norm, NT, preferred_element_type=F32)
            gated_t = mrow_ref[...] * jax.nn.sigmoid(opened) * value
            for d in range(n_dev):
                for i in range(n_res):
                    tile = gated_t[d * n_chan:(d + 1) * n_chan, i * length:(i + 1) * length]
                    stage[pl.ds(d * n_chan * n_res + i, n_chan, stride=n_res), :] = tile
            ab_send[turn, :, part] = stage[...].reshape(n_dev, n_chan, n_res, length).astype(BF16)
        arrived = exchange.start(ab_send.at[turn], ab_recv.at[turn])
        m_steps(1 + 4 * turn, 3 + 4 * turn)
        gate[...] = jax.nn.sigmoid(jnp.dot(x_norm, g_ref[...], preferred_element_type=F32))
        arrived()
        for c in range(n_chan):
            left = ab_recv[turn, :, 0, c].astype(F32).reshape(length, length).astype(BF16)
            right = ab_recv[turn, :, 1, c].astype(F32).reshape(length, length).astype(BF16)
            product = lax.dot_general(left, right, contract, preferred_element_type=F32)
            x_send[turn, :, c] = product.reshape(n_dev, n_res, length)
        arrived = exchange.start(x_send.at[turn], x_recv.at[turn])
        m_steps(3 + 4 * turn, 5 + 4 * turn)
        arrived()
        values = x_recv[turn].reshape(tri, n_res, length)
        centered = values - jnp.mean(values, axis=0, keepdims=True)
        inverse = lax.rsqrt(jnp.mean(centered * centered, axis=0, keepdims=True) + 1e-5)
        pitch = tri + 8
        for c in range(tri):
            ln_stage[pl.ds(c, n_res, stride=pitch), :] = centered[c] * inverse[0]
        for i in range(n_res):
            columns = ln_stage[i * pitch:i * pitch + tri, :].astype(BF16)
            update = gate[i * length:(i + 1) * length, :] * lax.dot_general(columns, out_ref[...], TN, preferred_element_type=F32)
            zbuf[i] = (zbuf[i].astype(F32) + update).astype(BF16)

    def local_bias(x_norm, b_ref, send_ref):
        heads_pad = b_ref.shape[0]
        rows = lax.dot_general(b_ref[...], x_norm, NT, preferred_element_type=F32)
        for i in range(n_res):
            stage[pl.ds(i, heads_pad, stride=n_res), :] = rows[:, i * length:(i + 1) * length]
        heads = send_ref.shape[0]
        send_ref[...] = stage[0:heads * n_res, :].reshape(heads, n_res, length).astype(BF16)

    def attention(source, w_ref, out_ref, mask_ref, heads):
        width = out_ref.shape[0]
        head_dim = width // heads
        scale = head_dim ** -0.5 * LOG2E
        half = proj.shape[0]
        head_rows = lambda j, part, h: proj[j, part * width + h * head_dim:part * width + (h + 1) * head_dim, :]

        def some(t, carry):
            base = t * half
            normed = [layer_norm_f32(source[base + j].astype(F32)) for j in range(half)]
            for j in range(half):
                proj[j] = lax.dot_general(w_ref[...], normed[j], NT, preferred_element_type=F32).astype(BF16)

            def logits_of(j, h):
                return lax.dot_general(head_rows(j, 1, h), head_rows(j, 0, h), TN, preferred_element_type=F32)

            def finish(raw, j, h):
                logits = jnp.where(mask_ref[base + j] > 0.0, raw * scale + bias_t[h], MASKED)
                out_t = jnp.dot(head_rows(j, 2, h), softmax_keys_first(logits), preferred_element_type=F32)
                opened = jax.nn.sigmoid(head_rows(j, 3, h).astype(F32))
                gated[j, h * head_dim:(h + 1) * head_dim, :] = (out_t * opened).astype(BF16)

            pipelined_units([(j, h) for j in range(half) for h in range(heads)], AHEAD, logits_of, finish)
            for j in range(half):
                update = lax.dot_general(gated[j], out_ref[...], TN, preferred_element_type=F32)
                source[base + j] = (source[base + j].astype(F32) + update).astype(BF16)
            return carry

        lax.fori_loop(0, n_res // half, some, 0)

    def swap_blocks(source):
        for i in range(n_res):
            row = source[i].astype(F32)
            for d in range(n_dev):
                stage[pl.ds(d * n_res * n_res + i, n_res, stride=n_res), :] = row[d * n_res:(d + 1) * n_res, :]
        return stage[...].reshape(n_dev, n_res, n_res, dim).astype(BF16)

    def rows_of(received, i):
        return received[:, i].astype(F32).reshape(length, dim).astype(BF16)

    heads = bias_send.shape[1]
    zbuf[...] = z_ref[...]
    tri_mul(0, tmo_w, tmo_g, tmo_out, NT)
    tri_mul(1, tmi_w, tmi_g, tmi_out, TN)
    local_bias(normed_tokens(), tas_b, bias_send.at[0])
    arrived = exchange.start(bias_send.at[0], bias_recv.at[0], broadcast=True)
    m_steps(9, 11)
    arrived()
    for h in range(heads):
        bias_t[h] = rows_of(bias_recv.at[0], h).astype(F32).T * LOG2E
    attention(zbuf, tas_w, tas_out, start_ref, heads)
    local_bias(normed_tokens(), tae_b, bias_send.at[1])
    bias_arrived = exchange.start(bias_send.at[1], bias_recv.at[1], broadcast=True)
    z_send[0] = swap_blocks(zbuf)
    arrived = exchange.start(z_send.at[0], z_recv)
    m_steps(11, 13)
    bias_arrived()
    for h in range(heads):
        bias_t[h] = rows_of(bias_recv.at[1], h).astype(F32) * LOG2E
    arrived()
    for j in range(n_res):
        tbuf[j] = rows_of(z_recv, j)
    attention(tbuf, tae_w, tae_out, end_ref, heads)
    z_send[1] = swap_blocks(tbuf)
    arrived = exchange.start(z_send.at[1], zb_recv)
    m_steps(13, n_dev)
    arrived()
    for i in range(n_res):
        zbuf[i] = rows_of(zb_recv, i)
    x_norm = normed_tokens()
    hidden = jnp.maximum(jnp.dot(x_norm, ptr_in[...], preferred_element_type=F32), 0.0).astype(BF16)
    update = jnp.dot(hidden, ptr_out[...], preferred_element_type=F32)
    result = (zbuf[...].astype(F32) + update.reshape(n_res, length, dim)).astype(BF16)
    o_ref[...] = result
    if with_bias:
        zbuf[...] = result
        local_bias(normed_tokens(), next_b, nb_send)
        arrived = exchange.start(nb_send, nb_recv, broadcast=True)
        arrived()
        for h in range(bias_ref.shape[0]):
            bias_ref[h] = rows_of(nb_recv, h).astype(F32).T * LOG2E
    else:
        bias_ref[...] = jnp.zeros_like(bias_ref)
    own.wait()

    def m_wait(step, carry):
        other = lax.rem(me + step, n_dev)
        m_copy(other, other).wait_recv()
        m_copy(other, me).wait_send()
        return carry

    lax.fori_loop(1, n_dev, m_wait, 0)


def pair_stack(pair_loc, by_res, masks, pair_w, next_bias, collective_id):
    (tmo_proj, tmo_out, tmi_proj, tmi_out, tas_qkvg, tas_bias, tas_out,
     tae_qkvg, tae_bias, tae_out, ptr_in, ptr_out) = pair_w
    n_res, length, dim = pair_loc.shape
    n_dev = masks['n_dev']
    tri = tmo_out.shape[0]
    heads = tas_bias.shape[1]
    n_chan = tri // n_dev
    row_heads = (next_bias if next_bias is not None else masks['row_bias']).shape[1]
    padded = lambda w: jnp.pad(w.T, ((0, -w.shape[1] % 8), (0, 0)))
    weights = (tmo_proj[:, :4 * tri].T, tmo_proj[:, 4 * tri:], tmo_out, tmi_proj[:, :4 * tri].T, tmi_proj[:, 4 * tri:], tmi_out,
               tas_qkvg.T, padded(tas_bias), tas_out, tae_qkvg.T, padded(tae_bias), tae_out, ptr_in, ptr_out,
               padded(next_bias if next_bias is not None else masks['row_bias']))
    vmem = pl.BlockSpec(memory_space=pltpu.VMEM)
    any_space = pl.BlockSpec(memory_space=pl.ANY)
    n_phases = 9
    width = tas_out.shape[0]
    scratch = [
        pltpu.VMEM((n_res, length, dim), BF16), pltpu.VMEM((n_res, length, dim), BF16),
        pltpu.VMEM((n_dev * n_res * n_res, LANES), F32),
        pltpu.VMEM((2, n_dev, 2, n_chan, n_res, length), BF16), pltpu.VMEM((2, n_dev, 2, n_chan, n_res, length), BF16),
        pltpu.VMEM((2, n_dev, n_chan, n_res, length), F32), pltpu.VMEM((2, n_dev, n_chan, n_res, length), F32),
        pltpu.VMEM((n_res * (tri + 8), length), F32), pltpu.VMEM((n_res * length, dim), F32),
        pltpu.VMEM((n_res, 4 * width, length), BF16), pltpu.VMEM((n_res, width, length), BF16),
        pltpu.VMEM((heads, length, length), F32),
        pltpu.VMEM((2, heads, n_res, length), BF16), pltpu.VMEM((2, n_dev, heads, n_res, length), BF16),
        pltpu.VMEM((2, n_dev, n_res, n_res, dim), BF16), pltpu.VMEM((n_dev, n_res, n_res, dim), BF16), pltpu.VMEM((n_dev, n_res, n_res, dim), BF16),
        pltpu.VMEM((row_heads, n_res, length), BF16), pltpu.VMEM((n_dev, row_heads, n_res, length), BF16),
        pltpu.SemaphoreType.DMA((n_phases, n_dev)), pltpu.SemaphoreType.DMA((n_phases, n_dev)),
        pltpu.SemaphoreType.DMA((n_dev,)), pltpu.SemaphoreType.DMA((n_dev,)), pltpu.SemaphoreType.DMA,
    ]
    return pl.pallas_call(
        functools.partial(pair_kernel, n_dev, next_bias is not None),
        in_specs=[vmem] * 4 + [any_space] + [vmem] * len(weights),
        out_specs=[vmem, any_space, vmem],
        out_shape=[jax.ShapeDtypeStruct(pair_loc.shape, BF16), jax.ShapeDtypeStruct(by_res.shape, BF16), jax.ShapeDtypeStruct((row_heads, length, length), F32)],
        scratch_shapes=scratch,
        compiler_params=pltpu.CompilerParams(collective_id=collective_id, has_side_effects=True),
        cost_estimate=pl.CostEstimate(flops=4_000_000_000, bytes_accessed=16_000_000, transcendentals=4_000_000),
        name='pair_stack',
    )(pair_loc, masks['pair_rows'].reshape(1, n_res * length), masks['start'], masks['end'], by_res, *weights)


def head_bias(pair_norm, w_bias):
    return jnp.einsum('ijc,ch->hij', pair_norm, w_bias, preferred_element_type=F32).astype(BF16)


def gather_bias(pair_rows, w_bias):
    full = lax.all_gather(head_bias(layer_norm(pair_rows), w_bias), GROUP_AXIS, axis=1, tiled=True)
    return jnp.swapaxes(full, 1, 2).astype(F32) * LOG2E


def outer_update(ab, overlap, w_out):
    opm_dim = ab.shape[1] // 2
    left_act = ab[:, :opm_dim]
    right_full = lax.all_gather(ab[:, opm_dim:], GROUP_AXIS, axis=0, tiled=True)
    outer_prod = jnp.einsum('ics,jes->ijce', left_act, right_full, preferred_element_type=F32).astype(BF16)
    n_rows, n_cols = outer_prod.shape[:2]
    update = dense(outer_prod.reshape(n_rows, n_cols, opm_dim * opm_dim), w_out)
    return update / (1e-3 + overlap)[:, :, None]


def evoformer_block(value_a7, pair_loc, bias_t, masks, layer_w, next_bias, layer_idx):
    (row_qkvg, row_bias, row_out, col_qkvg, col_out, mtr_in, mtr_out, opm_proj, opm_out) = layer_w[:9]
    heads = row_bias.shape[1]
    n_dev = masks['n_dev']
    value_a7 = row_attention(value_a7, masks['seq'], bias_t, row_qkvg.T, row_out, heads, 16, 4, swap_in=layer_idx > 0, swap_out=True)
    length, n_seq, dim = value_a7.shape
    by_dev = value_a7.reshape(n_dev, length // n_dev, n_seq, dim)
    by_res = lax.all_to_all(by_dev, GROUP_AXIS, 0, 0, tiled=True)
    by_res, ab = column_stack(by_res, masks['res'], masks['res_row'], col_qkvg.T, col_out, mtr_in, mtr_out, opm_proj.T, heads)
    pair_loc = residual(pair_loc, outer_update(ab, masks['overlap'], opm_out))
    pair_loc, value_a7, bias_t = pair_stack(pair_loc, by_res, masks, layer_w[9:], next_bias, layer_idx)
    return value_a7.reshape(length, n_seq, dim), pair_loc, bias_t


def make_masks(msa_mask, pair_mask, n_dev):
    shard_idx = lax.axis_index(GROUP_AXIS)
    n_seq, length = msa_mask.shape
    n_res = pair_mask.shape[0]
    packed = jnp.concatenate([msa_mask, pair_mask], 0).astype(BF16)
    full = lax.all_gather(packed, GROUP_AXIS, axis=0, tiled=True).reshape(n_dev, n_seq + n_res, length).astype(F32)
    full_msa = full[:, :n_seq].reshape(n_dev * n_seq, length)
    full_pair = full[:, n_seq:].reshape(n_dev * n_res, length)
    res_mask = lax.dynamic_slice_in_dim(full_msa, shard_idx * n_res, n_res, 1).T
    end_mask = lax.dynamic_slice_in_dim(full_pair, shard_idx * n_res, n_res, 1).T
    lanes = lambda mask: jnp.broadcast_to(mask.astype(F32)[:, :, None], mask.shape + (length,))
    return {
        'n_dev': n_dev,
        'seq': lanes(msa_mask),
        'res': lanes(res_mask),
        'res_row': res_mask[:, None, :],
        'pair_rows': pair_mask.astype(F32),
        'start': lanes(pair_mask),
        'end': lanes(end_mask),
        'overlap': jnp.dot(res_mask, full_msa, precision=lax.Precision.DEFAULT, preferred_element_type=F32),
    }


def solution(mesh):
    row_spec = P((PARTS_AXIS, GROUP_AXIS))
    n_dev = mesh.shape[GROUP_AXIS]

    def local_body(value_a7, pair_loc, msa_mask, pair_mask, *weights):
        masks = make_masks(msa_mask, pair_mask, n_dev)
        masks['row_bias'] = weights[1][0]
        bias_t = gather_bias(pair_loc, weights[1][0])
        n_layers = weights[0].shape[0]
        for layer_idx in range(n_layers):
            layer_w = tuple(weight[layer_idx] for weight in weights)
            next_bias = weights[1][layer_idx + 1] if layer_idx + 1 < n_layers else None
            value_a7, pair_loc, bias_t = evoformer_block(value_a7, pair_loc, bias_t, masks, layer_w, next_bias, layer_idx)
        return jnp.swapaxes(value_a7, 0, 1), pair_loc

    def run_blocks(*arrays):
        n_weights = len(arrays) - 4
        return jax.shard_map(local_body, mesh=mesh, in_specs=(row_spec,) * 4 + (P(),) * n_weights, out_specs=(row_spec, row_spec), check_vma=False)(*arrays)

    return run_blocks
```

time: 1200 us -> 757 us (0.63)
  blocking collectives: 275 us -> 83.2 us
  waiting for transfers between devices: 274 us -> 108 us
  local copies, waits for them, and re-layouts: 84.2 us -> 47.7 us
  starting transfers between devices: 38 us -> 10.5 us
  matrix products: 43.9 us -> 19.4 us
  Pallas kernels: 445 us -> 460 us
  other arithmetic: 18.7 us -> 4.14 us
    all_gather x6 -> x1, blocking collectives: 184 us -> 23.4 us  [gather_bias(): lax.all_gather(head_bias(layer_norm(pair_rows), w_bias), GROUP_AXIS, axis...]
    pallas_call x6 -> x4, Pallas kernels: 217 us -> 361 us  [the longest x2 306 us: pair_stack(): pl.pallas_call(functools.partial(pair_kernel, n_dev, next_bias is not Non...]
    pallas_call x2, Pallas kernels: 229 us -> 100 us  [column_stack(): pl.pallas_call(functools.partial(column_kernel, heads), grid=(n_res,), in...]
    all_gather x4 -> x0, waiting for transfers between devices: 111 us -> none  [pair_stack(): right_full = lax.all_gather(right_act, GROUP_AXIS, axis=0, tiled=True)]
    all_to_all x6 -> x0, waiting for transfers between devices: 38.9 us -> none  [the longest x2 21.4 us: pair_stack(): left_cols = lax.all_to_all(left_act, GROUP_AXIS, 1, 0, tiled=True)]
    all_to_all x2 -> x0, blocking collectives: 31.6 us -> none  [the longest x1 16.3 us: pair_stack(): lax.all_to_all(jnp.swapaxes(pair_t, 0, 1), GROUP_AXIS, 0, 1, tiled=True)]
    all_to_all x6 -> x0, starting transfers between devices: 27 us -> none  [the longest x2 8.74 us: pair_stack(): left_cols = lax.all_to_all(left_act, GROUP_AXIS, 1, 0, tiled=True)]
    all_gather x4 -> x0, local copies, waits for them, and re-layouts: 26.8 us -> none  [pair_stack(): right_full = lax.all_gather(right_act, GROUP_AXIS, axis=0, tiled=True)]
  transfers between devices with their start and end apart: 14 -> 4, of which waited for: 11 -> 3; matrix products, arithmetic and copies ran while one was open for 3% -> 4% of each run, Pallas kernels for 1% -> 0%
where the time goes in v2:
time: 757 us; the launch traced here: 748 us
  Pallas kernels  460 us (61%)
  waiting for transfers between devices  108 us (14%)
  blocking collectives  83.2 us (11%)
  local copies, waits for them, and re-layouts  47.7 us (6%)
  matrix products  19.4 us (3%)
  between operations  14.9 us (2%)
  starting transfers between devices  10.5 us (1%)
    pallas_call x2, Pallas kernels, pair_stack(): pl.pallas_call(functools.partial(pair_kernel, n_dev, next_bias is not Non...  306 us
    pallas_call x2, Pallas kernels, column_stack(): pl.pallas_call(functools.partial(column_kernel, heads), grid=(n_res,), in...  100 us
    all_gather x2, waiting for transfers between devices, outer_update(): right_full = lax.all_gather(ab[:, opm_dim:], GROUP_AXIS, axis=0, tiled=True)  60.1 us
    all_gather x1, blocking collectives, make_masks(): lax.all_gather(packed, GROUP_AXIS, axis=0, tiled=True)  59.9 us
    pallas_call x2, Pallas kernels, row_attention(): pl.pallas_call(functools.partial(row_attention_kernel, heads, group, swap...  54.3 us
    all_to_all x2, waiting for transfers between devices, evoformer_block(): by_res = lax.all_to_all(by_dev, GROUP_AXIS, 0, 0, tiled=True)  47.7 us
    all_gather x1, blocking collectives, gather_bias(): lax.all_gather(head_bias(layer_norm(pair_rows), w_bias), GROUP_AXIS, axis...  23.4 us
  transfers between devices with their start and end apart: 4, of which 3 were waited for; matrix products, arithmetic and copies ran while one was open for 4% of the time, Pallas kernels for 0%

profile of v2, /device:TPU:21, one launch (start us, length us, event | category | flops | bytes accessed | tf_op | source)
XLA Modules:
  0.0 748.2 jit_solution(15972032587734730120)
XLA Ops:
  7.2 0.8 fusion.36
  8.0 1.1 convert_reduce_fusion
  9.1 1.3 fusion.15
  10.5 1.4 fusion.12
  11.9 23.4 %all_gather.12 = bf16[8,128,128]{2,0,1:T(8,128)(2,1)S(1)} all-gather(bf16[8,8,128]{2,0,1:T(8,128)(2,1)S(1)} %fusion.12), channel_id=1, replica_groups=mesh['req'=4,'dap'=16] {'dap'}, dimensions={1}, use_global_device_ids=true | all-gather | bytes 278528 | tf_op jit(solution)/shard_map/all_gather | solution.py:457
  35.5 0.9 multiply_bitcast_fusion.bias_ref
  36.4 1.0 copy.96
  38.2 1.9 broadcast_in_dim.10.mask_ref
  40.1 26.3 %row_attention.2 = bf16[128,32,256]{2,1,0:T(8,128)(2,1)} custom-call(bf16[32,128,256]{2,1,0:T(8,128)(2,1)} %x_ref.1, f32[32,128,128]{2,1,0:T(8,128)} %broadcast_in_dim.10.mask_ref, f32[8,128,128]{2,1,0:T(8,128)} %multiply_bitcast_fusion.bias_ref, bf16[1024,256]{1,0:T(8,128)(2,1)} %bitcast.173, bf16[256,256]{1,0:T(8,128)(2,1)} %get-tuple-element.43.wo_ref), custom_call_target="tpu_custom_call" | custom-call | flops 3221225472 | bytes 4194304 | tf_op jit(solution)/shard_map/row_attention/pallas_call | solution.py:123
  66.4 4.0 all-to-all-start
  70.6 59.9 %all_gather.13 = bf16[640,128]{1,0:T(8,128)(2,1)S(1)} all-gather(bf16[40,128]{1,0:T(8,128)(2,1)S(1)} %pad_maximum_fusion), channel_id=1, replica_groups=mesh['req'=4,'dap'=16] {'dap'}, dimensions={0}, use_global_device_ids=true | all-gather | bytes 174080 | tf_op jit(solution)/shard_map/all_gather | solution.py:490
  131.3 2.1 fusion.32
  133.4 2.1 copy.98
  136.1 1.7 slice_bitcast_fusion.14
  137.8 2.2 slice_bitcast_fusion
  140.0 1.1 slice_bitcast_fusion.1
  141.1 2.0 broadcast_in_dim.11.mask_ref
  143.1 50.0 %column_stack.2 = (bf16[16,8,32,256]{3,2,1,0:T(8,128)(2,1)}, bf16[8,64,512]{2,1,0:T(8,128)(2,1)}) custom-call(bf16[16,8,32,256]{3,2,1,0:T(8,128)(2,1)} %copy-done, f32[8,512,128]{2,1,0:T(8,128)} %broadcast_in_dim.11.mask_ref, f32[8,1,512]{2,1,0:T(1,128)} %broadcast_in_dim.12.mrow_ref, bf16[1024,256]{1,0:T(8,128)(2,1)} %bitcast.171, ...), custom_call_target="tpu_custom_call" | custom-call | flops 9126805504 | bytes 4194304 | tf_op jit(solution)/shard_map/column_stack/pallas_call | solution.py:181
  193.2 1.7 slice.180
  195.9 0.8 copy.76.refs_5_
  197.4 0.8 copy.77.refs_8_
  198.2 0.8 copy.99
  199.0 0.8 copy.100
  200.9 1.0 copy.101
  205.5 28.1 %all-gather.3.cloned.1.call-done = bf16[128,32,512]{2,1,0:T(8,128)(2,1)} async-done(((bf16[8,32,512]{2,1,0:T(8,128)(2,1)}), bf16[128,32,512]{2,1,0:T(8,128)(2,1)}) %all-gather.3.cloned.1.call-update) | async-done | bytes 4194320 | tf_op jit(solution)/shard_map/all_gather | solution.py:464
  233.6 7.4 convert_bitcast_fusion.1
  241.1 1.4 copy.71
  242.4 1.5 fusion.10.refs_0_
  243.9 1.0 broadcast_in_dim.14.refs_3_
  244.9 1.0 broadcast_in_dim.13.refs_2_
  246.0 160.3 %pair_stack.2 = (bf16[8,128,128]{2,1,0:T(8,128)(2,1)}, bf16[16,8,32,256]{3,2,1,0:T(8,128)(2,1)}, f32[8,128,128]{2,1,0:T(8,128)}) custom-call(bf16[8,128,128]{2,1,0:T(8,128)(2,1)} %fusion.10.refs_0_, f32[1,1024]{1,0:T(1,128)} %bitcast.181, f32[8,128,128]{2,1,0:T(8,128)} %broadcast_in_dim.13.refs_2_, f32[8,128,128]{2,1,0:T(8,128)} %broadcast_in_dim.14.refs_3_, ...), custom_call_target="tpu_custom_call" | custom-call | flops 4000000000 | bytes 16000000 | tf_op jit(solution)/shard_map/pair_stack/pallas_call | solution.py:440
  406.3 28.0 %row_attention.3 = bf16[128,32,256]{2,1,0:T(8,128)(2,1)} custom-call(bf16[128,32,256]{2,1,0:T(8,128)(2,1)} %bitcast.185, f32[32,128,128]{2,1,0:T(8,128)} %broadcast_in_dim.10.mask_ref, f32[8,128,128]{2,1,0:T(8,128)} %get-tuple-element.15.bias_ref, bf16[1024,256]{1,0:T(8,128)(2,1)} %bitcast.170, bf16[256,256]{1,0:T(8,128)(2,1)} %get-tuple-element.42.wo_ref), custom_call_target="tpu_custom_call" | custom-call | flops 3221225472 | bytes 4194304 | tf_op jit(solution)/shard_map/row_attention/pallas_call | solution.py:123
  434.2 6.3 all-to-all-start.1
  440.6 1.1 copy.102
  441.7 47.7 %all-to-all-done.1.x_ref = bf16[16,8,32,256]{3,2,1,0:T(8,128)(2,1)S(1)} async-done(((bf16[16,8,32,256]{3,2,1,0:T(8,128)(2,1)}), bf16[16,8,32,256]{3,2,1,0:T(8,128)(2,1)S(1)}, u32[]{:S(2)}, u32[]{:S(2)}) %all-to-all-start.1) | async-done | bytes 2097184 | tf_op jit(solution)/shard_map/all_to_all | solution.py:478
  489.4 1.3 copy-done.1
  490.7 50.0 %column_stack.3 = (bf16[16,8,32,256]{3,2,1,0:T(8,128)(2,1)}, bf16[8,64,512]{2,1,0:T(8,128)(2,1)}) custom-call(bf16[16,8,32,256]{3,2,1,0:T(8,128)(2,1)} %copy-done.1, f32[8,512,128]{2,1,0:T(8,128)} %broadcast_in_dim.11.mask_ref, f32[8,1,512]{2,1,0:T(1,128)} %broadcast_in_dim.12.mrow_ref, bf16[1024,256]{1,0:T(8,128)(2,1)} %bitcast.172, ...), custom_call_target="tpu_custom_call" | custom-call | flops 9126805504 | bytes 4194304 | tf_op jit(solution)/shard_map/column_stack/pallas_call | solution.py:181
  540.7 1.7 slice.209
  543.1 0.8 copy.85.refs_5_
  544.5 0.8 copy.86.refs_8_
  545.2 0.8 copy.103
  546.0 0.8 copy.104
  547.9 32.0 %all-gather.5.cloned.1.call-done = bf16[128,32,512]{2,1,0:T(8,128)(2,1)} async-done(((bf16[8,32,512]{2,1,0:T(8,128)(2,1)}), bf16[128,32,512]{2,1,0:T(8,128)(2,1)}) %all-gather.5.cloned.1.call-update) | async-done | bytes 4194320 | tf_op jit(solution)/shard_map/all_gather | solution.py:464
  579.9 7.4 convert_bitcast_fusion
  587.3 1.4 copy.81
  588.7 1.5 fusion.11.refs_0_
  590.2 145.9 %pair_stack.3 = (bf16[8,128,128]{2,1,0:T(8,128)(2,1)}, bf16[16,8,32,256]{3,2,1,0:T(8,128)(2,1)}, f32[8,128,128]{2,1,0:T(8,128)}) custom-call(bf16[8,128,128]{2,1,0:T(8,128)(2,1)} %fusion.11.refs_0_, f32[1,1024]{1,0:T(1,128)} %bitcast.182, f32[8,128,128]{2,1,0:T(8,128)} %broadcast_in_dim.13.refs_2_, f32[8,128,128]{2,1,0:T(8,128)} %broadcast_in_dim.14.refs_3_, ...), custom_call_target="tpu_custom_call" | custom-call | flops 4000000000 | bytes 16000000 | tf_op jit(solution)/shard_map/pair_stack/pallas_call | solution.py:440
  736.1 4.1 copy.114
  (100 shorter events, 12.3 us)
Async XLA Ops:
  7.2 29.2 %copy-start.2 = (bf16[2,256,1024]{2,1,0:T(8,128)(2,1)S(1)}, bf16[2,256,1024]{2,1,0:T(8,128)(2,1)}, u32[]{:S(2)}) copy-start(bf16[2,256,1024]{2,1,0:T(8,128)(2,1)} %param.29) | copy-start | bytes 3145732
  35.5 2.0 copy-start.7
  66.4 4.1 copy-start.20
  66.4 74.7 %all-to-all-start = ((bf16[16,8,32,256]{3,2,1,0:T(8,128)(2,1)}), bf16[16,8,32,256]{3,2,1,0:T(8,128)(2,1)S(1)}, u32[]{:S(2)}, u32[]{:S(2)}) async-start(bf16[16,8,32,256]{3,2,1,0:T(8,128)(2,1)} %bitcast.163), calls=%async_computation | async-start | bytes 4194304 | tf_op jit(solution)/shard_map/all_to_all | solution.py:478
  70.4 163.2 %all-gather.3.cloned.1.call-start = ((), (), s32[]{:S(2)}) async-start(), calls=%async_computation.2 | async-start | bytes 4456448 | tf_op jit(solution)/shard_map/all_gather | solution.py:464
  70.5 174.4 %copy-start.19 = (f32[8,128]{1,0:T(8,128)}, f32[8,128]{1,0:T(8,128)S(1)}, u32[]{:S(2)}) copy-start(f32[8,128]{1,0:T(8,128)S(1)} %get-tuple-element.58) | copy-start | bytes 12292
  130.4 5.0 copy-start.14
  135.4 4.6 copy-start.3
  141.1 2.0 copy-start
  193.1 2.1 copy-start.5
  193.2 3.5 copy-start.6
  193.2 5.0 copy-start.8
  195.0 3.9 copy-start.9
  195.2 4.6 copy-start.22
  195.2 5.1 copy-start.23
  195.9 6.0 copy-start.21
  195.9 6.9 copy-start.15
  195.9 6.8 copy-start.16
  196.7 6.7 copy-start.17
  196.7 6.7 copy-start.18
  196.7 7.4 copy-start.10
  197.4 7.4 copy-start.11
  241.0 1.4 copy-start.4
  241.1 1.4 copy-start.24
  434.2 55.1 %all-to-all-start.1 = ((bf16[16,8,32,256]{3,2,1,0:T(8,128)(2,1)}), bf16[16,8,32,256]{3,2,1,0:T(8,128)(2,1)S(1)}, u32[]{:S(2)}, u32[]{:S(2)}) async-start(bf16[16,8,32,256]{3,2,1,0:T(8,128)(2,1)} %bitcast.166), calls=%async_computation.1 | async-start | bytes 4194304 | tf_op jit(solution)/shard_map/all_to_all | solution.py:478
  440.6 139.3 %all-gather.5.cloned.1.call-start = ((), (), s32[]{:S(2)}) async-start(), calls=%async_computation.3 | async-start | bytes 4456448 | tf_op jit(solution)/shard_map/all_gather | solution.py:464
  489.4 1.3 copy-start.1
  540.6 39.3 %copy-start.13 = (bf16[8,64,512]{2,1,0:T(8,128)(2,1)S(1)}, bf16[8,64,512]{2,1,0:T(8,128)(2,1)}, u32[]{:S(2)}) copy-start(bf16[8,64,512]{2,1,0:T(8,128)(2,1)} %get-tuple-element.16) | copy-start | bytes 1572868
  587.3 1.4 copy-start.25
  587.3 1.4 copy-start.26
  736.1 4.1 copy-start.12
Sparse Core Ops, SparseCore 0:
  195.1 38.4 all-gather.2
  542.6 37.2 all-gather.4

commit v3 on v2

v3 whole, which is shorter than its diff:
```python
import functools
import math

import jax
import jax.numpy as jnp
from jax import lax
from jax.experimental import pallas as pl
from jax.experimental.pallas import tpu as pltpu
from jax.sharding import PartitionSpec as P

GROUP_AXIS = 'dap'
PARTS_AXIS = 'req'
LOG2E = math.log2(math.e)
MASKED = -1e9 * LOG2E
LANES = 128
AHEAD = 4
F32 = jnp.float32
BF16 = jnp.bfloat16
NT = (((1,), (1,)), ((), ()))
TN = (((0,), (0,)), ((), ()))


def layer_norm_f32(values):
    centered = values - jnp.mean(values, axis=-1, keepdims=True)
    variance = jnp.mean(centered * centered, axis=-1, keepdims=True)
    return (centered * lax.rsqrt(variance + 1e-5)).astype(BF16)


def layer_norm(x):
    return layer_norm_f32(x.astype(F32))


def residual(x, update):
    return (x.astype(F32) + update).astype(BF16)


def dense(x, weight):
    return jnp.einsum('...c,cf->...f', x, weight, preferred_element_type=F32)


def softmax_keys_first(logits):
    top = jnp.max(logits, axis=0, keepdims=True)
    raised = jnp.exp2(logits - top)
    total = jnp.sum(raised, axis=0, keepdims=True)
    return (raised * (1.0 / total)).astype(BF16)


def pipelined_units(units, ahead, first_stage, second_stage):
    ready = {}
    for idx in range(min(ahead, len(units))):
        ready[idx] = first_stage(*units[idx])
    for idx in range(len(units)):
        if idx + ahead < len(units):
            ready[idx + ahead] = first_stage(*units[idx + ahead])
        second_stage(ready.pop(idx), *units[idx])


def attention_rows(proj, gated, base, rows, heads, width, load_row, w_t, w_out, mask_of, bias_of, store_row):
    head_dim = width // heads
    scale = head_dim ** -0.5 * LOG2E

    def head_rows(j, part, h):
        lo = part * width + h * head_dim
        return proj[j, lo:lo + head_dim, :]

    normed = [layer_norm_f32(load_row(base + j)) for j in range(rows)]
    for j in range(rows):
        proj[j] = lax.dot_general(w_t, normed[j], NT, preferred_element_type=F32).astype(BF16)

    def logits_of(j, h):
        return lax.dot_general(head_rows(j, 1, h), head_rows(j, 0, h), TN, preferred_element_type=F32)

    def finish(raw, j, h):
        logits = jnp.where(mask_of(base + j) > 0.0, raw * scale + bias_of(h), MASKED)
        out_t = jnp.dot(head_rows(j, 2, h), softmax_keys_first(logits), preferred_element_type=F32)
        gate = jax.nn.sigmoid(head_rows(j, 3, h).astype(F32))
        gated[j, h * head_dim:(h + 1) * head_dim, :] = (out_t * gate).astype(BF16)

    pipelined_units([(j, h) for j in range(rows) for h in range(heads)], AHEAD, logits_of, finish)
    for j in range(rows):
        store_row(base + j, load_row(base + j) + lax.dot_general(gated[j], w_out, TN, preferred_element_type=F32))


def column_residue(heads, x, proj, gated, mask_ref, mrow, w_ref, wo_ref, win_ref, wtr_ref, wopm_ref):
    width = wo_ref.shape[0]
    head_dim = width // heads
    scale = head_dim ** -0.5 * LOG2E
    length, lanes = mask_ref.shape
    proj[...] = lax.dot_general(w_ref[...], layer_norm_f32(x), NT, preferred_element_type=F32).astype(BF16)

    def head_rows(part, h, cols=slice(None)):
        lo = part * width + h * head_dim
        return proj[lo:lo + head_dim, cols]

    def columns(c):
        return slice(c * lanes, (c + 1) * lanes)

    def logits_of(h, c):
        return lax.dot_general(head_rows(1, h), head_rows(0, h, columns(c)), TN, preferred_element_type=F32)

    def finish(raw, h, c):
        logits = jnp.where(mask_ref[...] > 0.0, raw * scale, MASKED)
        out_t = jnp.dot(head_rows(2, h), softmax_keys_first(logits), preferred_element_type=F32)
        gate = jax.nn.sigmoid(head_rows(3, h, columns(c)).astype(F32))
        gated[h * head_dim:(h + 1) * head_dim, columns(c)] = (out_t * gate).astype(BF16)

    pipelined_units([(h, c) for h in range(heads) for c in range(length // lanes)], AHEAD, logits_of, finish)
    update = lax.dot_general(gated[...], wo_ref[...], TN, preferred_element_type=F32)
    x = (x + update).astype(BF16).astype(F32)
    hidden = jnp.maximum(jnp.dot(layer_norm_f32(x), win_ref[...], preferred_element_type=F32), 0.0).astype(BF16)
    x = (x + jnp.dot(hidden, wtr_ref[...], preferred_element_type=F32)).astype(BF16)
    ab_t = lax.dot_general(wopm_ref[...], layer_norm_f32(x.astype(F32)), NT, preferred_element_type=F32).astype(BF16)
    return x, (ab_t.astype(F32) * mrow).astype(BF16)


def peer_copy(source, target, send_sem, recv_sem, dst_dev):
    return pltpu.make_async_remote_copy(src_ref=source, dst_ref=target, send_sem=send_sem, recv_sem=recv_sem,
                                        device_id={GROUP_AXIS: dst_dev}, device_id_type=pl.DeviceIdType.MESH)


def for_peers(n_dev, me, body, lo=1, hi=None):
    def step(k, carry):
        body(lax.rem(me + k, n_dev))
        return carry
    lax.fori_loop(lo, n_dev if hi is None else hi, step, 0)


def rows_and_columns_kernel(heads, n_dev, first, group, *refs):
    n_m = 1 if first else 2
    m_refs, refs = refs[:n_m], refs[n_m:]
    (mask_ref, bias_ref, cmask_ref, mrow_ref, rw_ref, rwo_ref, cw_ref, cwo_ref, win_ref, wtr_ref, wopm_ref,
     o_ref, ab_ref, late_ref, proj, gated, cproj, cgated, stage_out, s_buf, r_buf, sends, recvs, own_sem) = refs[:24]
    n_seq, length = mask_ref.shape[:2]
    half = late_ref.shape[2]
    block = s_buf.shape[3]
    n_blocks = n_seq // block
    width = rwo_ref.shape[0]
    parts = stage_out.shape[0]
    me = lax.axis_index(GROUP_AXIS)
    entry_barrier(n_dev, me)
    if first:
        load_row = lambda s: m_refs[0][s].astype(F32)
    else:
        stage_in = refs[24]
        for part in range(parts):
            for d in range(n_dev):
                for k in range(2):
                    lo = (d * 2 + k) * half * n_seq
                    stage_in[part, lo:lo + half * n_seq, :] = m_refs[k][d, :, :, part * LANES:(part + 1) * LANES].astype(F32).reshape(half * n_seq, LANES)
        load_row = lambda s: jnp.concatenate([stage_in[part, pl.ds(s, length, stride=n_seq), :] for part in range(parts)], -1)

    def early(b, dst_dev, slot):
        return peer_copy(s_buf.at[b, dst_dev, pl.ds(0, half)], r_buf.at[slot, b], sends.at[0, b, dst_dev], recvs.at[0, b, slot], dst_dev)

    def late(b, dst_dev, slot):
        return peer_copy(s_buf.at[b, dst_dev, pl.ds(half, half)], late_ref.at[slot, b], sends.at[1, b, dst_dev], recvs.at[1, b, slot], dst_dev)

    def row_block(b, carry):
        def store_row(s, value):
            for part in range(parts):
                stage_out[part, pl.ds(s - b * block, length, stride=block), :] = value[:, part * LANES:(part + 1) * LANES]

        def some_rows(t, inner):
            attention_rows(proj, gated, b * block + t * group, group, heads, width, load_row, rw_ref[...], rwo_ref[...],
                           lambda s: mask_ref[s], lambda h: bias_ref[h], store_row)
            return inner

        lax.fori_loop(0, block // group, some_rows, 0)
        for part in range(parts):
            s_buf[b, :, :, :, part * LANES:(part + 1) * LANES] = stage_out[part].reshape(n_dev, 2 * half, block, LANES).astype(BF16)
        for_peers(n_dev, me, lambda d: early(b, d, me).start())
        r_buf[me, b] = s_buf[b, me, 0:half]
        return carry

    lax.fori_loop(0, n_blocks, row_block, 0)
    own = [pltpu.make_async_copy(s_buf.at[b, me, pl.ds(half, half)], late_ref.at[me, b], own_sem.at[b]) for b in range(n_blocks)]
    for b in range(n_blocks):
        for_peers(n_dev, me, lambda d: late(b, d, me).start())
        own[b].start()
    for b in range(n_blocks):
        for_peers(n_dev, me, lambda d: early(b, d, d).wait_recv())

    def residue(r, carry):
        x = r_buf[:, :, r].astype(F32).reshape(n_dev * n_seq, -1)
        x, ab = column_residue(heads, x, cproj, cgated, cmask_ref.at[r], mrow_ref[r], cw_ref, cwo_ref, win_ref, wtr_ref, wopm_ref)
        o_ref[:, r] = x.reshape(n_dev, n_seq, -1)
        ab_ref[r] = ab
        return carry

    lax.fori_loop(0, half, residue, 0)
    for b in range(n_blocks):
        own[b].wait()
        for_peers(n_dev, me, lambda d: late(b, d, d).wait_recv())
        for_peers(n_dev, me, lambda d: early(b, d, me).wait_send())
        for_peers(n_dev, me, lambda d: late(b, d, me).wait_send())


def layer_of(stacked, layer):
    return pl.BlockSpec((None,) + stacked.shape[1:], lambda step: (layer,) + (0,) * (stacked.ndim - 1))


VMEM_SPEC = pl.BlockSpec(memory_space=pltpu.VMEM)
ANY_SPEC = pl.BlockSpec(memory_space=pl.ANY)


def rows_and_columns(m_arrays, bias_t, masks, stacked, layer, heads, group=4, block=8):
    n_dev = masks['n_dev']
    n_seq, length = masks['seq'].shape[:2]
    first = len(m_arrays) == 1
    dim = m_arrays[0].shape[-1]
    half = length // n_dev // 2
    n_blocks = n_seq // block
    seq_all = n_dev * n_seq
    weights = [stacked[k] for k in ('row_qkvg', 'row_out', 'col_qkvg', 'col_out', 'mtr_in', 'mtr_out', 'opm_proj')]
    width = stacked['row_out'].shape[1]
    n_opm = stacked['opm_proj'].shape[1]
    scratch = [
        pltpu.VMEM((group, 4 * width, length), BF16), pltpu.VMEM((group, width, length), BF16),
        pltpu.VMEM((4 * width, seq_all), BF16), pltpu.VMEM((width, seq_all), BF16),
        pltpu.VMEM((dim // LANES, length * block, LANES), F32),
        pltpu.VMEM((n_blocks, n_dev, 2 * half, block, dim), BF16), pltpu.VMEM((n_dev, n_blocks, half, block, dim), BF16),
        pltpu.SemaphoreType.DMA((2, n_blocks, n_dev)), pltpu.SemaphoreType.DMA((2, n_blocks, n_dev)), pltpu.SemaphoreType.DMA((n_blocks,)),
    ]
    if not first:
        scratch.append(pltpu.VMEM((dim // LANES, length * n_seq, LANES), F32))
    n_data = len(m_arrays) + 4
    return pl.pallas_call(
        functools.partial(rows_and_columns_kernel, heads, n_dev, first, group),
        grid=(1,),
        in_specs=[VMEM_SPEC] * n_data + [layer_of(w, layer) for w in weights],
        out_specs=[VMEM_SPEC, VMEM_SPEC, ANY_SPEC],
        out_shape=[jax.ShapeDtypeStruct((n_dev, half, n_seq, dim), BF16), jax.ShapeDtypeStruct((half, n_opm, seq_all), BF16),
                   jax.ShapeDtypeStruct((n_dev, n_blocks, half, block, dim), BF16)],
        scratch_shapes=scratch,
        compiler_params=pltpu.CompilerParams(collective_id=3 * layer, has_side_effects=True),
        cost_estimate=pl.CostEstimate(flops=20_000_000_000, bytes_accessed=12_000_000, transcendentals=16_000_000),
        name='rows_and_columns',
    )(*m_arrays, masks['seq'], bias_t, masks['res'][:half], masks['res_row'][:half], *weights)


def late_columns_kernel(heads, n_dev, late_ref, cmask_ref, mrow_ref, m_ref, cw_ref, cwo_ref, win_ref, wtr_ref, wopm_ref,
                        o_ref, ab_ref, mback_ref, cproj, cgated, sends, recvs, own_sem):
    me = lax.axis_index(GROUP_AXIS)
    half = late_ref.shape[2]
    n_seq = late_ref.shape[1] * late_ref.shape[3]
    entry_barrier(n_dev, me)
    copy = lambda d, slot: peer_copy(m_ref.at[d], mback_ref.at[slot], sends.at[d], recvs.at[slot], d)
    own = pltpu.make_async_copy(m_ref.at[me], mback_ref.at[me], own_sem)
    own.start()
    for_peers(n_dev, me, lambda d: copy(d, me).start())

    def residue(r, carry):
        x = late_ref[:, :, r].astype(F32).reshape(n_dev * n_seq, -1)
        x, ab = column_residue(heads, x, cproj, cgated, cmask_ref.at[r], mrow_ref[r], cw_ref, cwo_ref, win_ref, wtr_ref, wopm_ref)
        o_ref[:, r] = x.reshape(n_dev, n_seq, -1)
        ab_ref[r] = ab
        return carry

    lax.fori_loop(0, half, residue, 0)
    own.wait()
    for_peers(n_dev, me, lambda d: copy(d, d).wait_recv())
    for_peers(n_dev, me, lambda d: copy(d, me).wait_send())


def late_columns(late, m_half, masks, stacked, layer, heads):
    n_dev, n_blocks, half, block, dim = late.shape
    seq_all = n_dev * n_blocks * block
    weights = [stacked[k] for k in ('col_qkvg', 'col_out', 'mtr_in', 'mtr_out', 'opm_proj')]
    width = stacked['row_out'].shape[1]
    n_opm = stacked['opm_proj'].shape[1]
    return pl.pallas_call(
        functools.partial(late_columns_kernel, heads, n_dev),
        grid=(1,),
        in_specs=[VMEM_SPEC] * 3 + [ANY_SPEC] + [layer_of(w, layer) for w in weights],
        out_specs=[VMEM_SPEC, VMEM_SPEC, ANY_SPEC],
        out_shape=[jax.ShapeDtypeStruct(m_half.shape, BF16), jax.ShapeDtypeStruct((half, n_opm, seq_all), BF16), jax.ShapeDtypeStruct(m_half.shape, BF16)],
        scratch_shapes=[pltpu.VMEM((4 * width, seq_all), BF16), pltpu.VMEM((width, seq_all), BF16),
                        pltpu.SemaphoreType.DMA((n_dev,)), pltpu.SemaphoreType.DMA((n_dev,)), pltpu.SemaphoreType.DMA],
        compiler_params=pltpu.CompilerParams(collective_id=3 * layer + 1, has_side_effects=True),
        cost_estimate=pl.CostEstimate(flops=20_000_000_000, bytes_accessed=12_000_000, transcendentals=8_000_000),
        name='late_columns',
    )(late, masks['res'][half:], masks['res_row'][half:], m_half, *weights)


class Exchange:
    def __init__(self, n_dev, me, sends, recvs):
        self.n_dev, self.me, self.sends, self.recvs, self.used = n_dev, me, sends, recvs, 0

    def start(self, source, target, broadcast=False):
        phase = self.used
        self.used += 1
        pick = (lambda d: source) if broadcast else (lambda d: source.at[d])

        def copy(dst_dev, slot):
            return pltpu.make_async_remote_copy(
                src_ref=pick(dst_dev), dst_ref=target.at[slot], send_sem=self.sends.at[phase, dst_dev], recv_sem=self.recvs.at[phase, slot],
                device_id={GROUP_AXIS: dst_dev}, device_id_type=pl.DeviceIdType.MESH)

        def send(step, carry):
            copy(lax.rem(self.me + step, self.n_dev), self.me).start()
            return carry

        lax.fori_loop(1, self.n_dev, send, 0)
        target[self.me] = source[...] if broadcast else source[self.me]

        def finish():
            def wait(step, carry):
                other = lax.rem(self.me + step, self.n_dev)
                copy(other, other).wait_recv()
                copy(other, self.me).wait_send()
                return carry

            lax.fori_loop(1, self.n_dev, wait, 0)

        return finish


def entry_barrier(n_dev, me):
    barrier = pltpu.get_barrier_semaphore()

    def signal(step, carry):
        pl.semaphore_signal(barrier, inc=1, device_id={GROUP_AXIS: lax.rem(me + step, n_dev)}, device_id_type=pl.DeviceIdType.MESH)
        return carry

    lax.fori_loop(1, n_dev, signal, 0)
    pl.semaphore_wait(barrier, n_dev - 1)


def pair_kernel(n_dev, with_bias, *refs):
    (z_ref, mrow_ref, start_ref, end_ref, m_ref,
     tmo_w, tmo_p, tmo_out, tmi_w, tmi_p, tmi_out, tas_w, tas_b, tas_out, tae_w, tae_b, tae_out, ptr_in, ptr_out, next_b,
     o_ref, mback_ref, bias_ref,
     zbuf, tbuf, stage, ab_send, ab_recv, x_send, x_recv, ln_stage, gate, proj, gated, bias_t, bias_send, bias_recv, z_send, z_recv, zb_recv, nb_send, nb_recv,
     sends, recvs, m_sends, m_recvs, m_own) = refs
    n_res, length, dim = z_ref.shape
    tri = tmo_out.shape[0]
    n_chan = tri // n_dev
    tokens = n_res * length
    me = lax.axis_index(GROUP_AXIS)
    entry_barrier(n_dev, me)
    exchange = Exchange(n_dev, me, sends, recvs)

    def m_copy(dst_dev, slot):
        return pltpu.make_async_remote_copy(
            src_ref=m_ref.at[dst_dev], dst_ref=mback_ref.at[slot], send_sem=m_sends.at[dst_dev], recv_sem=m_recvs.at[slot],
            device_id={GROUP_AXIS: dst_dev}, device_id_type=pl.DeviceIdType.MESH)

    own = pltpu.make_async_copy(m_ref.at[me], mback_ref.at[me], m_own)
    own.start()

    def m_steps(lo, hi):
        def send(step, carry):
            m_copy(lax.rem(me + step, n_dev), me).start()
            return carry
        lax.fori_loop(lo, hi, send, 0)

    def normed_tokens():
        return layer_norm_f32(zbuf[...].astype(F32).reshape(tokens, dim))

    def tri_mul(turn, w_ref, p_ref, out_ref, contract):
        x_norm = normed_tokens()
        for part in range(2):
            value = lax.dot_general(w_ref[part * tri:(part + 1) * tri, :], x_norm, NT, preferred_element_type=F32)
            opened = lax.dot_general(w_ref[(2 + part) * tri:(3 + part) * tri, :], x_norm, NT, preferred_element_type=F32)
            gated_t = mrow_ref[...] * jax.nn.sigmoid(opened) * value
            for d in range(n_dev):
                for i in range(n_res):
                    tile = gated_t[d * n_chan:(d + 1) * n_chan, i * length:(i + 1) * length]
                    stage[pl.ds(d * n_chan * n_res + i, n_chan, stride=n_res), :] = tile
            ab_send[turn, :, part] = stage[...].reshape(n_dev, n_chan, n_res, length).astype(BF16)
        arrived = exchange.start(ab_send.at[turn], ab_recv.at[turn])
        m_steps(1 + 4 * turn, 3 + 4 * turn)
        gate[...] = jax.nn.sigmoid(jnp.dot(x_norm, p_ref[:, 4 * tri:], preferred_element_type=F32))
        arrived()
        for c in range(n_chan):
            left = ab_recv[turn, :, 0, c].astype(F32).reshape(length, length).astype(BF16)
            right = ab_recv[turn, :, 1, c].astype(F32).reshape(length, length).astype(BF16)
            product = lax.dot_general(left, right, contract, preferred_element_type=F32)
            x_send[turn, :, c] = product.reshape(n_dev, n_res, length)
        arrived = exchange.start(x_send.at[turn], x_recv.at[turn])
        m_steps(3 + 4 * turn, 5 + 4 * turn)
        arrived()
        values = x_recv[turn].reshape(tri, n_res, length)
        centered = values - jnp.mean(values, axis=0, keepdims=True)
        inverse = lax.rsqrt(jnp.mean(centered * centered, axis=0, keepdims=True) + 1e-5)
        pitch = tri + 8
        for c in range(tri):
            ln_stage[pl.ds(c, n_res, stride=pitch), :] = centered[c] * inverse[0]
        for i in range(n_res):
            columns = ln_stage[i * pitch:i * pitch + tri, :].astype(BF16)
            update = gate[i * length:(i + 1) * length, :] * lax.dot_general(columns, out_ref[...], TN, preferred_element_type=F32)
            zbuf[i] = (zbuf[i].astype(F32) + update).astype(BF16)

    def local_bias(x_norm, b_ref, send_ref):
        heads_pad = b_ref.shape[0]
        rows = lax.dot_general(b_ref[...], x_norm, NT, preferred_element_type=F32)
        for i in range(n_res):
            stage[pl.ds(i, heads_pad, stride=n_res), :] = rows[:, i * length:(i + 1) * length]
        heads = send_ref.shape[0]
        send_ref[...] = stage[0:heads * n_res, :].reshape(heads, n_res, length).astype(BF16)

    def attention(source, w_ref, out_ref, mask_ref, heads):
        def store_row(j, value):
            source[j] = value.astype(BF16)

        attention_rows(proj, gated, 0, n_res, heads, out_ref.shape[0], lambda j: source[j].astype(F32), w_ref[...], out_ref[...],
                       lambda j: mask_ref[j], lambda h: bias_t[h], store_row)

    def swap_blocks(source):
        for i in range(n_res):
            row = source[i].astype(F32)
            for d in range(n_dev):
                stage[pl.ds(d * n_res * n_res + i, n_res, stride=n_res), :] = row[d * n_res:(d + 1) * n_res, :]
        return stage[...].reshape(n_dev, n_res, n_res, dim).astype(BF16)

    def rows_of(received, i):
        return received[:, i].astype(F32).reshape(length, dim).astype(BF16)

    heads = bias_send.shape[1]
    zbuf[...] = z_ref[...]
    tri_mul(0, tmo_w, tmo_p, tmo_out, NT)
    tri_mul(1, tmi_w, tmi_p, tmi_out, TN)
    local_bias(normed_tokens(), tas_b, bias_send.at[0])
    arrived = exchange.start(bias_send.at[0], bias_recv.at[0], broadcast=True)
    m_steps(9, 11)
    arrived()
    for h in range(heads):
        bias_t[h] = rows_of(bias_recv.at[0], h).astype(F32).T * LOG2E
    attention(zbuf, tas_w, tas_out, start_ref, heads)
    local_bias(normed_tokens(), tae_b, bias_send.at[1])
    bias_arrived = exchange.start(bias_send.at[1], bias_recv.at[1], broadcast=True)
    z_send[0] = swap_blocks(zbuf)
    arrived = exchange.start(z_send.at[0], z_recv)
    m_steps(11, 13)
    bias_arrived()
    for h in range(heads):
        bias_t[h] = rows_of(bias_recv.at[1], h).astype(F32) * LOG2E
    arrived()
    for j in range(n_res):
        tbuf[j] = rows_of(z_recv, j)
    attention(tbuf, tae_w, tae_out, end_ref, heads)
    z_send[1] = swap_blocks(tbuf)
    arrived = exchange.start(z_send.at[1], zb_recv)
    m_steps(13, n_dev)
    arrived()
    for i in range(n_res):
        zbuf[i] = rows_of(zb_recv, i)
    x_norm = normed_tokens()
    hidden = jnp.maximum(jnp.dot(x_norm, ptr_in[...], preferred_element_type=F32), 0.0).astype(BF16)
    update = jnp.dot(hidden, ptr_out[...], preferred_element_type=F32)
    result = (zbuf[...].astype(F32) + update.reshape(n_res, length, dim)).astype(BF16)
    o_ref[...] = result
    if with_bias:
        zbuf[...] = result
        local_bias(normed_tokens(), next_b, nb_send)
        arrived = exchange.start(nb_send, nb_recv, broadcast=True)
        arrived()
        for h in range(bias_ref.shape[0]):
            bias_ref[h] = rows_of(nb_recv, h).astype(F32).T * LOG2E
    else:
        bias_ref[...] = jnp.zeros_like(bias_ref)
    own.wait()

    def m_wait(step, carry):
        other = lax.rem(me + step, n_dev)
        m_copy(other, other).wait_recv()
        m_copy(other, me).wait_send()
        return carry

    lax.fori_loop(1, n_dev, m_wait, 0)


def pair_stack(pair_loc, m_half, masks, stacked, layer, with_bias):
    n_res, length, dim = pair_loc.shape
    n_dev = masks['n_dev']
    tri = stacked['tmo_out'].shape[1]
    heads = masks['pair_heads']
    row_heads = stacked['row_bias'].shape[1]
    n_chan = tri // n_dev
    next_layer = layer + 1 if with_bias else layer
    names = ('tmo_w', 'tmo_proj', 'tmo_out', 'tmi_w', 'tmi_proj', 'tmi_out', 'tas_qkvg', 'tas_bias', 'tas_out', 'tae_qkvg', 'tae_bias', 'tae_out', 'ptr_in', 'ptr_out')
    weights = [stacked[k] for k in names] + [stacked['row_bias']]
    specs = [layer_of(w, layer) for w in weights[:-1]] + [layer_of(weights[-1], next_layer)]
    width = stacked['tas_out'].shape[1]
    n_phases = 9
    scratch = [
        pltpu.VMEM((n_res, length, dim), BF16), pltpu.VMEM((n_res, length, dim), BF16),
        pltpu.VMEM((n_dev * n_res * n_res, LANES), F32),
        pltpu.VMEM((2, n_dev, 2, n_chan, n_res, length), BF16), pltpu.VMEM((2, n_dev, 2, n_chan, n_res, length), BF16),
        pltpu.VMEM((2, n_dev, n_chan, n_res, length), F32), pltpu.VMEM((2, n_dev, n_chan, n_res, length), F32),
        pltpu.VMEM((n_res * (tri + 8), length), F32), pltpu.VMEM((n_res * length, dim), F32),
        pltpu.VMEM((n_res, 4 * width, length), BF16), pltpu.VMEM((n_res, width, length), BF16),
        pltpu.VMEM((heads, length, length), F32),
        pltpu.VMEM((2, heads, n_res, length), BF16), pltpu.VMEM((2, n_dev, heads, n_res, length), BF16),
        pltpu.VMEM((2, n_dev, n_res, n_res, dim), BF16), pltpu.VMEM((n_dev, n_res, n_res, dim), BF16), pltpu.VMEM((n_dev, n_res, n_res, dim), BF16),
        pltpu.VMEM((row_heads, n_res, length), BF16), pltpu.VMEM((n_dev, row_heads, n_res, length), BF16),
        pltpu.SemaphoreType.DMA((n_phases, n_dev)), pltpu.SemaphoreType.DMA((n_phases, n_dev)),
        pltpu.SemaphoreType.DMA((n_dev,)), pltpu.SemaphoreType.DMA((n_dev,)), pltpu.SemaphoreType.DMA,
    ]
    return pl.pallas_call(
        functools.partial(pair_kernel, n_dev, with_bias),
        grid=(1,),
        in_specs=[VMEM_SPEC] * 4 + [ANY_SPEC] + specs,
        out_specs=[VMEM_SPEC, ANY_SPEC, VMEM_SPEC],
        out_shape=[jax.ShapeDtypeStruct(pair_loc.shape, BF16), jax.ShapeDtypeStruct(m_half.shape, BF16), jax.ShapeDtypeStruct((row_heads, length, length), F32)],
        scratch_shapes=scratch,
        compiler_params=pltpu.CompilerParams(collective_id=3 * layer + 2, has_side_effects=True),
        cost_estimate=pl.CostEstimate(flops=4_000_000_000, bytes_accessed=16_000_000, transcendentals=4_000_000),
        name='pair_stack',
    )(pair_loc, masks['pair_rows'].reshape(1, n_res * length), masks['start'], masks['end'], m_half, *weights)


def head_bias(pair_norm, w_bias):
    return jnp.einsum('ijc,ch->hij', pair_norm, w_bias, preferred_element_type=F32).astype(BF16)


def gather_bias(pair_rows, w_bias):
    full = lax.all_gather(head_bias(layer_norm(pair_rows), w_bias), GROUP_AXIS, axis=1, tiled=True)
    return jnp.swapaxes(full, 1, 2).astype(F32) * LOG2E


def outer_product(left_act, right_half, w_out):
    opm_dim = left_act.shape[1]
    right_full = lax.all_gather(right_half, GROUP_AXIS, axis=0, tiled=True)
    outer_prod = jnp.einsum('ics,jes->ijce', left_act, right_full, preferred_element_type=F32).astype(BF16)
    n_rows, n_cols = outer_prod.shape[:2]
    return dense(outer_prod.reshape(n_rows, n_cols, opm_dim * opm_dim), w_out)


def outer_update(ab_halves, overlap, w_out, n_dev):
    opm_dim = ab_halves[0].shape[1] // 2
    left_act = jnp.concatenate([ab[:, :opm_dim] for ab in ab_halves], 0)
    halves = [outer_product(left_act, ab[:, opm_dim:], w_out) for ab in ab_halves]
    n_rows, n_cols, dim = halves[0].shape
    update = jnp.stack([part.reshape(n_rows, n_dev, n_cols // n_dev, dim) for part in halves], 2).reshape(n_rows, 2 * n_cols, dim)
    return update / (1e-3 + overlap)[:, :, None]


def evoformer_block(m_arrays, pair_loc, bias_t, masks, stacked, layer, with_bias):
    heads = masks['msa_heads']
    early, ab_early, late = rows_and_columns(m_arrays, bias_t, masks, stacked, layer, heads)
    late, ab_late, m_early = late_columns(late, early, masks, stacked, layer, heads)
    pair_loc = residual(pair_loc, outer_update((ab_early, ab_late), masks['overlap'], stacked['opm_out'][layer], masks['n_dev']))
    pair_loc, m_late, bias_t = pair_stack(pair_loc, late, masks, stacked, layer, with_bias)
    return (m_early, m_late), pair_loc, bias_t


WEIGHT_NAMES = ('row_qkvg', 'row_bias', 'row_out', 'col_qkvg', 'col_out', 'mtr_in', 'mtr_out', 'opm_proj', 'opm_out', 'tmo_proj', 'tmo_out',
                'tmi_proj', 'tmi_out', 'tas_qkvg', 'tas_bias', 'tas_out', 'tae_qkvg', 'tae_bias', 'tae_out', 'ptr_in', 'ptr_out')


def prepare_weights(weights):
    stacked = dict(zip(WEIGHT_NAMES, weights))
    for kind in ('tmo', 'tmi'):
        tri = stacked[kind + '_out'].shape[1]
        stacked[kind + '_w'] = jnp.swapaxes(stacked[kind + '_proj'][:, :, :4 * tri], 1, 2)
    for name in ('row_qkvg', 'col_qkvg', 'opm_proj', 'tas_qkvg', 'tae_qkvg'):
        stacked[name] = jnp.swapaxes(stacked[name], 1, 2)
    for name in ('row_bias', 'tas_bias', 'tae_bias'):
        stacked[name] = jnp.pad(jnp.swapaxes(stacked[name], 1, 2), ((0, 0), (0, -stacked[name].shape[2] % 8), (0, 0)))
    return stacked


def make_masks(msa_mask, pair_mask, n_dev):
    shard_idx = lax.axis_index(GROUP_AXIS)
    n_seq, length = msa_mask.shape
    n_res = pair_mask.shape[0]
    packed = jnp.concatenate([msa_mask, pair_mask], 0).astype(BF16)
    full = lax.all_gather(packed, GROUP_AXIS, axis=0, tiled=True).reshape(n_dev, n_seq + n_res, length).astype(F32)
    full_msa = full[:, :n_seq].reshape(n_dev * n_seq, length)
    full_pair = full[:, n_seq:].reshape(n_dev * n_res, length)
    res_mask = lax.dynamic_slice_in_dim(full_msa, shard_idx * n_res, n_res, 1).T
    end_mask = lax.dynamic_slice_in_dim(full_pair, shard_idx * n_res, n_res, 1).T
    lanes = lambda mask: jnp.broadcast_to(mask.astype(F32)[:, :, None], mask.shape + (length,))
    return {
        'n_dev': n_dev,
        'seq': lanes(msa_mask),
        'res': lanes(res_mask),
        'res_row': res_mask[:, None, :],
        'pair_rows': pair_mask.astype(F32),
        'start': lanes(pair_mask),
        'end': lanes(end_mask),
        'overlap': jnp.dot(res_mask, full_msa, precision=lax.Precision.DEFAULT, preferred_element_type=F32),
    }


def solution(mesh):
    row_spec = P((PARTS_AXIS, GROUP_AXIS))
    n_dev = mesh.shape[GROUP_AXIS]

    def local_body(value_a7, pair_loc, msa_mask, pair_mask, *weights):
        masks = make_masks(msa_mask, pair_mask, n_dev)
        stacked = prepare_weights(weights)
        masks['msa_heads'] = weights[1].shape[2]
        masks['pair_heads'] = weights[14].shape[2]
        bias_t = gather_bias(pair_loc, weights[1][0])
        n_layers = weights[0].shape[0]
        m_arrays = (value_a7,)
        for layer in range(n_layers):
            m_arrays, pair_loc, bias_t = evoformer_block(m_arrays, pair_loc, bias_t, masks, stacked, layer, layer + 1 < n_layers)
        n_seq, length, dim = value_a7.shape
        value_a7 = jnp.transpose(jnp.stack(m_arrays, 1), (3, 0, 1, 2, 4)).reshape(n_seq, length, dim)
        return value_a7, pair_loc

    def run_blocks(*arrays):
        n_weights = len(arrays) - 4
        return jax.shard_map(local_body, mesh=mesh, in_specs=(row_spec,) * 4 + (P(),) * n_weights, out_specs=(row_spec, row_spec), check_vma=False)(*arrays)

    return run_blocks
```

time: 757 us -> 690 us (0.911)
  waiting for transfers between devices: 108 us -> 46.9 us
  blocking collectives: 83.2 us -> 38.4 us
  local copies, waits for them, and re-layouts: 47.7 us -> 76.9 us
  Pallas kernels: 460 us -> 475 us
  starting transfers between devices: 10.5 us -> 0.51 us
    all_to_all x2 -> x0, waiting for transfers between devices: 47.7 us -> none  [evoformer_block(): by_res = lax.all_to_all(by_dev, GROUP_AXIS, 0, 0, tiled=True)]
    all_gather x1, blocking collectives: 59.9 us -> 23.2 us  [make_masks(): lax.all_gather(packed, GROUP_AXIS, axis=0, tiled=True)]
    another operation x0 -> x6, local copies, waits for them, and re-layouts: none -> 25.1 us  [the longest x4 24.9 us: run_blocks(): jax.shard_map(local_body, mesh=mesh, in_specs=(row_spec,) * 4 + (P(),) *...]
    convert_element_type x2 -> x4, local copies, waits for them, and re-layouts: 2.71 us -> 25.6 us  [outer_product(): jnp.einsum('ics,jes->ijce', left_act, right_full, preferred_element_type=...]
    pallas_call x6, Pallas kernels: 460 us -> 475 us  [the longest x2 254 us: pair_stack(): pl.pallas_call(functools.partial(pair_kernel, n_dev, with_bias), grid=(1,...]
    all_gather x2 -> x4, waiting for transfers between devices: 60.1 us -> 46.7 us  [outer_product(): right_full = lax.all_gather(right_half, GROUP_AXIS, axis=0, tiled=True)]
    all_to_all x2 -> x0, starting transfers between devices: 10.3 us -> none  [evoformer_block(): by_res = lax.all_to_all(by_dev, GROUP_AXIS, 0, 0, tiled=True)]
    squeeze x10 -> x0, local copies, waits for them, and re-layouts: 8.55 us -> none  [local_body(): layer_w = tuple((weight[layer_idx] for weight in weights))]
  transfers between devices with their start and end apart: 4 -> 4, of which waited for: 3 -> 4; matrix products, arithmetic and copies ran while one was open for 4% -> 7% of each run, Pallas kernels for 0% -> 11%
where the time goes in v3:
time: 690 us; the launch traced here: 683 us
  Pallas kernels  475 us (69%)
  local copies, waits for them, and re-layouts  76.9 us (11%)
  waiting for transfers between devices  46.9 us (7%)
  blocking collectives  38.4 us (6%)
  matrix products  24.8 us (4%)
  between operations  14.4 us (2%)
    pallas_call x2, Pallas kernels, pair_stack(): pl.pallas_call(functools.partial(pair_kernel, n_dev, with_bias), grid=(1,...  254 us
    pallas_call x2, Pallas kernels, rows_and_columns(): pl.pallas_call(functools.partial(rows_and_columns_kernel, heads, n_dev, f...  144 us
    pallas_call x2, Pallas kernels, late_columns(): pl.pallas_call(functools.partial(late_columns_kernel, heads, n_dev), grid...  76.9 us
    all_gather x4, waiting for transfers between devices, outer_product(): right_full = lax.all_gather(right_half, GROUP_AXIS, axis=0, tiled=True)  46.7 us
    convert_element_type x4, local copies, waits for them, and re-layouts, outer_product(): jnp.einsum('ics,jes->ijce', left_act, right_full, preferred_element_type=...  25.6 us
    another operation x4, local copies, waits for them, and re-layouts, run_blocks(): jax.shard_map(local_body, mesh=mesh, in_specs=(row_spec,) * 4 + (P(),) *...  24.9 us
    all_gather x1, blocking collectives, make_masks(): lax.all_gather(packed, GROUP_AXIS, axis=0, tiled=True)  23.2 us
    dot_general x4, matrix products, outer_product(): jnp.einsum('ics,jes->ijce', left_act, right_full, preferred_element_type=...  22.4 us
  transfers between devices with their start and end apart: 4, of which 4 were waited for; matrix products, arithmetic and copies ran while one was open for 7% of the time, Pallas kernels for 11%

profile of v3, /device:TPU:21, one launch (start us, length us, event | category | flops | bytes accessed | tf_op | source)
XLA Modules:
  0.0 682.9 jit_solution(4361211813222990692)
XLA Ops:
  7.3 0.8 fusion.34
  8.1 0.8 fusion.35
  8.9 23.2 %all_gather.19 = bf16[640,128]{1,0:T(8,128)(2,1)S(1)} all-gather(bf16[40,128]{1,0:T(8,128)(2,1)S(1)} %pad_maximum_fusion.2), channel_id=1, replica_groups=mesh['req'=4,'dap'=16] {'dap'}, dimensions={0}, use_global_device_ids=true | all-gather | bytes 174080 | tf_op jit(solution)/shard_map/all_gather | solution.py:569
  32.3 0.6 copy.66.refs_4_.refs_5_
  32.9 1.3 copy.65
  35.2 15.2 %all_gather.18 = bf16[8,128,128]{2,0,1:T(8,128)(2,1)S(1)} all-gather(bf16[8,8,128]{2,0,1:T(8,128)(2,1)S(1)} %fusion.4), channel_id=1, replica_groups=mesh['req'=4,'dap'=16] {'dap'}, dimensions={1}, use_global_device_ids=true | all-gather | bytes 278528 | tf_op jit(solution)/shard_map/all_gather | solution.py:518
  50.7 0.8 multiply_bitcast_fusion.refs_2_
  51.5 1.3 copy.64
  52.8 1.3 broadcast_in_dim.11.refs_3_.refs_4_
  54.2 1.9 broadcast_in_dim.10.refs_1_.refs_2_
  56.1 68.9 %rows_and_columns.2 = (bf16[16,4,32,256]{3,2,1,0:T(8,128)(2,1)}, bf16[4,64,512]{2,1,0:T(8,128)(2,1)}, bf16[16,4,4,8,256]{4,3,2,1,0:T(8,128)(2,1)}) custom-call(bf16[32,128,256]{2,1,0:T(8,128)(2,1)} %refs_0_.1, f32[32,128,128]{2,1,0:T(8,128)} %broadcast_in_dim.10.refs_1_.refs_2_, f32[8,128,128]{2,1,0:T(8,128)} %multiply_bitcast_fusion.refs_2_, ...), custom_call_target="tpu_custom_call" | custom-call | flops 20000000000 | bytes 12000000 | tf_op jit(solution)/shard_map/rows_and_columns/pallas_call | solution.py:227
  125.0 1.7 fusion.31
  127.7 1.3 broadcast_in_dim.12.cmask_ref
  129.0 36.4 %late_columns.2 = (bf16[16,4,32,256]{3,2,1,0:T(8,128)(2,1)}, bf16[4,64,512]{2,1,0:T(8,128)(2,1)}, bf16[16,4,32,256]{3,2,1,0:T(8,128)(2,1)}) custom-call(bf16[16,4,4,8,256]{4,3,2,1,0:T(8,128)(2,1)} %get-tuple-element.19.late_ref, f32[4,512,128]{2,1,0:T(8,128)} %broadcast_in_dim.12.cmask_ref, f32[4,1,512]{2,1,0:T(1,128)} %slice.73.mrow_ref, ...), custom_call_target="tpu_custom_call" | custom-call | flops 20000000000 | bytes 12000000 | tf_op jit(solution)/shard_map/late_columns/pallas_call | solution.py:271
  165.5 1.7 fusion.32
  167.5 0.9 copy.88
  168.4 0.8 copy.89
  169.3 0.8 copy.73
  170.1 0.8 copy.74
  172.4 1.0 all-gather.5.cloned.1.call-done
  173.4 5.6 convert_bitcast_fusion.3
  179.0 6.4 copy.67
  185.4 6.2 reshape.82
  191.5 20.4 %all-gather.7.cloned.1.call-done = bf16[64,32,512]{2,1,0:T(8,128)(2,1)} async-done(((bf16[4,32,512]{2,1,0:T(8,128)(2,1)}), bf16[64,32,512]{2,1,0:T(8,128)(2,1)}) %all-gather.7.cloned.1.call-update) | async-done | bytes 2097168 | tf_op jit(solution)/shard_map/all_gather | solution.py:524
  211.9 5.6 convert_bitcast_fusion.2
  217.5 6.4 copy.68
  223.9 6.2 reshape.83
  231.2 0.9 fusion.9.refs_0_
  232.1 1.0 broadcast_in_dim.14.refs_3_
  233.2 1.0 broadcast_in_dim.13.refs_2_
  234.2 136.1 %pair_stack.2 = (bf16[8,128,128]{2,1,0:T(8,128)(2,1)}, bf16[16,4,32,256]{3,2,1,0:T(8,128)(2,1)}, f32[8,128,128]{2,1,0:T(8,128)}) custom-call(bf16[8,128,128]{2,1,0:T(8,128)(2,1)} %fusion.9.refs_0_, f32[1,1024]{1,0:T(1,128)} %bitcast.144, f32[8,128,128]{2,1,0:T(8,128)} %broadcast_in_dim.13.refs_2_, f32[8,128,128]{2,1,0:T(8,128)} %broadcast_in_dim.14.refs_3_, ...), custom_call_target="tpu_custom_call" | custom-call | flops 4000000000 | bytes 16000000 | tf_op jit(solution)/shard_map/pair_stack/pallas_call | solution.py:500
  370.3 75.3 %rows_and_columns.3 = (bf16[16,4,32,256]{3,2,1,0:T(8,128)(2,1)}, bf16[4,64,512]{2,1,0:T(8,128)(2,1)}, bf16[16,4,4,8,256]{4,3,2,1,0:T(8,128)(2,1)}) custom-call(bf16[16,4,32,256]{3,2,1,0:T(8,128)(2,1)} %get-tuple-element.21.refs_0_, bf16[16,4,32,256]{3,2,1,0:T(8,128)(2,1)} %get-tuple-element.25.refs_1_, f32[32,128,128]{2,1,0:T(8,128)} %broadcast_in_dim.10.refs_1_.refs_2_, ...), custom_call_target="tpu_custom_call" | custom-call | flops 20000000000 | bytes 12000000 | tf_op jit(solution)/shard_map/rows_and_columns/pallas_call | solution.py:227
  445.6 1.6 fusion.29
  447.4 40.5 %late_columns.3 = (bf16[16,4,32,256]{3,2,1,0:T(8,128)(2,1)}, bf16[4,64,512]{2,1,0:T(8,128)(2,1)}, bf16[16,4,32,256]{3,2,1,0:T(8,128)(2,1)}) custom-call(bf16[16,4,4,8,256]{4,3,2,1,0:T(8,128)(2,1)} %get-tuple-element.27.late_ref, f32[4,512,128]{2,1,0:T(8,128)} %broadcast_in_dim.12.cmask_ref, f32[4,1,512]{2,1,0:T(1,128)} %slice.73.mrow_ref, ...), custom_call_target="tpu_custom_call" | custom-call | flops 20000000000 | bytes 12000000 | tf_op jit(solution)/shard_map/late_columns/pallas_call | solution.py:271
  487.9 1.7 fusion.30
  489.6 2.1 all-gather.9.cloned.1.call-done
  491.8 5.6 convert_bitcast_fusion.1
  497.4 6.4 copy.76
  503.8 6.2 reshape.88
  510.4 23.2 %all-gather.11.cloned.1.call-done = bf16[64,32,512]{2,1,0:T(8,128)(2,1)} async-done(((bf16[4,32,512]{2,1,0:T(8,128)(2,1)}), bf16[64,32,512]{2,1,0:T(8,128)(2,1)}) %all-gather.11.cloned.1.call-update) | async-done | bytes 2097168 | tf_op jit(solution)/shard_map/all_gather | solution.py:524
  533.5 5.6 convert_bitcast_fusion
  539.1 6.4 copy.77
  545.5 6.3 reshape.89
  552.8 0.9 add_convert_fusion.refs_0_
  553.7 117.4 %pair_stack.3 = (bf16[8,128,128]{2,1,0:T(8,128)(2,1)}, bf16[16,4,32,256]{3,2,1,0:T(8,128)(2,1)}, f32[8,128,128]{2,1,0:T(8,128)}) custom-call(bf16[8,128,128]{2,1,0:T(8,128)(2,1)} %add_convert_fusion.refs_0_, f32[1,1024]{1,0:T(1,128)} %bitcast.145, f32[8,128,128]{2,1,0:T(8,128)} %broadcast_in_dim.13.refs_2_, f32[8,128,128]{2,1,0:T(8,128)} %broadcast_in_dim.14.refs_3_, ...), custom_call_target="tpu_custom_call" | custom-call | flops 4000000000 | bytes 16000000 | tf_op jit(solution)/shard_map/pair_stack/pallas_call | solution.py:500
  671.2 1.4 maximum_bitcast_fusion
  672.9 2.5 copy.80
  675.4 0.7 copy.91
  (67 shorter events, 7.2 us)
Async XLA Ops:
  7.2 25.7 %copy-start.2 = (bf16[2,256,1024]{2,1,0:T(8,128)(2,1)S(1)}, bf16[2,256,1024]{2,1,0:T(8,128)(2,1)}, u32[]{:S(2)}) copy-start(bf16[2,256,1024]{2,1,0:T(8,128)(2,1)} %param.32) | copy-start | bytes 3145732
  7.2 27.0 %copy-start = (bf16[8,128,128]{2,1,0:T(8,128)(2,1)S(1)}, bf16[8,128,128]{2,1,0:T(8,128)(2,1)}, u32[]{:S(2)}) copy-start(bf16[8,128,128]{2,1,0:T(8,128)(2,1)} %param.26) | copy-start | bytes 786436
  7.2 166.2 %all-gather.5.cloned.1.call-start = ((), (), s32[]{:S(2)}) async-start(), calls=%async_computation | async-start | bytes 2228224 | tf_op jit(solution)/shard_map/all_gather | solution.py:524
  8.9 224.3 %copy-start.9 = (f32[8,128]{1,0:T(8,128)}, f32[8,128]{1,0:T(8,128)S(1)}, u32[]{:S(2)}) copy-start(f32[8,128]{1,0:T(8,128)S(1)} %get-tuple-element.53) | copy-start | bytes 12292
  8.9 25.9 %copy-start.12 = (bf16[2,128,8]{1,2,0:T(8,128)(2,1)S(1)}, bf16[2,128,8]{1,2,0:T(8,128)(2,1)}, u32[]{:S(2)}) copy-start(bf16[2,128,8]{1,2,0:T(8,128)(2,1)} %param.30) | copy-start | bytes 12292
  32.9 18.6 %copy-start.3 = (bf16[2,256,1024]{2,1,0:T(8,128)(2,1)S(1)}, bf16[2,256,1024]{2,1,0:T(8,128)(2,1)}, u32[]{:S(2)}) copy-start(bf16[2,256,1024]{2,1,0:T(8,128)(2,1)} %param.29) | copy-start | bytes 3145732
  126.7 85.2 %all-gather.7.cloned.1.call-start = ((), (), s32[]{:S(2)}) async-start(), calls=%async_computation.1 | async-start | bytes 2228224 | tf_op jit(solution)/shard_map/all_gather | solution.py:524
  165.4 2.1 slice-start
  165.4 3.0 slice-start.1
  165.4 3.8 copy-start.5
  165.4 4.7 copy-start.6
  167.2 3.7 copy-start.10
  167.3 4.3 copy-start.11
  167.3 324.5 %all-gather.9.cloned.1.call-start = ((), (), s32[]{:S(2)}) async-start(), calls=%async_computation.2 | async-start | bytes 2228224 | tf_op jit(solution)/shard_map/all_gather | solution.py:524
  223.9 6.2 copy-start.1
  447.3 86.2 %all-gather.11.cloned.1.call-start = ((), (), s32[]{:S(2)}) async-start(), calls=%async_computation.3 | async-start | bytes 2228224 | tf_op jit(solution)/shard_map/all_gather | solution.py:524
  551.9 1.0 copy-start.8
  553.7 117.4 %copy-start.4 = (bf16[16,4,32,256]{3,2,1,0:T(8,128)(2,1)S(1)}, bf16[16,4,32,256]{3,2,1,0:T(8,128)(2,1)}, u32[]{:S(2)}) copy-start(bf16[16,4,32,256]{3,2,1,0:T(8,128)(2,1)} %get-tuple-element.29) | copy-start | bytes 3145732
  672.9 2.5 copy-start.7
Sparse Core Ops, SparseCore 0:
  126.9 46.4 all-gather.4
  175.6 36.2 all-gather.6
  447.4 44.2 all-gather.8
  493.8 39.6 all-gather.10

commit v4 on v3

--- a/solution.py
+++ b/solution.py
@@ -369,7 +369,7 @@
                     stage[pl.ds(d * n_chan * n_res + i, n_chan, stride=n_res), :] = tile
             ab_send[turn, :, part] = stage[...].reshape(n_dev, n_chan, n_res, length).astype(BF16)
         arrived = exchange.start(ab_send.at[turn], ab_recv.at[turn])
-        m_steps(1 + 4 * turn, 3 + 4 * turn)
+        m_steps(3 + 2 * turn, 4 + 2 * turn)
         gate[...] = jax.nn.sigmoid(jnp.dot(x_norm, p_ref[:, 4 * tri:], preferred_element_type=F32))
         arrived()
         for c in range(n_chan):
@@ -378,7 +378,7 @@
             product = lax.dot_general(left, right, contract, preferred_element_type=F32)
             x_send[turn, :, c] = product.reshape(n_dev, n_res, length)
         arrived = exchange.start(x_send.at[turn], x_recv.at[turn])
-        m_steps(3 + 4 * turn, 5 + 4 * turn)
+        m_steps(4 + 2 * turn, 5 + 2 * turn)
         arrived()
         values = x_recv[turn].reshape(tri, n_res, length)
         centered = values - jnp.mean(values, axis=0, keepdims=True)
@@ -417,13 +417,14 @@
         return received[:, i].astype(F32).reshape(length, dim).astype(BF16)
 
     heads = bias_send.shape[1]
+    m_steps(1, 3)
     zbuf[...] = z_ref[...]
     tri_mul(0, tmo_w, tmo_p, tmo_out, NT)
     tri_mul(1, tmi_w, tmi_p, tmi_out, TN)
     local_bias(normed_tokens(), tas_b, bias_send.at[0])
     arrived = exchange.start(bias_send.at[0], bias_recv.at[0], broadcast=True)
-    m_steps(9, 11)
     arrived()
+    m_steps(7, 10)
     for h in range(heads):
         bias_t[h] = rows_of(bias_recv.at[0], h).astype(F32).T * LOG2E
     attention(zbuf, tas_w, tas_out, start_ref, heads)
@@ -431,11 +432,11 @@
     bias_arrived = exchange.start(bias_send.at[1], bias_recv.at[1], broadcast=True)
     z_send[0] = swap_blocks(zbuf)
     arrived = exchange.start(z_send.at[0], z_recv)
-    m_steps(11, 13)
     bias_arrived()
     for h in range(heads):
         bias_t[h] = rows_of(bias_recv.at[1], h).astype(F32) * LOG2E
     arrived()
+    m_steps(10, 13)
     for j in range(n_res):
         tbuf[j] = rows_of(z_recv, j)
     attention(tbuf, tae_w, tae_out, end_ref, heads)
@@ -510,6 +511,46 @@
     )(pair_loc, masks['pair_rows'].reshape(1, n_res * length), masks['start'], masks['end'], m_half, *weights)
 
 
+def pair_stack(pair_loc, m_half, masks, stacked, layer, with_bias):
+    n_res, length, dim = pair_loc.shape
+    n_dev = masks['n_dev']
+    tri = stacked['tmo_out'].shape[1]
+    heads = masks['pair_heads']
+    row_heads = stacked['row_bias'].shape[1]
+    n_chan = tri // n_dev
+    next_layer = layer + 1 if with_bias else layer
+    names = ('tmo_w', 'tmo_proj', 'tmo_out', 'tmi_w', 'tmi_proj', 'tmi_out', 'tas_qkvg', 'tas_bias', 'tas_out', 'tae_qkvg', 'tae_bias', 'tae_out', 'ptr_in', 'ptr_out')
+    weights = [stacked[k] for k in names] + [stacked['row_bias']]
+    specs = [layer_of(w, layer) for w in weights[:-1]] + [layer_of(weights[-1], next_layer)]
+    width = stacked['tas_out'].shape[1]
+    n_phases = 9
+    scratch = [
+        pltpu.VMEM((n_res, length, dim), BF16), pltpu.VMEM((n_res, length, dim), BF16),
+        pltpu.VMEM((n_dev * n_res * n_res, LANES), F32),
+        pltpu.VMEM((2, n_dev, 2, n_chan, n_res, length), BF16), pltpu.VMEM((2, n_dev, 2, n_chan, n_res, length), BF16),
+        pltpu.VMEM((2, n_dev, n_chan, n_res, length), F32), pltpu.VMEM((2, n_dev, n_chan, n_res, length), F32),
+        pltpu.VMEM((n_res * (tri + 8), length), F32), pltpu.VMEM((n_res * length, dim), F32),
+        pltpu.VMEM((n_res, 4 * width, length), BF16), pltpu.VMEM((n_res, width, length), BF16),
+        pltpu.VMEM((heads, length, length), F32),
+        pltpu.VMEM((2, heads, n_res, length), BF16), pltpu.VMEM((2, n_dev, heads, n_res, length), BF16),
+        pltpu.VMEM((2, n_dev, n_res, n_res, dim), BF16), pltpu.VMEM((n_dev, n_res, n_res, dim), BF16), pltpu.VMEM((n_dev, n_res, n_res, dim), BF16),
+        pltpu.VMEM((row_heads, n_res, length), BF16), pltpu.VMEM((n_dev, row_heads, n_res, length), BF16),
+        pltpu.SemaphoreType.DMA((n_phases, n_dev)), pltpu.SemaphoreType.DMA((n_phases, n_dev)),
+        pltpu.SemaphoreType.DMA((n_dev,)), pltpu.SemaphoreType.DMA((n_dev,)), pltpu.SemaphoreType.DMA,
+    ]
+    return pl.pallas_call(
+        functools.partial(pair_kernel, n_dev, with_bias),
+        grid=(1,),
+        in_specs=[VMEM_SPEC] * 4 + [ANY_SPEC] + specs,
+        out_specs=[VMEM_SPEC, ANY_SPEC, VMEM_SPEC],
+        out_shape=[jax.ShapeDtypeStruct(pair_loc.shape, BF16), jax.ShapeDtypeStruct(m_half.shape, BF16), jax.ShapeDtypeStruct((row_heads, length, length), F32)],
+        scratch_shapes=scratch,
+        compiler_params=pltpu.CompilerParams(collective_id=3 * layer + 2, has_side_effects=True),
+        cost_estimate=pl.CostEstimate(flops=4_000_000_000, bytes_accessed=16_000_000, transcendentals=4_000_000),
+        name='pair_stack',
+    )(pair_loc, masks['pair_rows'].reshape(1, n_res * length), masks['start'], masks['end'], m_half, *weights)
+
+
 def head_bias(pair_norm, w_bias):
     return jnp.einsum('ijc,ch->hij', pair_norm, w_bias, preferred_element_type=F32).astype(BF16)
 
@@ -519,28 +560,126 @@
     return jnp.swapaxes(full, 1, 2).astype(F32) * LOG2E
 
 
-def outer_product(left_act, right_half, w_out):
-    opm_dim = left_act.shape[1]
-    right_full = lax.all_gather(right_half, GROUP_AXIS, axis=0, tiled=True)
-    outer_prod = jnp.einsum('ics,jes->ijce', left_act, right_full, preferred_element_type=F32).astype(BF16)
-    n_rows, n_cols = outer_prod.shape[:2]
-    return dense(outer_prod.reshape(n_rows, n_cols, opm_dim * opm_dim), w_out)
-
-
-def outer_update(ab_halves, overlap, w_out, n_dev):
-    opm_dim = ab_halves[0].shape[1] // 2
-    left_act = jnp.concatenate([ab[:, :opm_dim] for ab in ab_halves], 0)
-    halves = [outer_product(left_act, ab[:, opm_dim:], w_out) for ab in ab_halves]
-    n_rows, n_cols, dim = halves[0].shape
-    update = jnp.stack([part.reshape(n_rows, n_dev, n_cols // n_dev, dim) for part in halves], 2).reshape(n_rows, 2 * n_cols, dim)
+def residues_inside(right_ref, stage, store):
+    n_rows, n_e, length = right_ref.shape
+    pitch = stage.shape[1] // n_e
+
+    def one(j, carry):
+        tile = right_ref[j].astype(F32)
+        for part in range(length // LANES):
+            for lo in range(0, n_e, 8):
+                stage[part, pl.ds(lo * pitch + j, 8, stride=pitch), :] = tile[lo:lo + 8, part * LANES:(part + 1) * LANES]
+        return carry
+
+    lax.fori_loop(0, n_rows, one, 0)
+    for e in range(n_e):
+        for part in range(length // LANES):
+            store(e, part, stage[part, e * pitch:e * pitch + n_rows, :].astype(BF16))
+
+
+def outer_layout_kernel(right_ref, o_ref, stage):
+    def store(e, part, value):
+        o_ref[e, :, part * LANES:(part + 1) * LANES] = value
+    residues_inside(right_ref, stage, store)
+
+
+def outer_product_kernel(early_ref, late_ref, right_ref, right_late_ref, w_ref, o_ref, stage, left, rows, flat):
+    half = early_ref.shape[0]
+    n_half = right_ref.shape[1]
+    dim = early_ref.shape[1] // 2
+    for k, ab_ref in enumerate((early_ref, late_ref)):
+        for r in range(half):
+            left[(k * half + r) * dim:(k * half + r + 1) * dim, :] = ab_ref[r, 0:dim, :]
+
+    def store(e, part, value):
+        rows[e, n_half:2 * n_half, part * LANES:(part + 1) * LANES] = value
+
+    residues_inside(right_late_ref, stage, store)
+    for e in range(dim):
+        rows[e, 0:n_half, :] = right_ref[e]
+
+    def one(step, carry):
+        some = [step * 4 + k for k in range(4)]
+        products = [lax.dot_general(left[...], rows[e], NT, preferred_element_type=F32).astype(BF16) for e in some]
+        for e, product in zip(some, products):
+            for i in range(2 * half):
+                flat[i, pl.ds(pl.multiple_of(e * dim, dim), dim), :] = product[i * dim:(i + 1) * dim, :]
+        return carry
+
+    lax.fori_loop(0, dim // 4, one, 0)
+    for i in range(2 * half):
+        o_ref[i] = jnp.dot(w_ref[...], flat[i], preferred_element_type=F32).T
+
+
+def outer_update(ab_halves, overlap, stacked, layer, n_dev):
+    half, n_ab, seq_all = ab_halves[0].shape
+    opm_dim = n_ab // 2
+    n_half = n_dev * half
+    length = 2 * n_half
+    dim = stacked['opm_w'].shape[1]
+    gathered = [lax.all_gather(ab[:, opm_dim:], GROUP_AXIS, axis=0, tiled=True) for ab in ab_halves]
+    stage = pltpu.VMEM((seq_all // LANES, opm_dim * (n_half + 8), LANES), F32)
+    early_rows = pl.pallas_call(
+        outer_layout_kernel,
+        in_specs=[VMEM_SPEC], out_specs=VMEM_SPEC,
+        out_shape=jax.ShapeDtypeStruct((opm_dim, n_half, seq_all), BF16),
+        scratch_shapes=[stage],
+        cost_estimate=pl.CostEstimate(flops=2_000_000_000, bytes_accessed=4_000_000, transcendentals=0),
+        name='outer_layout',
+    )(gathered[0])
+    update = pl.pallas_call(
+        outer_product_kernel,
+        grid=(1,),
+        in_specs=[VMEM_SPEC] * 4 + [layer_of(stacked['opm_w'], layer)], out_specs=VMEM_SPEC,
+        out_shape=jax.ShapeDtypeStruct((2 * half, length, dim), F32),
+        scratch_shapes=[stage, pltpu.VMEM((2 * half * opm_dim, seq_all), BF16), pltpu.VMEM((opm_dim, length, seq_all), BF16),
+                        pltpu.VMEM((2 * half, opm_dim * opm_dim, length), BF16)],
+        cost_estimate=pl.CostEstimate(flops=4_000_000_000, bytes_accessed=6_000_000, transcendentals=0),
+        name='outer_product',
+    )(ab_halves[0], ab_halves[1], early_rows, gathered[1], stacked['opm_w'])
+    update = update.reshape(2 * half, 2, n_dev, half, dim)
+    update = jnp.swapaxes(update, 1, 2).reshape(2 * half, length, dim)
     return update / (1e-3 + overlap)[:, :, None]
+
+
+def first_gather_kernel(n_dev, z_ref, b_ref, masks_ref, bias_ref, full_ref, stage, bias_send, bias_recv, sends, recvs):
+    n_res, length, dim = z_ref.shape
+    me = lax.axis_index(GROUP_AXIS)
+    entry_barrier(n_dev, me)
+    exchange = Exchange(n_dev, me, sends, recvs)
+    masks_arrived = exchange.start(masks_ref, full_ref, broadcast=True)
+    rows = lax.dot_general(b_ref[...], layer_norm_f32(z_ref[...].astype(F32).reshape(n_res * length, dim)), NT, preferred_element_type=F32)
+    heads = bias_send.shape[0]
+    for i in range(n_res):
+        stage[pl.ds(i, heads, stride=n_res), :] = rows[:, i * length:(i + 1) * length]
+    bias_send[...] = stage[...].reshape(heads, n_res, length).astype(BF16)
+    exchange.start(bias_send, bias_recv, broadcast=True)()
+    for h in range(heads):
+        bias_ref[h] = bias_recv[:, h].astype(F32).reshape(length, length).T * LOG2E
+    masks_arrived()
+
+
+def first_gather(pair_loc, packed_masks, stacked, n_dev):
+    n_res, length, dim = pair_loc.shape
+    heads = stacked['row_bias'].shape[1]
+    return pl.pallas_call(
+        functools.partial(first_gather_kernel, n_dev),
+        grid=(1,),
+        in_specs=[VMEM_SPEC, layer_of(stacked['row_bias'], 0), VMEM_SPEC], out_specs=[VMEM_SPEC, VMEM_SPEC],
+        out_shape=[jax.ShapeDtypeStruct((heads, length, length), F32), jax.ShapeDtypeStruct((n_dev,) + packed_masks.shape, BF16)],
+        scratch_shapes=[pltpu.VMEM((heads * n_res, length), F32), pltpu.VMEM((heads, n_res, length), BF16), pltpu.VMEM((n_dev, heads, n_res, length), BF16),
+                        pltpu.SemaphoreType.DMA((2, n_dev)), pltpu.SemaphoreType.DMA((2, n_dev))],
+        compiler_params=pltpu.CompilerParams(collective_id=3 * stacked['row_bias'].shape[0], has_side_effects=True),
+        cost_estimate=pl.CostEstimate(flops=1_000_000_000, bytes_accessed=2_000_000, transcendentals=0),
+        name='first_gather',
+    )(pair_loc, stacked['row_bias'], packed_masks)
 
 
 def evoformer_block(m_arrays, pair_loc, bias_t, masks, stacked, layer, with_bias):
     heads = masks['msa_heads']
     early, ab_early, late = rows_and_columns(m_arrays, bias_t, masks, stacked, layer, heads)
     late, ab_late, m_early = late_columns(late, early, masks, stacked, layer, heads)
-    pair_loc = residual(pair_loc, outer_update((ab_early, ab_late), masks['overlap'], stacked['opm_out'][layer], masks['n_dev']))
+    pair_loc = residual(pair_loc, outer_update((ab_early, ab_late), masks['overlap'], stacked, layer, masks['n_dev']))
     pair_loc, m_late, bias_t = pair_stack(pair_loc, late, masks, stacked, layer, with_bias)
     return (m_early, m_late), pair_loc, bias_t
 
@@ -558,15 +697,21 @@
         stacked[name] = jnp.swapaxes(stacked[name], 1, 2)
     for name in ('row_bias', 'tas_bias', 'tae_bias'):
         stacked[name] = jnp.pad(jnp.swapaxes(stacked[name], 1, 2), ((0, 0), (0, -stacked[name].shape[2] % 8), (0, 0)))
+    n_layers, flat, dim = stacked['opm_out'].shape
+    opm_dim = stacked['opm_proj'].shape[1] // 2
+    stacked['opm_w'] = jnp.transpose(stacked['opm_out'].reshape(n_layers, opm_dim, opm_dim, dim), (0, 3, 2, 1)).reshape(n_layers, dim, flat)
     return stacked
 
 
-def make_masks(msa_mask, pair_mask, n_dev):
+def pack_masks(msa_mask, pair_mask):
+    return jnp.concatenate([msa_mask, pair_mask], 0).astype(BF16)
+
+
+def make_masks(msa_mask, pair_mask, full, n_dev):
     shard_idx = lax.axis_index(GROUP_AXIS)
     n_seq, length = msa_mask.shape
     n_res = pair_mask.shape[0]
-    packed = jnp.concatenate([msa_mask, pair_mask], 0).astype(BF16)
-    full = lax.all_gather(packed, GROUP_AXIS, axis=0, tiled=True).reshape(n_dev, n_seq + n_res, length).astype(F32)
+    full = full.astype(F32)
     full_msa = full[:, :n_seq].reshape(n_dev * n_seq, length)
     full_pair = full[:, n_seq:].reshape(n_dev * n_res, length)
     res_mask = lax.dynamic_slice_in_dim(full_msa, shard_idx * n_res, n_res, 1).T
@@ -589,11 +734,11 @@
     n_dev = mesh.shape[GROUP_AXIS]
 
     def local_body(value_a7, pair_loc, msa_mask, pair_mask, *weights):
-        masks = make_masks(msa_mask, pair_mask, n_dev)
         stacked = prepare_weights(weights)
+        bias_t, full = first_gather(pair_loc, pack_masks(msa_mask, pair_mask), stacked, n_dev)
+        masks = make_masks(msa_mask, pair_mask, full, n_dev)
         masks['msa_heads'] = weights[1].shape[2]
         masks['pair_heads'] = weights[14].shape[2]
-        bias_t = gather_bias(pair_loc, weights[1][0])
         n_layers = weights[0].shape[0]
         m_arrays = (value_a7,)
         for layer in range(n_layers):

time: 690 us -> 660 us (0.957)
  Pallas kernels: 475 us -> 532 us
  local copies, waits for them, and re-layouts: 76.9 us -> 29.8 us
  blocking collectives: 38.4 us -> 0 us
  matrix products: 24.8 us -> 0.25 us
  waiting for transfers between devices: 46.9 us -> 69 us
    pallas_call x0 -> x5, Pallas kernels: none -> 50.2 us  [the longest x1 23.4 us: first_gather(): pl.pallas_call(functools.partial(first_gather_kernel, n_dev), grid=(1,),...]
    all_gather x2 -> x0, blocking collectives: 38.4 us -> none  [the longest x1 23.2 us: make_masks(): lax.all_gather(packed, GROUP_AXIS, axis=0, tiled=True)]
    convert_element_type x4 -> x0, local copies, waits for them, and re-layouts: 25.6 us -> none  [outer_product(): jnp.einsum('ics,jes->ijce', left_act, right_full, preferred_element_type=...]
    another operation x6 -> x0, local copies, waits for them, and re-layouts: 25.1 us -> none  [the longest x4 24.9 us: run_blocks(): jax.shard_map(local_body, mesh=mesh, in_specs=(row_spec,) * 4 + (P(),) *...]
    dot_general x9 -> x0, matrix products: 24.6 us -> none  [the longest x4 22.4 us: outer_product(): jnp.einsum('ics,jes->ijce', left_act, right_full, preferred_element_type=...]
    all_gather x4, waiting for transfers between devices: 46.7 us -> 68.8 us  [outer_update(): lax.all_gather(ab[:, opm_dim:], GROUP_AXIS, axis=0, tiled=True)]
    pallas_call x2, Pallas kernels: 254 us -> 261 us  [pair_stack(): pl.pallas_call(functools.partial(pair_kernel, n_dev, with_bias), grid=(1,...]
  transfers between devices with their start and end apart: 4 -> 4, of which waited for: 4 -> 3; matrix products, arithmetic and copies ran while one was open for 7% -> 2% of each run, Pallas kernels for 11% -> 13%
where the time goes in v4:
time: 660 us; the launch traced here: 652 us
  Pallas kernels  532 us (81%)
  waiting for transfers between devices  69 us (10%)
  local copies, waits for them, and re-layouts  29.8 us (5%)
  between operations  14.5 us (2%)
    pallas_call x2, Pallas kernels, pair_stack(): pl.pallas_call(functools.partial(pair_kernel, n_dev, with_bias), grid=(1,...  261 us
    pallas_call x2, Pallas kernels, rows_and_columns(): pl.pallas_call(functools.partial(rows_and_columns_kernel, heads, n_dev, f...  143 us
    pallas_call x2, Pallas kernels, late_columns(): pl.pallas_call(functools.partial(late_columns_kernel, heads, n_dev), grid...  78 us
    all_gather x4, waiting for transfers between devices, outer_update(): lax.all_gather(ab[:, opm_dim:], GROUP_AXIS, axis=0, tiled=True)  68.8 us
    pallas_call x1, Pallas kernels, first_gather(): pl.pallas_call(functools.partial(first_gather_kernel, n_dev), grid=(1,),...  23.4 us
    pallas_call x2, Pallas kernels, outer_update(): pl.pallas_call(outer_product_kernel, grid=(1,), in_specs=[VMEM_SPEC] * 4...  17.9 us
  transfers between devices with their start and end apart: 4, of which 3 were waited for; matrix products, arithmetic and copies ran while one was open for 2% of the time, Pallas kernels for 13%

profile of v4, /device:TPU:21, one launch (start us, length us, event | category | flops | bytes accessed | tf_op | source)
XLA Modules:
  0.0 651.9 jit_solution(17198807391932647467)
XLA Ops:
  7.2 0.8 fusion.3
  8.0 0.8 fusion.4
  8.8 0.6 pad_maximum_fusion.masks_ref
  9.4 23.4 %first_gather.1 = (f32[8,128,128]{2,1,0:T(8,128)}, bf16[16,40,128]{2,1,0:T(8,128)(2,1)}) custom-call(bf16[8,128,128]{2,1,0:T(8,128)(2,1)} %z_ref.1, bf16[2,8,128]{2,1,0:T(8,128)(2,1)} %bitcast.72, bf16[40,128]{1,0:T(8,128)(2,1)} %pad_maximum_fusion.masks_ref), custom_call_target="tpu_custom_call" | custom-call | flops 1000000000 | bytes 2000000 | tf_op jit(solution)/shard_map/first_gather/pallas_call | solution.py:665
  32.8 1.0 slice.60
  34.1 0.6 copy.76.refs_4_.refs_5_
  34.7 1.3 copy.74
  36.0 1.3 copy.75
  37.3 1.9 broadcast_in_dim.10.refs_1_.refs_2_
  39.2 1.3 broadcast_in_dim.11.refs_3_.refs_4_
  40.6 69.9 %rows_and_columns.2 = (bf16[16,4,32,256]{3,2,1,0:T(8,128)(2,1)}, bf16[4,64,512]{2,1,0:T(8,128)(2,1)}, bf16[16,4,4,8,256]{4,3,2,1,0:T(8,128)(2,1)}) custom-call(bf16[32,128,256]{2,1,0:T(8,128)(2,1)} %refs_0_.1, f32[32,128,128]{2,1,0:T(8,128)} %broadcast_in_dim.10.refs_1_.refs_2_, f32[8,128,128]{2,1,0:T(8,128)} %get-tuple-element.21.refs_2_, ...), custom_call_target="tpu_custom_call" | custom-call | flops 20000000000 | bytes 12000000 | tf_op jit(solution)/shard_map/rows_and_columns/pallas_call | solution.py:227
  110.5 1.6 slice.52
  112.2 0.3 all-gather.7.cloned.1.call-start
  112.4 0.6 slice.51.mrow_ref
  113.0 1.4 broadcast_in_dim.12.cmask_ref
  114.4 37.5 %late_columns.2 = (bf16[16,4,32,256]{3,2,1,0:T(8,128)(2,1)}, bf16[4,64,512]{2,1,0:T(8,128)(2,1)}, bf16[16,4,32,256]{3,2,1,0:T(8,128)(2,1)}) custom-call(bf16[16,4,4,8,256]{4,3,2,1,0:T(8,128)(2,1)} %get-tuple-element.23.late_ref, f32[4,512,128]{2,1,0:T(8,128)} %broadcast_in_dim.12.cmask_ref, f32[4,1,512]{2,1,0:T(1,128)} %slice.51.mrow_ref, ...), custom_call_target="tpu_custom_call" | custom-call | flops 20000000000 | bytes 12000000 | tf_op jit(solution)/shard_map/late_columns/pallas_call | solution.py:271
  151.9 1.6 slice.53
  154.0 1.0 copy.78.w_ref
  155.2 0.9 copy.92
  156.1 0.8 copy.93
  156.9 0.8 copy.83
  157.8 0.9 copy.84
  158.6 0.6 pad.7.refs_12_
  159.2 0.6 pad.8.refs_15_
  159.8 0.3 convolution_add_fusion
  160.1 4.7 outer_layout.2.right_ref
  164.7 32.0 %all-gather.7.cloned.1.call-done.right_late_ref = bf16[64,32,512]{2,1,0:T(8,128)(2,1)} async-done(((bf16[4,32,512]{2,1,0:T(8,128)(2,1)}), bf16[64,32,512]{2,1,0:T(8,128)(2,1)}) %all-gather.7.cloned.1.call-update) | async-done | bytes 2097168 | tf_op jit(solution)/shard_map/all_gather | solution.py:620
  196.8 9.0 %outer_product.2 = f32[8,128,128]{2,1,0:T(8,128)} custom-call(bf16[4,64,512]{2,1,0:T(8,128)(2,1)} %get-tuple-element.26.early_ref, bf16[4,64,512]{2,1,0:T(8,128)(2,1)} %get-tuple-element.27.late_ref, bf16[32,64,512]{2,1,0:T(8,128)(2,1)} %outer_layout.2.right_ref, bf16[64,32,512]{2,1,0:T(8,128)(2,1)} %all-gather.7.cloned.1.call-done.right_late_ref, ...), custom_call_target="tpu_custom_call" | custom-call | flops 4000000000 | bytes 6000000 | tf_op jit(solution)/shard_map/outer_product/pallas_call | solution.py:630
  205.7 1.1 copy.79
  206.9 0.9 add_convert_fusion.1.refs_0_
  207.8 1.0 broadcast_in_dim.13.refs_2_
  208.8 1.0 broadcast_in_dim.14.refs_3_
  209.8 134.4 %pair_stack.2 = (bf16[8,128,128]{2,1,0:T(8,128)(2,1)}, bf16[16,4,32,256]{3,2,1,0:T(8,128)(2,1)}, f32[8,128,128]{2,1,0:T(8,128)}) custom-call(bf16[8,128,128]{2,1,0:T(8,128)(2,1)} %add_convert_fusion.1.refs_0_, f32[1,1024]{1,0:T(1,128)} %bitcast.64, f32[8,128,128]{2,1,0:T(8,128)} %broadcast_in_dim.13.refs_2_, f32[8,128,128]{2,1,0:T(8,128)} %broadcast_in_dim.14.refs_3_, ...), custom_call_target="tpu_custom_call" | custom-call | flops 4000000000 | bytes 16000000 | tf_op jit(solution)/shard_map/pair_stack/pallas_call | solution.py:541
  344.2 73.4 %rows_and_columns.3 = (bf16[16,4,32,256]{3,2,1,0:T(8,128)(2,1)}, bf16[4,64,512]{2,1,0:T(8,128)(2,1)}, bf16[16,4,4,8,256]{4,3,2,1,0:T(8,128)(2,1)}) custom-call(bf16[16,4,32,256]{3,2,1,0:T(8,128)(2,1)} %get-tuple-element.25.refs_0_, bf16[16,4,32,256]{3,2,1,0:T(8,128)(2,1)} %get-tuple-element.29.refs_1_, f32[32,128,128]{2,1,0:T(8,128)} %broadcast_in_dim.10.refs_1_.refs_2_, ...), custom_call_target="tpu_custom_call" | custom-call | flops 20000000000 | bytes 12000000 | tf_op jit(solution)/shard_map/rows_and_columns/pallas_call | solution.py:227
  417.5 1.6 slice.58
  419.2 40.6 %late_columns.3 = (bf16[16,4,32,256]{3,2,1,0:T(8,128)(2,1)}, bf16[4,64,512]{2,1,0:T(8,128)(2,1)}, bf16[16,4,32,256]{3,2,1,0:T(8,128)(2,1)}) custom-call(bf16[16,4,4,8,256]{4,3,2,1,0:T(8,128)(2,1)} %get-tuple-element.31.late_ref, f32[4,512,128]{2,1,0:T(8,128)} %broadcast_in_dim.12.cmask_ref, f32[4,1,512]{2,1,0:T(1,128)} %slice.51.mrow_ref, ...), custom_call_target="tpu_custom_call" | custom-call | flops 20000000000 | bytes 12000000 | tf_op jit(solution)/shard_map/late_columns/pallas_call | solution.py:271
  459.8 1.6 slice.59
  461.4 2.6 all-gather.9.cloned.1.call-done.right_ref
  464.0 4.2 outer_layout.3.right_ref
  468.2 34.2 %all-gather.11.cloned.1.call-done.right_late_ref = bf16[64,32,512]{2,1,0:T(8,128)(2,1)} async-done(((bf16[4,32,512]{2,1,0:T(8,128)(2,1)}), bf16[64,32,512]{2,1,0:T(8,128)(2,1)}) %all-gather.11.cloned.1.call-update) | async-done | bytes 2097168 | tf_op jit(solution)/shard_map/all_gather | solution.py:620
  502.4 9.0 %outer_product.3 = f32[8,128,128]{2,1,0:T(8,128)} custom-call(bf16[4,64,512]{2,1,0:T(8,128)(2,1)} %get-tuple-element.35.early_ref, bf16[4,64,512]{2,1,0:T(8,128)(2,1)} %get-tuple-element.36.late_ref, bf16[32,64,512]{2,1,0:T(8,128)(2,1)} %outer_layout.3.right_ref, bf16[64,32,512]{2,1,0:T(8,128)(2,1)} %all-gather.11.cloned.1.call-done.right_late_ref, ...), custom_call_target="tpu_custom_call" | custom-call | flops 4000000000 | bytes 6000000 | tf_op jit(solution)/shard_map/outer_product/pallas_call | solution.py:630
  511.4 1.1 copy.87
  512.5 0.9 add_convert_fusion.refs_0_
  513.4 126.5 %pair_stack.3 = (bf16[8,128,128]{2,1,0:T(8,128)(2,1)}, bf16[16,4,32,256]{3,2,1,0:T(8,128)(2,1)}, f32[8,128,128]{2,1,0:T(8,128)}) custom-call(bf16[8,128,128]{2,1,0:T(8,128)(2,1)} %add_convert_fusion.refs_0_, f32[1,1024]{1,0:T(1,128)} %bitcast.65, f32[8,128,128]{2,1,0:T(8,128)} %broadcast_in_dim.13.refs_2_, f32[8,128,128]{2,1,0:T(8,128)} %broadcast_in_dim.14.refs_3_, ...), custom_call_target="tpu_custom_call" | custom-call | flops 4000000000 | bytes 16000000 | tf_op jit(solution)/shard_map/pair_stack/pallas_call | solution.py:541
  640.0 1.4 maximum_bitcast_fusion
  641.4 0.3 copy.88
  641.7 2.5 copy.89
  644.2 0.7 copy.95
  (47 shorter events, 1.1 us)
Async XLA Ops:
  7.2 152.9 %all-gather.5.cloned.1.call-start = ((), (), s32[]{:S(2)}) async-start(), calls=%async_computation | async-start | bytes 2228224 | tf_op jit(solution)/shard_map/all_gather | solution.py:620
  8.8 199.0 %copy-start.10 = (f32[8,128]{1,0:T(8,128)}, f32[8,128]{1,0:T(8,128)S(1)}, u32[]{:S(2)}) copy-start(f32[8,128]{1,0:T(8,128)S(1)} %get-tuple-element.51) | copy-start | bytes 12292
  9.4 25.3 %copy-start.1 = (bf16[2,256,1024]{2,1,0:T(8,128)(2,1)S(1)}, bf16[2,256,1024]{2,1,0:T(8,128)(2,1)}, u32[]{:S(2)}) copy-start(bf16[2,256,1024]{2,1,0:T(8,128)(2,1)} %param.29) | copy-start | bytes 3145732
  32.8 3.2 copy-start.2
  112.2 84.6 %all-gather.7.cloned.1.call-start = ((), (), s32[]{:S(2)}) async-start(), calls=%async_computation.1 | async-start | bytes 2228224 | tf_op jit(solution)/shard_map/all_gather | solution.py:620
  114.4 39.2 %copy-start = (bf16[16,40,128]{2,1,0:T(8,128)(2,1)S(1)}, bf16[16,40,128]{2,1,0:T(8,128)(2,1)}, u32[]{:S(2)}) copy-start(bf16[16,40,128]{2,1,0:T(8,128)(2,1)} %get-tuple-element.22) | copy-start | bytes 491524
  114.4 39.3 %copy-start.4 = (bf16[2,1024,128]{2,1,0:T(8,128)(2,1)S(1)}, bf16[2,1024,128]{2,1,0:T(8,128)(2,1)}, u32[]{:S(2)}) copy-start(bf16[2,1024,128]{2,1,0:T(8,128)(2,1)} %param.37) | copy-start | bytes 1572868
  151.9 3.3 slice-start
  153.6 310.4 %all-gather.9.cloned.1.call-start = ((), (), s32[]{:S(2)}) async-start(), calls=%async_computation.2 | async-start | bytes 2228224 | tf_op jit(solution)/shard_map/all_gather | solution.py:620
  153.7 2.3 slice-start.1
  153.8 3.2 copy-start.5
  154.0 3.8 copy-start.6
  154.0 4.6 copy-start.11
  154.0 5.2 copy-start.12
  164.7 42.1 %copy-start.8 = (bf16[8,128,128]{2,1,0:T(8,128)(2,1)S(1)}, bf16[8,128,128]{2,1,0:T(8,128)(2,1)}, u32[]{:S(2)}) copy-start(bf16[8,128,128]{2,1,0:T(8,128)(2,1)} %z_ref.1) | copy-start | bytes 786436
  419.2 83.3 %all-gather.11.cloned.1.call-start = ((), (), s32[]{:S(2)}) async-start(), calls=%async_computation.3 | async-start | bytes 2228224 | tf_op jit(solution)/shard_map/all_gather | solution.py:620
  468.2 44.3 %copy-start.9 = (bf16[8,128,128]{2,1,0:T(8,128)(2,1)S(1)}, bf16[8,128,128]{2,1,0:T(8,128)(2,1)}, u32[]{:S(2)}) copy-start(bf16[8,128,128]{2,1,0:T(8,128)(2,1)} %get-tuple-element.34) | copy-start | bytes 786436
  513.4 126.5 %copy-start.3 = (bf16[16,4,32,256]{3,2,1,0:T(8,128)(2,1)S(1)}, bf16[16,4,32,256]{3,2,1,0:T(8,128)(2,1)}, u32[]{:S(2)}) copy-start(bf16[16,4,32,256]{3,2,1,0:T(8,128)(2,1)} %get-tuple-element.33) | copy-start | bytes 3145732
  641.7 2.5 copy-start.7
Sparse Core Ops, SparseCore 0:
  112.3 47.4 all-gather.4
  161.4 35.3 all-gather.6
  419.3 44.6 all-gather.8
  465.5 36.8 all-gather.10

commit v5 on v4

--- a/solution.py
+++ b/solution.py
@@ -238,31 +238,77 @@
     )(*m_arrays, masks['seq'], bias_t, masks['res'][:half], masks['res_row'][:half], *weights)
 
 
-def late_columns_kernel(heads, n_dev, late_ref, cmask_ref, mrow_ref, m_ref, cw_ref, cwo_ref, win_ref, wtr_ref, wopm_ref,
-                        o_ref, ab_ref, mback_ref, cproj, cgated, sends, recvs, own_sem):
+def late_columns_kernel(heads, n_dev, late_ref, cmask_ref, mrow_ref, m_ref, ab_early_ref, cw_ref, cwo_ref, win_ref, wtr_ref, wopm_ref,
+                        o_ref, ab_ref, mback_ref, b_ref, cproj, cgated, sends, recvs, own_sem, b_sem, *ring_sems):
     me = lax.axis_index(GROUP_AXIS)
     half = late_ref.shape[2]
     n_seq = late_ref.shape[1] * late_ref.shape[3]
     entry_barrier(n_dev, me)
+    n_opm = ab_early_ref.shape[1] // 2
+    b_own = ab_early_ref.at[:, pl.ds(n_opm, n_opm)]
+    ring = ChipRing(n_dev, me, b_own, b_ref, *ring_sems)
+    b_local = pltpu.make_async_copy(b_own, b_ref.at[me], b_sem)
+    ring.send(1)
+    b_local.start()
     copy = lambda d, slot: peer_copy(m_ref.at[d], mback_ref.at[slot], sends.at[d], recvs.at[slot], d)
     own = pltpu.make_async_copy(m_ref.at[me], mback_ref.at[me], own_sem)
     own.start()
-    for_peers(n_dev, me, lambda d: copy(d, me).start())
-
-    def residue(r, carry):
+
+    def residue(r):
         x = late_ref[:, :, r].astype(F32).reshape(n_dev * n_seq, -1)
         x, ab = column_residue(heads, x, cproj, cgated, cmask_ref.at[r], mrow_ref[r], cw_ref, cwo_ref, win_ref, wtr_ref, wopm_ref)
         o_ref[:, r] = x.reshape(n_dev, n_seq, -1)
         ab_ref[r] = ab
+
+    share = -(-(n_dev - 1) // half)
+
+    def step(r, carry):
+        hop = r + 1
+
+        def send_m(k, inner):
+            @pl.when(k < n_dev)
+            def _():
+                d = lax.rem(me + k, n_dev)
+                copy(d, me).start()
+            return inner
+
+        lax.fori_loop(1 + r * share, 1 + (r + 1) * share, send_m, 0)
+        residue(r)
+
+        @pl.when(hop <= ring.right_hops)
+        def _():
+            ring.receive_from(-hop)
+
+        @pl.when(hop <= ring.left_hops)
+        def _():
+            ring.receive_from(hop)
+
+        @pl.when(hop + 1 <= ring.right_hops)
+        def _():
+            ring.right(hop + 1).start()
+
+        @pl.when(hop + 1 <= ring.left_hops)
+        def _():
+            ring.left(hop + 1).start()
+
         return carry
 
-    lax.fori_loop(0, half, residue, 0)
+    lax.fori_loop(0, half, step, 0)
+    for hop in range(half + 1, ring.right_hops + 1):
+        ring.receive(hop)
+        ring.send(hop + 1)
     own.wait()
+    b_local.wait()
     for_peers(n_dev, me, lambda d: copy(d, d).wait_recv())
     for_peers(n_dev, me, lambda d: copy(d, me).wait_send())
-
-
-def late_columns(late, m_half, masks, stacked, layer, heads):
+    ring.receive_mate(0)
+    for k in range(1, ring.right_hops + 1):
+        for away in ring.arrivals(k):
+            ring.receive_mate(away)
+    ring.drain()
+
+
+def late_columns(late, m_half, ab_early, masks, stacked, layer, heads):
     n_dev, n_blocks, half, block, dim = late.shape
     seq_all = n_dev * n_blocks * block
     weights = [stacked[k] for k in ('col_qkvg', 'col_out', 'mtr_in', 'mtr_out', 'opm_proj')]
@@ -271,15 +317,16 @@
     return pl.pallas_call(
         functools.partial(late_columns_kernel, heads, n_dev),
         grid=(1,),
-        in_specs=[VMEM_SPEC] * 3 + [ANY_SPEC] + [layer_of(w, layer) for w in weights],
-        out_specs=[VMEM_SPEC, VMEM_SPEC, ANY_SPEC],
-        out_shape=[jax.ShapeDtypeStruct(m_half.shape, BF16), jax.ShapeDtypeStruct((half, n_opm, seq_all), BF16), jax.ShapeDtypeStruct(m_half.shape, BF16)],
+        in_specs=[VMEM_SPEC] * 3 + [ANY_SPEC] * 2 + [layer_of(w, layer) for w in weights],
+        out_specs=[VMEM_SPEC, VMEM_SPEC, ANY_SPEC, ANY_SPEC],
+        out_shape=[jax.ShapeDtypeStruct(m_half.shape, BF16), jax.ShapeDtypeStruct((half, n_opm, seq_all), BF16), jax.ShapeDtypeStruct(m_half.shape, BF16),
+                   jax.ShapeDtypeStruct((n_dev, half, n_opm // 2, seq_all), BF16)],
         scratch_shapes=[pltpu.VMEM((4 * width, seq_all), BF16), pltpu.VMEM((width, seq_all), BF16),
-                        pltpu.SemaphoreType.DMA((n_dev,)), pltpu.SemaphoreType.DMA((n_dev,)), pltpu.SemaphoreType.DMA],
+                        pltpu.SemaphoreType.DMA((n_dev,)), pltpu.SemaphoreType.DMA((n_dev,)), pltpu.SemaphoreType.DMA, pltpu.SemaphoreType.DMA] + ring_semaphores(n_dev),
         compiler_params=pltpu.CompilerParams(collective_id=3 * layer + 1, has_side_effects=True),
         cost_estimate=pl.CostEstimate(flops=20_000_000_000, bytes_accessed=12_000_000, transcendentals=8_000_000),
         name='late_columns',
-    )(late, masks['res'][half:], masks['res_row'][half:], m_half, *weights)
+    )(late, masks['res'][half:], masks['res_row'][half:], m_half, ab_early, *weights)
 
 
 class Exchange:
@@ -313,6 +360,71 @@
             lax.fori_loop(1, self.n_dev, wait, 0)
 
         return finish
+
+
+class ChipRing:
+    def __init__(self, n_dev, me, own, slots, recvs, rights, lefts, partners):
+        self.n_dev, self.me, self.own, self.slots = n_dev, me, own, slots
+        self.recvs, self.rights, self.lefts, self.partners = recvs, rights, lefts, partners
+        chips = n_dev // 2
+        self.right_hops, self.left_hops = chips // 2, (chips - 1) // 2
+        self.partner = me + 1 - 2 * lax.rem(me, 2)
+
+    def device(self, chips_away):
+        return lax.rem(self.me + 2 * chips_away + self.n_dev, self.n_dev)
+
+    def mate(self, src):
+        return src + 1 - 2 * lax.rem(src, 2)
+
+    def copy(self, src, first, send_sem, to):
+        return peer_copy(self.own if first else self.slots.at[src], self.slots.at[src], send_sem, self.recvs.at[src], to)
+
+    def right(self, hop):
+        return self.copy(self.device(1 - hop), isinstance(hop, int) and hop == 1, self.rights.at[hop], self.device(1))
+
+    def left(self, hop):
+        return self.copy(self.device(hop - 1), isinstance(hop, int) and hop == 1, self.lefts.at[hop], self.device(-1))
+
+    def hand(self, src, first=False):
+        return self.copy(src, first, self.partners.at[src], self.partner)
+
+    def send(self, hop):
+        if hop == 1:
+            self.hand(self.me, True).start()
+        if hop <= self.right_hops:
+            self.right(hop).start()
+        if hop <= self.left_hops:
+            self.left(hop).start()
+
+    def arrivals(self, hop):
+        return ([-hop] if hop <= self.right_hops else []) + ([hop] if hop <= self.left_hops else [])
+
+    def receive(self, hop):
+        for away in self.arrivals(hop):
+            self.receive_from(away)
+
+    def receive_from(self, away):
+        src = self.device(away)
+        self.copy(src, False, self.rights.at[0], self.partner).wait_recv()
+        self.hand(src).start()
+
+    def receive_mate(self, away):
+        src = self.mate(self.device(away))
+        self.copy(src, False, self.rights.at[0], self.partner).wait_recv()
+        return src
+
+    def drain(self):
+        self.hand(self.me, True).wait_send()
+        for hop in range(1, self.right_hops + 1):
+            self.right(hop).wait_send()
+            if hop <= self.left_hops:
+                self.left(hop).wait_send()
+            for away in self.arrivals(hop):
+                self.hand(self.device(away)).wait_send()
+
+
+def ring_semaphores(n_dev):
+    return [pltpu.SemaphoreType.DMA((n_dev,)) for k in range(4)]
 
 
 def entry_barrier(n_dev, me):
@@ -560,43 +672,58 @@
     return jnp.swapaxes(full, 1, 2).astype(F32) * LOG2E
 
 
-def residues_inside(right_ref, stage, store):
-    n_rows, n_e, length = right_ref.shape
-    pitch = stage.shape[1] // n_e
-
-    def one(j, carry):
-        tile = right_ref[j].astype(F32)
-        for part in range(length // LANES):
-            for lo in range(0, n_e, 8):
-                stage[part, pl.ds(lo * pitch + j, 8, stride=pitch), :] = tile[lo:lo + 8, part * LANES:(part + 1) * LANES]
-        return carry
-
-    lax.fori_loop(0, n_rows, one, 0)
-    for e in range(n_e):
-        for part in range(length // LANES):
-            store(e, part, stage[part, e * pitch:e * pitch + n_rows, :].astype(BF16))
-
-
-def outer_layout_kernel(right_ref, o_ref, stage):
-    def store(e, part, value):
-        o_ref[e, :, part * LANES:(part + 1) * LANES] = value
-    residues_inside(right_ref, stage, store)
-
-
-def outer_product_kernel(early_ref, late_ref, right_ref, right_late_ref, w_ref, o_ref, stage, left, rows, flat):
+def outer_product_kernel(n_dev, early_ref, late_ref, b_ref, w_ref, o_ref, stage, left, rows, flat, slots, *ring_sems):
     half = early_ref.shape[0]
-    n_half = right_ref.shape[1]
     dim = early_ref.shape[1] // 2
+    length = early_ref.shape[2]
+    n_half = n_dev * half
+    pitch = stage.shape[2] // dim
+    parts = [slice(part * LANES, (part + 1) * LANES) for part in range(length // LANES)]
+    me = lax.axis_index(GROUP_AXIS)
+    entry_barrier(n_dev, me)
+    ring = ChipRing(n_dev, me, late_ref.at[:, pl.ds(dim, dim)], slots, *ring_sems)
+    ring.send(1)
+
+    def spread(k, source, src):
+        for r in range(half):
+            tile = source(r).astype(F32)
+            for part, lanes in enumerate(parts):
+                for lo in range(0, dim, 8):
+                    stage[k, part, pl.ds(lo * pitch + src * half + r, 8, stride=pitch), :] = tile[lo:lo + 8, lanes]
+
+    def collect(k):
+        for e in range(dim):
+            for part, lanes in enumerate(parts):
+                rows[e, k * n_half:(k + 1) * n_half, lanes] = stage[k, part, e * pitch:e * pitch + n_half, :].astype(BF16)
+
+    def spread_early(lo, hi):
+        def one(src, carry):
+            spread(0, lambda r: b_ref[src, r], src)
+            return carry
+        lax.fori_loop(lo, hi, one, 0)
+
+    def spread_late(src):
+        spread(1, lambda r: slots[src, r], src)
+
+    hops = ring.right_hops
+    shares = [n_dev * k // hops for k in range(hops + 1)]
+    spread(1, lambda r: late_ref[r, dim:2 * dim, :], me)
     for k, ab_ref in enumerate((early_ref, late_ref)):
         for r in range(half):
             left[(k * half + r) * dim:(k * half + r + 1) * dim, :] = ab_ref[r, 0:dim, :]
-
-    def store(e, part, value):
-        rows[e, n_half:2 * n_half, part * LANES:(part + 1) * LANES] = value
-
-    residues_inside(right_late_ref, stage, store)
-    for e in range(dim):
-        rows[e, 0:n_half, :] = right_ref[e]
+    for hop in range(1, hops + 1):
+        spread_early(shares[hop - 1], shares[hop])
+        if hop == hops:
+            collect(0)
+        ring.receive(hop)
+        ring.send(hop + 1)
+        for away in ([0] if hop == 1 else ring.arrivals(hop - 1)):
+            spread_late(ring.receive_mate(away))
+        for away in ring.arrivals(hop):
+            spread_late(ring.device(away))
+    for away in ring.arrivals(hops):
+        spread_late(ring.receive_mate(away))
+    collect(1)
 
     def one(step, carry):
         some = [step * 4 + k for k in range(4)]
@@ -609,34 +736,27 @@
     lax.fori_loop(0, dim // 4, one, 0)
     for i in range(2 * half):
         o_ref[i] = jnp.dot(w_ref[...], flat[i], preferred_element_type=F32).T
-
-
-def outer_update(ab_halves, overlap, stacked, layer, n_dev):
+    ring.drain()
+
+
+def outer_update(ab_halves, b_early, overlap, stacked, layer, n_dev):
     half, n_ab, seq_all = ab_halves[0].shape
     opm_dim = n_ab // 2
     n_half = n_dev * half
     length = 2 * n_half
     dim = stacked['opm_w'].shape[1]
-    gathered = [lax.all_gather(ab[:, opm_dim:], GROUP_AXIS, axis=0, tiled=True) for ab in ab_halves]
-    stage = pltpu.VMEM((seq_all // LANES, opm_dim * (n_half + 8), LANES), F32)
-    early_rows = pl.pallas_call(
-        outer_layout_kernel,
-        in_specs=[VMEM_SPEC], out_specs=VMEM_SPEC,
-        out_shape=jax.ShapeDtypeStruct((opm_dim, n_half, seq_all), BF16),
-        scratch_shapes=[stage],
-        cost_estimate=pl.CostEstimate(flops=2_000_000_000, bytes_accessed=4_000_000, transcendentals=0),
-        name='outer_layout',
-    )(gathered[0])
     update = pl.pallas_call(
-        outer_product_kernel,
+        functools.partial(outer_product_kernel, n_dev),
         grid=(1,),
-        in_specs=[VMEM_SPEC] * 4 + [layer_of(stacked['opm_w'], layer)], out_specs=VMEM_SPEC,
+        in_specs=[VMEM_SPEC] * 3 + [layer_of(stacked['opm_w'], layer)], out_specs=VMEM_SPEC,
         out_shape=jax.ShapeDtypeStruct((2 * half, length, dim), F32),
-        scratch_shapes=[stage, pltpu.VMEM((2 * half * opm_dim, seq_all), BF16), pltpu.VMEM((opm_dim, length, seq_all), BF16),
-                        pltpu.VMEM((2 * half, opm_dim * opm_dim, length), BF16)],
+        scratch_shapes=[pltpu.VMEM((2, seq_all // LANES, opm_dim * (n_half + 8), LANES), F32),
+                        pltpu.VMEM((2 * half * opm_dim, seq_all), BF16), pltpu.VMEM((opm_dim, length, seq_all), BF16),
+                        pltpu.VMEM((2 * half, opm_dim * opm_dim, length), BF16), pltpu.VMEM(b_early.shape, BF16)] + ring_semaphores(n_dev),
+        compiler_params=pltpu.CompilerParams(collective_id=3 * stacked['opm_w'].shape[0] + 1 + layer, has_side_effects=True),
         cost_estimate=pl.CostEstimate(flops=4_000_000_000, bytes_accessed=6_000_000, transcendentals=0),
         name='outer_product',
-    )(ab_halves[0], ab_halves[1], early_rows, gathered[1], stacked['opm_w'])
+    )(ab_halves[0], ab_halves[1], b_early, stacked['opm_w'])
     update = update.reshape(2 * half, 2, n_dev, half, dim)
     update = jnp.swapaxes(update, 1, 2).reshape(2 * half, length, dim)
     return update / (1e-3 + overlap)[:, :, None]
@@ -678,8 +798,8 @@
 def evoformer_block(m_arrays, pair_loc, bias_t, masks, stacked, layer, with_bias):
     heads = masks['msa_heads']
     early, ab_early, late = rows_and_columns(m_arrays, bias_t, masks, stacked, layer, heads)
-    late, ab_late, m_early = late_columns(late, early, masks, stacked, layer, heads)
-    pair_loc = residual(pair_loc, outer_update((ab_early, ab_late), masks['overlap'], stacked, layer, masks['n_dev']))
+    late, ab_late, m_early, b_early = late_columns(late, early, ab_early, masks, stacked, layer, heads)
+    pair_loc = residual(pair_loc, outer_update((ab_early, ab_late), b_early, masks['overlap'], stacked, layer, masks['n_dev']))
     pair_loc, m_late, bias_t = pair_stack(pair_loc, late, masks, stacked, layer, with_bias)
     return (m_early, m_late), pair_loc, bias_t
 

time: 660 us -> 618 us (0.936)
  waiting for transfers between devices: 69 us -> 0 us
  Pallas kernels: 532 us -> 577 us
  between operations: 14.5 us -> 1.31 us
    all_gather x4 -> x0, waiting for transfers between devices: 68.8 us -> none  [outer_update(): lax.all_gather(ab[:, opm_dim:], GROUP_AXIS, axis=0, tiled=True)]
    pallas_call x4 -> x2, Pallas kernels: 26.8 us -> 62.9 us  [outer_update(): pl.pallas_call(functools.partial(outer_product_kernel, n_dev), grid=(1,),...]
    pallas_call x2, Pallas kernels: 78 us -> 93.7 us  [late_columns(): pl.pallas_call(functools.partial(late_columns_kernel, heads, n_dev), grid...]
    pallas_call x2, Pallas kernels: 261 us -> 253 us  [pair_stack(): pl.pallas_call(functools.partial(pair_kernel, n_dev, with_bias), grid=(1,...]
  transfers between devices with their start and end apart: 4 -> 0, of which waited for: 3 -> 0; matrix products, arithmetic and copies ran while one was open for 2% -> 0% of each run, Pallas kernels for 13% -> 0%
where the time goes in v5:
time: 618 us; the launch traced here: 608 us
  Pallas kernels  577 us (93%)
  local copies, waits for them, and re-layouts  23.4 us (4%)
    pallas_call x2, Pallas kernels, pair_stack(): pl.pallas_call(functools.partial(pair_kernel, n_dev, with_bias), grid=(1,...  253 us
    pallas_call x2, Pallas kernels, rows_and_columns(): pl.pallas_call(functools.partial(rows_and_columns_kernel, heads, n_dev, f...  145 us
    pallas_call x2, Pallas kernels, late_columns(): pl.pallas_call(functools.partial(late_columns_kernel, heads, n_dev), grid...  93.7 us
    pallas_call x2, Pallas kernels, outer_update(): pl.pallas_call(functools.partial(outer_product_kernel, n_dev), grid=(1,),...  62.9 us
    pallas_call x1, Pallas kernels, first_gather(): pl.pallas_call(functools.partial(first_gather_kernel, n_dev), grid=(1,),...  23.3 us

profile of v5, /device:TPU:21, one launch (start us, length us, event | category | flops | bytes accessed | tf_op | source)
XLA Modules:
  0.0 607.6 jit_solution(9646263158303429249)
XLA Ops:
  0.6 0.8 fusion.3
  1.4 0.8 fusion.4
  2.2 0.6 pad_maximum_fusion.masks_ref
  2.8 23.3 %first_gather.1 = (f32[8,128,128]{2,1,0:T(8,128)}, bf16[16,40,128]{2,1,0:T(8,128)(2,1)}) custom-call(bf16[8,128,128]{2,1,0:T(8,128)(2,1)} %z_ref.1, bf16[2,8,128]{2,1,0:T(8,128)(2,1)} %bitcast.72, bf16[40,128]{1,0:T(8,128)(2,1)} %pad_maximum_fusion.masks_ref), custom_call_target="tpu_custom_call" | custom-call | flops 1000000000 | bytes 2000000 | tf_op jit(solution)/shard_map/first_gather/pallas_call | solution.py:785
  26.1 0.0 copy-start.1
  26.1 1.0 slice.44
  27.1 0.1 constant_dynamic-slice_fusion.1
  27.3 0.1 copy.73
  27.4 1.4 broadcast_in_dim.11.refs_3_.refs_4_
  28.7 0.6 copy.59.refs_4_.refs_5_
  29.3 1.3 copy.58
  30.6 1.9 broadcast_in_dim.10.refs_1_.refs_2_
  32.5 1.3 copy.57
  33.9 69.7 %rows_and_columns.2 = (bf16[16,4,32,256]{3,2,1,0:T(8,128)(2,1)}, bf16[4,64,512]{2,1,0:T(8,128)(2,1)}, bf16[16,4,4,8,256]{4,3,2,1,0:T(8,128)(2,1)}) custom-call(bf16[32,128,256]{2,1,0:T(8,128)(2,1)} %refs_0_.1, f32[32,128,128]{2,1,0:T(8,128)} %broadcast_in_dim.10.refs_1_.refs_2_, f32[8,128,128]{2,1,0:T(8,128)} %get-tuple-element.23.refs_2_, ...), custom_call_target="tpu_custom_call" | custom-call | flops 20000000000 | bytes 12000000 | tf_op jit(solution)/shard_map/rows_and_columns/pallas_call | solution.py:227
  103.6 1.3 broadcast_in_dim.12.cmask_ref
  104.9 0.6 slice.39.mrow_ref
  105.5 46.9 %late_columns.2 = (bf16[16,4,32,256]{3,2,1,0:T(8,128)(2,1)}, bf16[4,64,512]{2,1,0:T(8,128)(2,1)}, bf16[16,4,32,256]{3,2,1,0:T(8,128)(2,1)}, bf16[16,4,32,512]{3,2,1,0:T(8,128)(2,1)}) custom-call(bf16[16,4,4,8,256]{4,3,2,1,0:T(8,128)(2,1)} %get-tuple-element.25.late_ref, f32[4,512,128]{2,1,0:T(8,128)} %broadcast_in_dim.12.cmask_ref, ...), custom_call_target="tpu_custom_call" | custom-call | flops 20000000000 | bytes 12000000 | tf_op jit(solution)/shard_map/late_columns/pallas_call | solution.py:317
  152.4 0.0 copy-done.4
  152.4 0.2 copy.60
  152.6 1.0 copy.61.w_ref
  153.6 32.1 %outer_product.2 = f32[8,128,128]{2,1,0:T(8,128)} custom-call(bf16[4,64,512]{2,1,0:T(8,128)(2,1)} %get-tuple-element.27.ab_early_ref.early_ref, bf16[4,64,512]{2,1,0:T(8,128)(2,1)} %get-tuple-element.29.late_ref, bf16[16,4,32,512]{3,2,1,0:T(8,128)(2,1)} %get-tuple-element.30.b_ref, bf16[2,128,1024]{2,1,0:T(8,128)(2,1)} %copy.61.w_ref), custom_call_target="tpu_custom_call" | custom-call | flops 4000000000 | bytes 6000000 | tf_op jit(solution)/shard_map/outer_product/pallas_call | solution.py:748
  185.7 1.1 copy.62
  186.9 0.0 slice-start
  186.9 0.3 convolution_add_fusion
  187.1 0.0 copy-done.8
  187.2 0.9 add_convert_fusion.1.refs_0_
  188.1 0.0 copy-start.6
  188.1 0.1 constant_dynamic-slice_fusion
  188.2 0.1 copy.74
  188.3 1.1 broadcast_in_dim.14.refs_3_
  189.3 1.0 broadcast_in_dim.13.refs_2_
  190.3 0.8 copy.75
  191.2 0.8 copy.76
  192.0 0.8 copy.66
  192.9 0.8 copy.67
  193.7 0.6 pad.7.refs_12_
  194.3 0.6 pad.8.refs_15_
  194.9 131.1 %pair_stack.2 = (bf16[8,128,128]{2,1,0:T(8,128)(2,1)}, bf16[16,4,32,256]{3,2,1,0:T(8,128)(2,1)}, f32[8,128,128]{2,1,0:T(8,128)}) custom-call(bf16[8,128,128]{2,1,0:T(8,128)(2,1)} %add_convert_fusion.1.refs_0_, f32[1,1024]{1,0:T(1,128)} %bitcast.64, f32[8,128,128]{2,1,0:T(8,128)} %broadcast_in_dim.13.refs_2_, f32[8,128,128]{2,1,0:T(8,128)} %broadcast_in_dim.14.refs_3_, ...), custom_call_target="tpu_custom_call" | custom-call | flops 4000000000 | bytes 16000000 | tf_op jit(solution)/shard_map/pair_stack/pallas_call | solution.py:653
  326.0 74.8 %rows_and_columns.3 = (bf16[16,4,32,256]{3,2,1,0:T(8,128)(2,1)}, bf16[4,64,512]{2,1,0:T(8,128)(2,1)}, bf16[16,4,4,8,256]{4,3,2,1,0:T(8,128)(2,1)}) custom-call(bf16[16,4,32,256]{3,2,1,0:T(8,128)(2,1)} %get-tuple-element.28.refs_0_, bf16[16,4,32,256]{3,2,1,0:T(8,128)(2,1)} %get-tuple-element.32.refs_1_, f32[32,128,128]{2,1,0:T(8,128)} %broadcast_in_dim.10.refs_1_.refs_2_, ...), custom_call_target="tpu_custom_call" | custom-call | flops 20000000000 | bytes 12000000 | tf_op jit(solution)/shard_map/rows_and_columns/pallas_call | solution.py:227
  400.9 46.8 %late_columns.3 = (bf16[16,4,32,256]{3,2,1,0:T(8,128)(2,1)}, bf16[4,64,512]{2,1,0:T(8,128)(2,1)}, bf16[16,4,32,256]{3,2,1,0:T(8,128)(2,1)}, bf16[16,4,32,512]{3,2,1,0:T(8,128)(2,1)}) custom-call(bf16[16,4,4,8,256]{4,3,2,1,0:T(8,128)(2,1)} %get-tuple-element.34.late_ref, f32[4,512,128]{2,1,0:T(8,128)} %broadcast_in_dim.12.cmask_ref, ...), custom_call_target="tpu_custom_call" | custom-call | flops 20000000000 | bytes 12000000 | tf_op jit(solution)/shard_map/late_columns/pallas_call | solution.py:317
  447.7 30.8 %outer_product.3 = f32[8,128,128]{2,1,0:T(8,128)} custom-call(bf16[4,64,512]{2,1,0:T(8,128)(2,1)} %get-tuple-element.36.ab_early_ref.early_ref, bf16[4,64,512]{2,1,0:T(8,128)(2,1)} %get-tuple-element.39.late_ref, bf16[16,4,32,512]{3,2,1,0:T(8,128)(2,1)} %get-tuple-element.40.b_ref, bf16[2,128,1024]{2,1,0:T(8,128)(2,1)} %copy.61.w_ref), custom_call_target="tpu_custom_call" | custom-call | flops 4000000000 | bytes 6000000 | tf_op jit(solution)/shard_map/outer_product/pallas_call | solution.py:748
  478.5 1.1 copy.70
  479.6 0.9 add_convert_fusion.refs_0_
  480.6 121.7 %pair_stack.3 = (bf16[8,128,128]{2,1,0:T(8,128)(2,1)}, bf16[16,4,32,256]{3,2,1,0:T(8,128)(2,1)}, f32[8,128,128]{2,1,0:T(8,128)}) custom-call(bf16[8,128,128]{2,1,0:T(8,128)(2,1)} %add_convert_fusion.refs_0_, f32[1,1024]{1,0:T(1,128)} %bitcast.65, f32[8,128,128]{2,1,0:T(8,128)} %broadcast_in_dim.13.refs_2_, f32[8,128,128]{2,1,0:T(8,128)} %broadcast_in_dim.14.refs_3_, ...), custom_call_target="tpu_custom_call" | custom-call | flops 4000000000 | bytes 16000000 | tf_op jit(solution)/shard_map/pair_stack/pallas_call | solution.py:653
  602.3 1.4 maximum_bitcast_fusion
  603.7 0.3 copy.71
  604.0 2.5 copy.72
  606.5 0.7 copy.78
  (29 shorter events, 0.1 us)
Async XLA Ops:
  2.2 187.1 %copy-start.10 = (f32[8,128]{1,0:T(8,128)}, f32[8,128]{1,0:T(8,128)S(1)}, u32[]{:S(2)}) copy-start(f32[8,128]{1,0:T(8,128)S(1)} %get-tuple-element.53) | copy-start | bytes 12292
  26.1 3.2 copy-start.1
  29.3 3.2 copy-start.2
  105.5 46.9 %copy-start.4 = (bf16[2,1024,128]{2,1,0:T(8,128)(2,1)S(1)}, bf16[2,1024,128]{2,1,0:T(8,128)(2,1)}, u32[]{:S(2)}) copy-start(bf16[2,1024,128]{2,1,0:T(8,128)(2,1)} %param.37) | copy-start | bytes 1572868
  153.6 33.2 %copy-start = (bf16[16,40,128]{2,1,0:T(8,128)(2,1)S(1)}, bf16[16,40,128]{2,1,0:T(8,128)(2,1)}, u32[]{:S(2)}) copy-start(bf16[16,40,128]{2,1,0:T(8,128)(2,1)} %get-tuple-element.24) | copy-start | bytes 491524
  153.6 33.5 %copy-start.8 = (bf16[8,128,128]{2,1,0:T(8,128)(2,1)S(1)}, bf16[8,128,128]{2,1,0:T(8,128)(2,1)}, u32[]{:S(2)}) copy-start(bf16[8,128,128]{2,1,0:T(8,128)(2,1)} %z_ref.1) | copy-start | bytes 786436
  186.9 3.5 slice-start
  187.2 4.0 slice-start.1
  188.1 3.9 copy-start.5
  188.1 4.7 copy-start.6
  188.3 5.4 copy-start.11
  188.3 6.0 copy-start.12
  447.7 32.0 %copy-start.9 = (bf16[8,128,128]{2,1,0:T(8,128)(2,1)S(1)}, bf16[8,128,128]{2,1,0:T(8,128)(2,1)}, u32[]{:S(2)}) copy-start(bf16[8,128,128]{2,1,0:T(8,128)(2,1)} %get-tuple-element.38) | copy-start | bytes 786436
  480.6 121.7 %copy-start.3 = (bf16[16,4,32,256]{3,2,1,0:T(8,128)(2,1)S(1)}, bf16[16,4,32,256]{3,2,1,0:T(8,128)(2,1)}, u32[]{:S(2)}) copy-start(bf16[16,4,32,256]{3,2,1,0:T(8,128)(2,1)} %get-tuple-element.37) | copy-start | bytes 3145732
  604.0 2.5 copy-start.7

commit v6 on v5

--- a/solution.py
+++ b/solution.py
@@ -481,7 +481,7 @@
                     stage[pl.ds(d * n_chan * n_res + i, n_chan, stride=n_res), :] = tile
             ab_send[turn, :, part] = stage[...].reshape(n_dev, n_chan, n_res, length).astype(BF16)
         arrived = exchange.start(ab_send.at[turn], ab_recv.at[turn])
-        m_steps(3 + 2 * turn, 4 + 2 * turn)
+        m_steps(3 + 3 * turn, 5 + 3 * turn)
         gate[...] = jax.nn.sigmoid(jnp.dot(x_norm, p_ref[:, 4 * tri:], preferred_element_type=F32))
         arrived()
         for c in range(n_chan):
@@ -490,7 +490,7 @@
             product = lax.dot_general(left, right, contract, preferred_element_type=F32)
             x_send[turn, :, c] = product.reshape(n_dev, n_res, length)
         arrived = exchange.start(x_send.at[turn], x_recv.at[turn])
-        m_steps(4 + 2 * turn, 5 + 2 * turn)
+        m_steps(5 + 3 * turn, 6 + 3 * turn)
         arrived()
         values = x_recv[turn].reshape(tri, n_res, length)
         centered = values - jnp.mean(values, axis=0, keepdims=True)
@@ -536,7 +536,7 @@
     local_bias(normed_tokens(), tas_b, bias_send.at[0])
     arrived = exchange.start(bias_send.at[0], bias_recv.at[0], broadcast=True)
     arrived()
-    m_steps(7, 10)
+    m_steps(9, 13)
     for h in range(heads):
         bias_t[h] = rows_of(bias_recv.at[0], h).astype(F32).T * LOG2E
     attention(zbuf, tas_w, tas_out, start_ref, heads)
@@ -548,13 +548,12 @@
     for h in range(heads):
         bias_t[h] = rows_of(bias_recv.at[1], h).astype(F32) * LOG2E
     arrived()
-    m_steps(10, 13)
+    m_steps(13, n_dev)
     for j in range(n_res):
         tbuf[j] = rows_of(z_recv, j)
     attention(tbuf, tae_w, tae_out, end_ref, heads)
     z_send[1] = swap_blocks(tbuf)
     arrived = exchange.start(z_send.at[1], zb_recv)
-    m_steps(13, n_dev)
     arrived()
     for i in range(n_res):
         zbuf[i] = rows_of(zb_recv, i)

time: 618 us -> 621 us (level)
  the two profiles are of different devices: /device:TPU:21 before, /device:TPU:29 now
where the time goes in v6:
time: 621 us; the launch traced here: 613 us
  Pallas kernels  582 us (94%)
  local copies, waits for them, and re-layouts  23.4 us (4%)
    pallas_call x2, Pallas kernels, pair_stack(): pl.pallas_call(functools.partial(pair_kernel, n_dev, with_bias), grid=(1,...  259 us
    pallas_call x2, Pallas kernels, rows_and_columns(): pl.pallas_call(functools.partial(rows_and_columns_kernel, heads, n_dev, f...  143 us
    pallas_call x2, Pallas kernels, late_columns(): pl.pallas_call(functools.partial(late_columns_kernel, heads, n_dev), grid...  94.1 us
    pallas_call x2, Pallas kernels, outer_update(): pl.pallas_call(functools.partial(outer_product_kernel, n_dev), grid=(1,),...  63.5 us
    pallas_call x1, Pallas kernels, first_gather(): pl.pallas_call(functools.partial(first_gather_kernel, n_dev), grid=(1,),...  22.4 us

profile of v6, /device:TPU:29, one launch (start us, length us, event | category | flops | bytes accessed | tf_op | source)
XLA Modules:
  0.0 612.9 jit_solution(13276901154221490991)
XLA Ops:
  0.6 0.8 fusion.3
  1.4 0.8 fusion.4
  2.2 0.6 pad_maximum_fusion.masks_ref
  2.8 22.4 %first_gather.1 = (f32[8,128,128]{2,1,0:T(8,128)}, bf16[16,40,128]{2,1,0:T(8,128)(2,1)}) custom-call(bf16[8,128,128]{2,1,0:T(8,128)(2,1)} %z_ref.1, bf16[2,8,128]{2,1,0:T(8,128)(2,1)} %bitcast.72, bf16[40,128]{1,0:T(8,128)(2,1)} %pad_maximum_fusion.masks_ref), custom_call_target="tpu_custom_call" | custom-call | flops 1000000000 | bytes 2000000 | tf_op jit(solution)/shard_map/first_gather/pallas_call | solution.py:784
  25.3 0.0 copy-start.1
  25.3 1.0 slice.44
  26.3 0.1 constant_dynamic-slice_fusion.1
  26.4 0.1 copy.73
  26.5 1.4 broadcast_in_dim.11.refs_3_.refs_4_
  27.9 0.6 copy.59.refs_4_.refs_5_
  28.5 1.3 copy.58
  29.8 1.9 broadcast_in_dim.10.refs_1_.refs_2_
  31.7 1.3 copy.57
  33.0 69.1 %rows_and_columns.2 = (bf16[16,4,32,256]{3,2,1,0:T(8,128)(2,1)}, bf16[4,64,512]{2,1,0:T(8,128)(2,1)}, bf16[16,4,4,8,256]{4,3,2,1,0:T(8,128)(2,1)}) custom-call(bf16[32,128,256]{2,1,0:T(8,128)(2,1)} %refs_0_.1, f32[32,128,128]{2,1,0:T(8,128)} %broadcast_in_dim.10.refs_1_.refs_2_, f32[8,128,128]{2,1,0:T(8,128)} %get-tuple-element.23.refs_2_, ...), custom_call_target="tpu_custom_call" | custom-call | flops 20000000000 | bytes 12000000 | tf_op jit(solution)/shard_map/rows_and_columns/pallas_call | solution.py:227
  102.1 1.3 broadcast_in_dim.12.cmask_ref
  103.4 0.6 slice.39.mrow_ref
  104.0 48.1 %late_columns.2 = (bf16[16,4,32,256]{3,2,1,0:T(8,128)(2,1)}, bf16[4,64,512]{2,1,0:T(8,128)(2,1)}, bf16[16,4,32,256]{3,2,1,0:T(8,128)(2,1)}, bf16[16,4,32,512]{3,2,1,0:T(8,128)(2,1)}) custom-call(bf16[16,4,4,8,256]{4,3,2,1,0:T(8,128)(2,1)} %get-tuple-element.25.late_ref, f32[4,512,128]{2,1,0:T(8,128)} %broadcast_in_dim.12.cmask_ref, ...), custom_call_target="tpu_custom_call" | custom-call | flops 20000000000 | bytes 12000000 | tf_op jit(solution)/shard_map/late_columns/pallas_call | solution.py:317
  152.1 0.2 copy.60
  152.3 1.0 copy.61.w_ref
  153.4 31.0 %outer_product.2 = f32[8,128,128]{2,1,0:T(8,128)} custom-call(bf16[4,64,512]{2,1,0:T(8,128)(2,1)} %get-tuple-element.27.ab_early_ref.early_ref, bf16[4,64,512]{2,1,0:T(8,128)(2,1)} %get-tuple-element.29.late_ref, bf16[16,4,32,512]{3,2,1,0:T(8,128)(2,1)} %get-tuple-element.30.b_ref, bf16[2,128,1024]{2,1,0:T(8,128)(2,1)} %copy.61.w_ref), custom_call_target="tpu_custom_call" | custom-call | flops 4000000000 | bytes 6000000 | tf_op jit(solution)/shard_map/outer_product/pallas_call | solution.py:747
  184.4 1.1 copy.62
  185.5 0.0 slice-start
  185.5 0.3 convolution_add_fusion
  185.8 0.9 add_convert_fusion.1.refs_0_
  186.8 0.0 copy-start.6
  186.8 0.1 constant_dynamic-slice_fusion
  186.9 0.1 copy.74
  186.9 1.1 broadcast_in_dim.14.refs_3_
  188.0 1.0 broadcast_in_dim.13.refs_2_
  189.0 0.0 slice-done
  189.0 0.8 copy.75
  189.8 0.8 copy.76
  190.7 0.8 copy.66
  191.5 0.8 copy.67
  192.4 0.6 pad.7.refs_12_
  193.0 0.6 pad.8.refs_15_
  193.6 134.5 %pair_stack.2 = (bf16[8,128,128]{2,1,0:T(8,128)(2,1)}, bf16[16,4,32,256]{3,2,1,0:T(8,128)(2,1)}, f32[8,128,128]{2,1,0:T(8,128)}) custom-call(bf16[8,128,128]{2,1,0:T(8,128)(2,1)} %add_convert_fusion.1.refs_0_, f32[1,1024]{1,0:T(1,128)} %bitcast.64, f32[8,128,128]{2,1,0:T(8,128)} %broadcast_in_dim.13.refs_2_, f32[8,128,128]{2,1,0:T(8,128)} %broadcast_in_dim.14.refs_3_, ...), custom_call_target="tpu_custom_call" | custom-call | flops 4000000000 | bytes 16000000 | tf_op jit(solution)/shard_map/pair_stack/pallas_call | solution.py:652
  328.0 74.0 %rows_and_columns.3 = (bf16[16,4,32,256]{3,2,1,0:T(8,128)(2,1)}, bf16[4,64,512]{2,1,0:T(8,128)(2,1)}, bf16[16,4,4,8,256]{4,3,2,1,0:T(8,128)(2,1)}) custom-call(bf16[16,4,32,256]{3,2,1,0:T(8,128)(2,1)} %get-tuple-element.28.refs_0_, bf16[16,4,32,256]{3,2,1,0:T(8,128)(2,1)} %get-tuple-element.32.refs_1_, f32[32,128,128]{2,1,0:T(8,128)} %broadcast_in_dim.10.refs_1_.refs_2_, ...), custom_call_target="tpu_custom_call" | custom-call | flops 20000000000 | bytes 12000000 | tf_op jit(solution)/shard_map/rows_and_columns/pallas_call | solution.py:227
  402.1 46.0 %late_columns.3 = (bf16[16,4,32,256]{3,2,1,0:T(8,128)(2,1)}, bf16[4,64,512]{2,1,0:T(8,128)(2,1)}, bf16[16,4,32,256]{3,2,1,0:T(8,128)(2,1)}, bf16[16,4,32,512]{3,2,1,0:T(8,128)(2,1)}) custom-call(bf16[16,4,4,8,256]{4,3,2,1,0:T(8,128)(2,1)} %get-tuple-element.34.late_ref, f32[4,512,128]{2,1,0:T(8,128)} %broadcast_in_dim.12.cmask_ref, ...), custom_call_target="tpu_custom_call" | custom-call | flops 20000000000 | bytes 12000000 | tf_op jit(solution)/shard_map/late_columns/pallas_call | solution.py:317
  448.1 32.5 %outer_product.3 = f32[8,128,128]{2,1,0:T(8,128)} custom-call(bf16[4,64,512]{2,1,0:T(8,128)(2,1)} %get-tuple-element.36.ab_early_ref.early_ref, bf16[4,64,512]{2,1,0:T(8,128)(2,1)} %get-tuple-element.39.late_ref, bf16[16,4,32,512]{3,2,1,0:T(8,128)(2,1)} %get-tuple-element.40.b_ref, bf16[2,128,1024]{2,1,0:T(8,128)(2,1)} %copy.61.w_ref), custom_call_target="tpu_custom_call" | custom-call | flops 4000000000 | bytes 6000000 | tf_op jit(solution)/shard_map/outer_product/pallas_call | solution.py:747
  480.6 1.1 copy.70
  481.7 0.0 copy-done.9
  481.8 0.9 add_convert_fusion.refs_0_
  482.7 124.9 %pair_stack.3 = (bf16[8,128,128]{2,1,0:T(8,128)(2,1)}, bf16[16,4,32,256]{3,2,1,0:T(8,128)(2,1)}, f32[8,128,128]{2,1,0:T(8,128)}) custom-call(bf16[8,128,128]{2,1,0:T(8,128)(2,1)} %add_convert_fusion.refs_0_, f32[1,1024]{1,0:T(1,128)} %bitcast.65, f32[8,128,128]{2,1,0:T(8,128)} %broadcast_in_dim.13.refs_2_, f32[8,128,128]{2,1,0:T(8,128)} %broadcast_in_dim.14.refs_3_, ...), custom_call_target="tpu_custom_call" | custom-call | flops 4000000000 | bytes 16000000 | tf_op jit(solution)/shard_map/pair_stack/pallas_call | solution.py:652
  607.5 1.4 maximum_bitcast_fusion
  609.0 0.3 copy.71
  609.2 2.5 copy.72
  611.8 0.7 copy.78
  (29 shorter events, 0.1 us)
Async XLA Ops:
  2.2 185.8 %copy-start.10 = (f32[8,128]{1,0:T(8,128)}, f32[8,128]{1,0:T(8,128)S(1)}, u32[]{:S(2)}) copy-start(f32[8,128]{1,0:T(8,128)S(1)} %get-tuple-element.53) | copy-start | bytes 12292
  25.3 3.2 copy-start.1
  28.5 3.2 copy-start.2
  104.0 48.1 %copy-start.4 = (bf16[2,1024,128]{2,1,0:T(8,128)(2,1)S(1)}, bf16[2,1024,128]{2,1,0:T(8,128)(2,1)}, u32[]{:S(2)}) copy-start(bf16[2,1024,128]{2,1,0:T(8,128)(2,1)} %param.37) | copy-start | bytes 1572868
  153.4 32.2 %copy-start = (bf16[16,40,128]{2,1,0:T(8,128)(2,1)S(1)}, bf16[16,40,128]{2,1,0:T(8,128)(2,1)}, u32[]{:S(2)}) copy-start(bf16[16,40,128]{2,1,0:T(8,128)(2,1)} %get-tuple-element.24) | copy-start | bytes 491524
  153.4 32.4 %copy-start.8 = (bf16[8,128,128]{2,1,0:T(8,128)(2,1)S(1)}, bf16[8,128,128]{2,1,0:T(8,128)(2,1)}, u32[]{:S(2)}) copy-start(bf16[8,128,128]{2,1,0:T(8,128)(2,1)} %z_ref.1) | copy-start | bytes 786436
  185.5 3.5 slice-start
  185.8 4.0 slice-start.1
  186.7 3.9 copy-start.5
  186.8 4.7 copy-start.6
  186.9 5.4 copy-start.11
  186.9 6.0 copy-start.12
  448.1 33.7 %copy-start.9 = (bf16[8,128,128]{2,1,0:T(8,128)(2,1)S(1)}, bf16[8,128,128]{2,1,0:T(8,128)(2,1)}, u32[]{:S(2)}) copy-start(bf16[8,128,128]{2,1,0:T(8,128)(2,1)} %get-tuple-element.38) | copy-start | bytes 786436
  482.7 124.9 %copy-start.3 = (bf16[16,4,32,256]{3,2,1,0:T(8,128)(2,1)S(1)}, bf16[16,4,32,256]{3,2,1,0:T(8,128)(2,1)}, u32[]{:S(2)}) copy-start(bf16[16,4,32,256]{3,2,1,0:T(8,128)(2,1)} %get-tuple-element.37) | copy-start | bytes 3145732
  609.2 2.5 copy-start.7
